TPU v7x, 256 devices: a whole 4x4x8 slice. The times are simulated.
256 devices in a mesh: tok: 8 (over z), tile: 16 (over y, x_lo, core), pair: 2 (over x_hi).
Axes of the slice: x: 4 (x_hi: 2, x_lo: 2; x = x_hi * 2 + x_lo), y: 4, z: 8, core: 2. Of those that a mesh axis runs over, the one named last changes fastest.
Arguments:
- inputs: bfloat16 [8192, 4096], P(('tok', 'pair'), 'tile'), may hold values from -6 to 6
- output_grads: bfloat16 [8192, 4096], P(('tok', 'pair'), 'tile'), may hold values from -0.0625 to 0.0625
- statistics: float32 [16, 2, 1024, 1024], P('tile', 'pair', 'tok'), may hold values from -30 to 43008, as said below
Outputs:
- update: bfloat16 [16, 1024, 1024], P('tile', ('tok', 'pair'))
- new_statistics: float32 [16, 2, 1024, 1024], P('tile', 'pair', 'tok')
Inputs may be any that keep to these rules, and one draw needn't show every extreme that they name: `statistics`: for every block and factor the 1024 x 1024 matrix is symmetric and positive definite.
All inputs are finite; a program needn't handle non-finite values. Where the computation divides by a largest or mean magnitude, that divisor is 1e-20 or more.
Results may differ from a plain program's by a relative error of at most 0.00325.
The roundings to bfloat16 on the way count: a program that leaves them out, or rounds other values in their place, can miss the bound.
Values may be sent and summed in bfloat16 or wider, within the bound.
No kernel may reach another device: no remote copies, remote signals or barrier semaphores. Data moves between devices by JAX's collectives and lax.ppermute only.
A program may use at most 64 MiB of HBM per device.

v0:
```python
import jax
import jax.numpy as jnp
from jax import lax
from jax.experimental import pallas as pl
from jax.experimental.pallas import tpu as pltpu
from jax.sharding import Mesh, PartitionSpec as P


F32 = jnp.float32
BF16 = jnp.bfloat16
F16 = jnp.float16
VMEM = pl.BlockSpec(memory_space=pltpu.VMEM)
SMEM = pl.BlockSpec(memory_space=pltpu.SMEM)
HBM = pl.BlockSpec(memory_space=pltpu.HBM)
Z = 8
SWAP = [(0, 0), (1, 2), (2, 1), (3, 3)]


def params(mib):
    return pltpu.CompilerParams(vmem_limit_bytes=mib * 1024 * 1024)


def sds(shape, dt):
    return jax.ShapeDtypeStruct(shape, dt)


def dot(a, b, ca=1, cb=0):
    return lax.dot_general(a, b, (((ca,), (cb,)), ((), ())), preferred_element_type=F32)


def cat(ref):
    return jnp.concatenate([ref[k] for k in range(ref.shape[0])], axis=1)


def loop(n, body):
    lax.fori_loop(0, n, lambda j, c: (body(j), c)[1], 0)


def diagonal(n):
    return lax.broadcasted_iota(jnp.int32, (n, n), 0) == lax.broadcasted_iota(jnp.int32, (n, n), 1)


def partial_kernel(idx, *refs):
    a_own, a_oth, (b, out, acc_s, top) = refs[:4], refs[4:8], refs[8:]
    co, xl, pair = idx[0], idx[2], idx[3]
    top[...] = jnp.zeros(top.shape, F32)
    for h in range(2):
        for ref, c in ((a_own, co), (a_oth, 1 - co)):
            r = pl.multiple_of(256 * (2 * (xl ^ h) + c), 256)
            for cb in range(2):
                acc = (dot(ref[2 * h][...], b[2 * cb + pair], 0, 0)
                       + dot(ref[2 * h + 1][...], b[2 * cb + 1 - pair], 0, 0))
                acc_s[pl.ds(r, 256), 256 * cb:256 * (cb + 1)] = acc
                top[...] = jnp.maximum(top[...], jnp.max(jnp.abs(acc), axis=0, keepdims=True))
    peak = jnp.max(top[...], axis=1, keepdims=True)
    power = jnp.floor(jnp.log2(jnp.maximum(peak, 1e-30)))
    up = jnp.exp2(14.0 - power)

    def body(k):
        out[k, :128, :] = acc_s[pl.ds(pl.multiple_of(128 * k, 128), 128), :] * up
        out[k, 128:, :] = jnp.broadcast_to(power, (16, 512))

    loop(Z, body)


def assemble_kernel(idx, *refs):
    pieces, s_out = refs[:Z], refs[Z]
    z = idx[0]
    for d in range(Z):
        rb = (z + Z - d) % Z
        r = pl.multiple_of(rb * 128, 128)
        for k in range(5):
            cb = (rb + k) % Z
            c = pl.multiple_of(cb * 128, 128)
            blk = pieces[d][:, 128 * k:128 * (k + 1)]
            s_out[cb, pl.ds(r, 128), :] = blk
            if 0 < k < 4:
                s_out[rb, pl.ds(c, 128), :] = blk.T


def chain_kernel(idx, st, g0, r1, r2, r3, r4, o1, o2, o3, o4,
                 root, grad, rows, s_s, x_s, before, f0, f1, t0, t1, sem):
    z, co = idx[0], idx[1]
    fetch = pltpu.make_async_copy(st, s_s, sem)
    fetch.start()
    step = 1 - 2 * co
    pieces = [(g0, z, 0), (r1, z - step, 0), (r2, z - 2 * step, 0), (r3, z - 3 * step, 0),
              (o1, z + step, 0), (o2, z + 2 * step, 0), (o3, z + 3 * step, 0),
              (r4, z + 4, 64 * co), (o4, z + 4, 64 * (1 - co))]
    for ref, src, off in pieces:
        n = ref.shape[1]
        blk = (src + 2 * Z) % Z
        r = pl.multiple_of(blk * 128 + off, 64)
        for c in range(2):
            for cb in range(2):
                grad[2 * cb + c, pl.ds(r, n), :] = ref[c, :, 256 * cb:256 * (cb + 1)]

    @pl.when(co == 0)
    def _():
        for j in range(4):
            x_s[2 * j] = grad[j, :, :128]
            x_s[2 * j + 1] = grad[j, :, 128:]

    @pl.when(co == 1)
    def _():
        def body(k):
            r = pl.multiple_of(k * 128, 128)
            for j in range(4):
                x_s[k, 256 * j:256 * (j + 1), :] = grad[j, pl.ds(r, 128), :].T

        loop(Z, body)

    fetch.wait()
    zr = pl.multiple_of(z * 128, 128)
    for j in range(Z):
        before[:, 128 * j:128 * (j + 1)] = s_s[j, pl.ds(zr, 128), :]

    def product(j):
        r = pl.multiple_of(j * 256, 256)
        p = dot(cat(x_s), jnp.concatenate([x_s[k, pl.ds(r, 256), :] for k in range(Z)], axis=1), 1, 1)
        s_s[2 * j] = s_s[2 * j] + 0.1 * p[:, :128]
        s_s[2 * j + 1] = s_s[2 * j + 1] + 0.1 * p[:, 128:]

    loop(4, product)

    for j in range(Z):
        c = slice(128 * j, 128 * (j + 1))
        rows[:, c] = s_s[j, pl.ds(zr, 128), :] - before[:, c]
    top = None
    for j in range(Z):
        m = jnp.sum(jnp.abs(s_s[j]), axis=0, keepdims=True)
        top = m if top is None else jnp.maximum(top, m)
    bound = jnp.max(top, axis=1, keepdims=True)
    inv = 1.0 / (1.1 * bound)
    ridge = jnp.where(diagonal(128), 0.1 * bound, 0.0)
    five = jnp.where(diagonal(256), 5.0, 0.0)

    def first(j):
        for h in range(2):
            lo = pl.multiple_of(256 * j + 128 * h, 128)
            c = slice(128 * h, 128 * (h + 1))
            t1[j, :, c] = (s_s[2 * j + h] * inv).astype(BF16)
            t1[j, pl.ds(lo, 128), c] = ((s_s[2 * j + h, pl.ds(lo, 128), :] + ridge) * inv).astype(BF16)
        r = pl.multiple_of(256 * j, 256)
        f0[j] = t1[j] * jnp.asarray(-0.25, BF16)
        f0[j, pl.ds(r, 256), :] = ((five - t1[j, pl.ds(r, 256), :].astype(F32)) * 0.25).astype(BF16)

    loop(4, first)

    def mul(dst, a, b):
        def body(j):
            dst[j] = dot(cat(a), b[j]).astype(BF16)

        loop(4, body)

    mul(t0, f0, f0)
    mul(f1, t0, t0)

    def second(j):
        r = pl.multiple_of(256 * j, 256)
        t0[j] = dot(cat(f1), t1[j]).astype(BF16)
        diag = ((five - t0[j, pl.ds(r, 256), :].astype(F32)) * 0.25).astype(BF16)
        t0[j] = t0[j] * jnp.asarray(-0.25, BF16)
        t0[j, pl.ds(r, 256), :] = diag

    loop(4, second)
    mul(root, f0, t0)


def update_kernel(idx, own, other, grad, out, mix, r_s, keep):
    z, co = idx[0], idx[1]
    zr = pl.multiple_of(z * 128 + co * 64, 64)

    def run(left, right):
        def mixed(j):
            mix[j] = dot(cat(left), grad[j]).astype(BF16)

        loop(4, mixed)

        def raw(j, acc):
            r = dot(cat(mix), right[j])
            r_s[...] = r
            keep[j] = r_s[pl.ds(zr, 64), :]
            return acc + jnp.sum(r * r, axis=0, keepdims=True)

        update_sq = jnp.sum(lax.fori_loop(0, 4, raw, jnp.zeros((1, 256), F32)), axis=1, keepdims=True)

        def square(j, acc):
            v = grad[j].astype(F32)
            return acc + jnp.sum(v * v, axis=0, keepdims=True)

        grad_sq = jnp.sum(lax.fori_loop(0, 4, square, jnp.zeros((1, 256), F32)), axis=1, keepdims=True)
        ratio = jnp.sqrt(grad_sq / (update_sq + 1e-6))
        for j in range(4):
            out[:, 256 * j:256 * (j + 1)] = (keep[j] * ratio).astype(BF16)

    pl.when(co == 0)(lambda: run(own, other))
    pl.when(co == 1)(lambda: run(other, own))


def pack(x, peak):
    power = jnp.floor(jnp.log2(jnp.maximum(peak, 1e-30)))
    scaled = (x * jnp.exp2(14.0 - power)).astype(F16)
    label = jnp.broadcast_to(power, (*x.shape[:-2], 16, x.shape[-1])).astype(F16)
    return jnp.concatenate([scaled, label], axis=-2)


def unpack(x):
    return x[..., :-16, :].astype(F32) * jnp.exp2(x[..., -16:-15, :].astype(F32) - 14.0)


def everyone(x, axis, n):
    return lax.all_to_all(jnp.broadcast_to(x, (n, *x.shape)), axis, 0, 0, tiled=True)


def sibling(x):
    return lax.ppermute(x, "co", [(0, 1), (1, 0)])


def around(x):
    up, down = [x], []
    for k in range(1, 5):
        up.append(lax.ppermute(up[-1], "tok", [(i, (i + 1) % Z) for i in range(Z)]))
        if k < 4:
            down.append(lax.ppermute((down or [x])[-1], "tok", [(i, (i - 1) % Z) for i in range(Z)]))
    return up + down[::-1]


def step(inputs, output_grads, statistics):
    z = lax.axis_index("tok")
    co = lax.axis_index("co")
    idx1 = jnp.stack([co, z, lax.axis_index("xl"), lax.axis_index("pair")]).astype(jnp.int32)
    idx2 = jnp.stack([z, co]).astype(jnp.int32)

    table = [(yy * 4 + xx, xx * 4 + yy) for yy in range(4) for xx in range(4)]
    cot = lax.ppermute(output_grads, ("y", "xl", "pair"), table)
    a_own = [inputs]
    for d in range(1, 4):
        a_own.append(lax.ppermute(inputs, ("xl", "pair"), [(i, i ^ d) for i in range(4)]))
    b = everyone(cot, "y", 4)
    a_oth = []
    for d in range(4):
        a_oth.append(sibling(a_own[d]))

    stat = statistics.reshape(128, 1024)
    wide = jnp.concatenate([stat, stat[:, :512]], axis=1)
    part = lax.dynamic_slice(wide, (0, z * 128), (128, 640))
    part = pack(part, jnp.max(jnp.abs(stat)))
    part = lax.ppermute(part, ("co", "pair"), SWAP)
    st = around(part)
    st = pl.pallas_call(
        assemble_kernel,
        out_shape=sds((8, 1024, 128), F32),
        in_specs=[SMEM] + [VMEM] * Z,
        out_specs=VMEM,
        compiler_params=params(10),
        name="assemble",
    )(idx2, *[0.9 * unpack(p) for p in st])

    partial = pl.pallas_call(
        partial_kernel,
        out_shape=sds((Z, 144, 512), F32),
        in_specs=[SMEM] + [VMEM] * 9,
        out_specs=VMEM,
        scratch_shapes=[pltpu.VMEM((1024, 512), F32), pltpu.VMEM((1, 256), F32)],
        compiler_params=params(14),
        name="partial_gradient",
    )(idx1, *a_own, *a_oth, b)

    got = lax.all_to_all(partial.astype(F16), "tok", 0, 0, tiled=True)
    mine = jnp.sum(unpack(got), axis=0).astype(BF16)
    theirs = sibling(mine)
    piece = jnp.where(co == 0, jnp.stack([mine, theirs]), jnp.stack([theirs, mine]))
    ring = []
    for i in range(Z):
        ring += [(2 * i, 2 * ((i + 1) % Z)), (2 * i + 1, 2 * ((i - 1) % Z) + 1)]
    runs, others = [piece], []
    for s in range(1, 5):
        src = runs[-1]
        if s == 4:
            src = lax.dynamic_slice_in_dim(src, co * 64, 64, 1)
        runs.append(lax.ppermute(src, ("tok", "co"), ring))
        others.append(sibling(runs[-1]))

    root, grad, rows = pl.pallas_call(
        chain_kernel,
        out_shape=(sds((4, 1024, 256), BF16), sds((4, 1024, 256), BF16), sds((128, 1024), F32)),
        in_specs=[SMEM, HBM] + [VMEM] * 9,
        out_specs=(VMEM,) * 3,
        scratch_shapes=[pltpu.VMEM((8, 1024, 128), F32), pltpu.VMEM((8, 1024, 128), BF16),
                        pltpu.VMEM((128, 1024), F32)] + [pltpu.VMEM((4, 1024, 256), BF16)] * 4
        + [pltpu.SemaphoreType.DMA],
        compiler_params=params(22),
        name="inverse_root",
    )(idx2, st, *runs, *others)

    other_root = sibling(root)
    back = lax.ppermute(rows, ("co", "pair"), SWAP)
    final = pl.pallas_call(
        update_kernel,
        out_shape=sds((64, 1024), BF16),
        in_specs=[SMEM] + [VMEM] * 3,
        out_specs=VMEM,
        scratch_shapes=[pltpu.VMEM((4, 1024, 256), BF16), pltpu.VMEM((1024, 256), F32), pltpu.VMEM((4, 64, 256), F32)],
        compiler_params=params(16),
        name="update_rows",
    )(idx2, root, other_root, grad)
    update = lax.ppermute(final, ("co", "pair"), SWAP)
    new_rows = 0.9 * stat + back
    return update[None], new_rows[None, None]


def solution(mesh):
    m = Mesh(mesh.devices.reshape(8, 4, 2, 2, 2), ("tok", "y", "xl", "co", "pair"))
    tile = ("y", "xl", "co")
    return jax.shard_map(
        step,
        mesh=m,
        in_specs=(P(("tok", "pair"), tile), P(("tok", "pair"), tile), P(tile, "pair", "tok", None)),
        out_specs=(P(tile, ("tok", "pair"), None), P(tile, "pair", "tok", None)),
        check_vma=False,
    )
```

profile of v0, /device:TPU:1, one launch (start us, length us, event | category | flops | bytes accessed | tf_op | source)
XLA Modules:
  0.0 165.2 jit_solution(8278679594669558333)
XLA Ops:
  3.4 21.3 %all-to-all-start = ((bf16[4,512,256]{2,1,0:T(8,128)(2,1)}), bf16[4,512,256]{2,1,0:T(8,128)(2,1)S(1)}, u32[]{:S(2)}, u32[]{:S(2)}) async-start(bf16[4,512,256]{2,1,0:T(8,128)(2,1)} %broadcast_in_dim.10), calls=%async_computation | async-start | bytes 2097152 | tf_op jit(solution)/shard_map/all_to_all | solution.py:213
  24.8 2.4 %collective-permute-start.10 = (bf16[512,256]{1,0:T(8,128)(2,1)S(1)}, bf16[512,256]{1,0:T(8,128)(2,1)S(1)}, u32[]{:S(2)}, u32[]{:S(2)}) collective-permute-start(bf16[512,256]{1,0:T(8,128)(2,1)S(1)} %copy-done), channel_id=1, source_target_pairs={{0,5},{1,4},{4,1},{5,0},{2,7},{3,6},{6,3},{7,2},{8,13},{9,12},{12,... | collective-permute-start | bytes 786440 | tf_op jit(solution)/shard_map/ppermute | solution.py:239
  30.5 2.2 %collective-permute-done.10.refs_3_ = bf16[512,256]{1,0:T(8,128)(2,1)S(1)} collective-permute-done((bf16[512,256]{1,0:T(8,128)(2,1)S(1)}, bf16[512,256]{1,0:T(8,128)(2,1)S(1)}, u32[]{:S(2)}, u32[]{:S(2)}) %collective-permute-start.10) | collective-permute-done | bytes 262176 | tf_op jit(solution)/shard_map/ppermute | solution.py:239
  32.8 2.5 %collective-permute-start.14 = (bf16[512,256]{1,0:T(8,128)(2,1)S(1)}, bf16[512,256]{1,0:T(8,128)(2,1)S(1)}, u32[]{:S(2)}, u32[]{:S(2)}) collective-permute-start(bf16[512,256]{1,0:T(8,128)(2,1)S(1)} %collective-permute-done.10.refs_3_), channel_id=1, source_target_pairs={{0,2},{2,0},{1,3},{3,1},{4,6},{6,4},{5,7},{7,5},{8,10},{10,8},{9,1... | collective-permute-start | bytes 786440 | tf_op jit(solution)/shard_map/ppermute | solution.py:217
  35.3 2.6 %collective-permute-start.13 = (bf16[512,256]{1,0:T(8,128)(2,1)S(1)}, bf16[512,256]{1,0:T(8,128)(2,1)S(1)}, u32[]{:S(2)}, u32[]{:S(2)}) collective-permute-start(bf16[512,256]{1,0:T(8,128)(2,1)S(1)} %collective-permute-done.9.refs_2_), channel_id=1, source_target_pairs={{0,2},{2,0},{1,3},{3,1},{4,6},{6,4},{5,7},{7,5},{8,10},{10,8},{9,1... | collective-permute-start | bytes 786440 | tf_op jit(solution)/shard_map/ppermute | solution.py:217
  46.1 8.2 %all-to-all-start.1 = ((f16[8,144,512]{2,1,0:T(8,128)(2,1)}), f16[8,144,512]{2,1,0:T(8,128)(2,1)S(1)}, u32[]{:S(2)}, u32[]{:S(2)}) async-start(f16[8,144,512]{2,1,0:T(8,128)(2,1)} %convert_element_type.95), calls=%async_computation.1 | async-start | bytes 2359296 | tf_op jit(solution)/shard_map/all_to_all | solution.py:270
  55.7 4.0 %collective-permute-start = (f16[144,640]{1,0:T(8,128)(2,1)S(1)}, f16[144,640]{1,0:T(8,128)(2,1)S(1)}, u32[]{:S(2)}, u32[]{:S(2)}) collective-permute-start(f16[144,640]{1,0:T(8,128)(2,1)S(1)} %concatenate.7), channel_id=1, source_target_pairs={{0,0},{1,2},{2,1},{3,3},{4,4},{5,6},{6,5},{7,7},{8,8},{9,10},{10,9... | collective-permute-start | bytes 552968 | tf_op jit(solution)/shard_map/ppermute | solution.py:249
  59.8 4.6 %collective-permute-done = f16[144,640]{1,0:T(8,128)(2,1)S(1)} collective-permute-done((f16[144,640]{1,0:T(8,128)(2,1)S(1)}, f16[144,640]{1,0:T(8,128)(2,1)S(1)}, u32[]{:S(2)}, u32[]{:S(2)}) %collective-permute-start) | collective-permute-done | bytes 184352 | tf_op jit(solution)/shard_map/ppermute | solution.py:249
  64.4 2.7 %collective-permute-start.5 = (f16[144,640]{1,0:T(8,128)(2,1)S(1)}, f16[144,640]{1,0:T(8,128)(2,1)S(1)}, u32[]{:S(2)}, u32[]{:S(2)}) collective-permute-start(f16[144,640]{1,0:T(8,128)(2,1)S(1)} %collective-permute-done), channel_id=1, source_target_pairs={{0,224},{32,0},{64,32},{96,64},{128,96},{160,128},{192,160},{224,1... | collective-permute-start | bytes 552968 | tf_op jit(solution)/shard_map/ppermute | solution.py:225
  67.2 18.2 %collective-permute-done.5 = f16[144,640]{1,0:T(8,128)(2,1)S(1)} collective-permute-done((f16[144,640]{1,0:T(8,128)(2,1)S(1)}, f16[144,640]{1,0:T(8,128)(2,1)S(1)}, u32[]{:S(2)}, u32[]{:S(2)}) %collective-permute-start.5) | collective-permute-done | bytes 184352 | tf_op jit(solution)/shard_map/ppermute | solution.py:225
  90.0 3.0 %collective-permute-start.7 = (f16[144,640]{1,0:T(8,128)(2,1)S(1)}, f16[144,640]{1,0:T(8,128)(2,1)S(1)}, u32[]{:S(2)}, u32[]{:S(2)}) collective-permute-start(f16[144,640]{1,0:T(8,128)(2,1)S(1)} %collective-permute-done.6), channel_id=1, source_target_pairs={{0,224},{32,0},{64,32},{96,64},{128,96},{160,128},{192,160},{224,1... | collective-permute-start | bytes 552968 | tf_op jit(solution)/shard_map/ppermute | solution.py:225
  94.9 5.4 %collective-permute-done.17.r1 = bf16[2,128,512]{2,1,0:T(8,128)(2,1)S(1)} collective-permute-done((bf16[2,128,512]{2,1,0:T(8,128)(2,1)S(1)}, bf16[2,128,512]{2,1,0:T(8,128)(2,1)S(1)}, u32[]{:S(2)}, u32[]{:S(2)}) %collective-permute-start.17) | collective-permute-done | bytes 262176 | tf_op jit(solution)/shard_map/ppermute | solution.py:282
  100.3 3.1 %collective-permute-start.18 = (bf16[2,128,512]{2,1,0:T(8,128)(2,1)S(1)}, bf16[2,128,512]{2,1,0:T(8,128)(2,1)S(1)}, u32[]{:S(2)}, u32[]{:S(2)}) collective-permute-start(bf16[2,128,512]{2,1,0:T(8,128)(2,1)S(1)} %collective-permute-done.17.r1), channel_id=1, source_target_pairs={{0,32},{2,226},{32,64},{34,2},{64,96},{66,34},{96,128},{98,66},{12... | collective-permute-start | bytes 786440 | tf_op jit(solution)/shard_map/ppermute | solution.py:282
  103.6 3.1 %collective-permute-done.18.r2 = bf16[2,128,512]{2,1,0:T(8,128)(2,1)S(1)} collective-permute-done((bf16[2,128,512]{2,1,0:T(8,128)(2,1)S(1)}, bf16[2,128,512]{2,1,0:T(8,128)(2,1)S(1)}, u32[]{:S(2)}, u32[]{:S(2)}) %collective-permute-start.18) | collective-permute-done | bytes 262176 | tf_op jit(solution)/shard_map/ppermute | solution.py:282
  106.7 3.1 %collective-permute-start.19 = (bf16[2,128,512]{2,1,0:T(8,128)(2,1)S(1)}, bf16[2,128,512]{2,1,0:T(8,128)(2,1)S(1)}, u32[]{:S(2)}, u32[]{:S(2)}) collective-permute-start(bf16[2,128,512]{2,1,0:T(8,128)(2,1)S(1)} %collective-permute-done.18.r2), channel_id=1, source_target_pairs={{0,32},{2,226},{32,64},{34,2},{64,96},{66,34},{96,128},{98,66},{12... | collective-permute-start | bytes 786440 | tf_op jit(solution)/shard_map/ppermute | solution.py:282
  109.9 3.2 %collective-permute-done.19.r3 = bf16[2,128,512]{2,1,0:T(8,128)(2,1)S(1)} collective-permute-done((bf16[2,128,512]{2,1,0:T(8,128)(2,1)S(1)}, bf16[2,128,512]{2,1,0:T(8,128)(2,1)S(1)}, u32[]{:S(2)}, u32[]{:S(2)}) %collective-permute-start.19) | collective-permute-done | bytes 262176 | tf_op jit(solution)/shard_map/ppermute | solution.py:282
  113.2 3.2 %collective-permute-start.20 = (bf16[2,64,512]{2,1,0:T(8,128)(2,1)S(1)}, bf16[2,64,512]{2,1,0:T(8,128)(2,1)S(1)}, u32[]{:S(2)}, u32[]{:S(2)}) collective-permute-start(bf16[2,64,512]{2,1,0:T(8,128)(2,1)S(1)} %constant_dynamic-slice_fusion), channel_id=1, source_target_pairs={{0,32},{2,226},{32,64},{34,2},{64,96},{66,34},{96,128},{98,66},{12... | collective-permute-start | bytes 393224 | tf_op jit(solution)/shard_map/ppermute | solution.py:282
  116.4 4.1 %collective-permute-start.21 = (bf16[2,128,512]{2,1,0:T(8,128)(2,1)S(1)}, bf16[2,128,512]{2,1,0:T(8,128)(2,1)S(1)}, u32[]{:S(2)}, u32[]{:S(2)}) collective-permute-start(bf16[2,128,512]{2,1,0:T(8,128)(2,1)S(1)} %collective-permute-done.17.r1), channel_id=1, source_target_pairs={{0,2},{2,0},{1,3},{3,1},{4,6},{6,4},{5,7},{7,5},{8,10},{10,8},{9,1... | collective-permute-start | bytes 786440 | tf_op jit(solution)/shard_map/ppermute | solution.py:217
  121.0 5.5 %collective-permute-start.24 = (bf16[2,64,512]{2,1,0:T(8,128)(2,1)S(1)}, bf16[2,64,512]{2,1,0:T(8,128)(2,1)S(1)}, u32[]{:S(2)}, u32[]{:S(2)}) collective-permute-start(bf16[2,64,512]{2,1,0:T(8,128)(2,1)S(1)} %collective-permute-done.20.r4), channel_id=1, source_target_pairs={{0,2},{2,0},{1,3},{3,1},{4,6},{6,4},{5,7},{7,5},{8,10},{10,8},{9,1... | collective-permute-start | bytes 393224 | tf_op jit(solution)/shard_map/ppermute | solution.py:217
  127.7 18.1 %inverse_root.1 = (bf16[4,1024,256]{2,1,0:T(8,128)(2,1)S(1)}, bf16[4,1024,256]{2,1,0:T(8,128)(2,1)S(1)}, f32[128,1024]{1,0:T(8,128)S(1)}) custom-call(s32[2]{0:T(128)S(1)} %pad_add_fusion.idx, f32[8,1024,128]{2,1,0:T(8,128)S(1)} %assemble.1.st, bf16[2,128,512]{2,1,0:T(8,128)(2,1)S(1)} %maximum_select_fusion.g0, ...), custom_call_target="tpu_custom_call" | custom-call | tf_op jit(solution)/shard_map/inverse_root/pallas_call | solution.py:285
  145.9 3.8 %collective-permute-start.27 = (f32[128,1024]{1,0:T(8,128)S(1)}, f32[128,1024]{1,0:T(8,128)S(1)}, u32[]{:S(2)}, u32[]{:S(2)}) collective-permute-start(f32[128,1024]{1,0:T(8,128)S(1)} %get-tuple-element.7), channel_id=1, source_target_pairs={{0,0},{1,2},{2,1},{3,3},{4,4},{5,6},{6,5},{7,7},{8,8},{9,10},{10,9... | collective-permute-start | bytes 1572872 | tf_op jit(solution)/shard_map/ppermute | solution.py:298
  150.0 6.8 %update_rows.1 = bf16[64,1024]{1,0:T(8,128)(2,1)S(1)} custom-call(s32[2]{0:T(128)S(1)} %pad_add_fusion.idx, bf16[4,1024,256]{2,1,0:T(8,128)(2,1)S(1)} %get-tuple-element.5.own, bf16[4,1024,256]{2,1,0:T(8,128)(2,1)S(1)} %collective-permute-done.25.other, bf16[4,1024,256]{2,1,0:T(8,128)(2,1)S(1)} %get-tuple-element.6.grad), custom_call_target="tpu_custom_call" | custom-call | tf_op jit(solution)/shard_map/update_rows/pallas_call | solution.py:299
  156.8 3.5 %collective-permute-start.26 = (bf16[64,1024]{1,0:T(8,128)(2,1)S(1)}, bf16[64,1024]{1,0:T(8,128)(2,1)S(1)}, u32[]{:S(2)}, u32[]{:S(2)}) collective-permute-start(bf16[64,1024]{1,0:T(8,128)(2,1)S(1)} %update_rows.1), channel_id=1, source_target_pairs={{0,0},{1,2},{2,1},{3,3},{4,4},{5,6},{6,5},{7,7},{8,8},{9,10},{10,9... | collective-permute-start | bytes 393224 | tf_op jit(solution)/shard_map/ppermute | solution.py:308
  161.1 3.5 %collective-permute-done.26 = bf16[64,1024]{1,0:T(8,128)(2,1)S(1)} collective-permute-done((bf16[64,1024]{1,0:T(8,128)(2,1)S(1)}, bf16[64,1024]{1,0:T(8,128)(2,1)S(1)}, u32[]{:S(2)}, u32[]{:S(2)}) %collective-permute-start.26) | collective-permute-done | bytes 131104 | tf_op jit(solution)/shard_map/ppermute | solution.py:308
  (75 shorter events, 25.6 us)
Async XLA Ops:
  3.4 39.2 %all-to-all-start = ((bf16[4,512,256]{2,1,0:T(8,128)(2,1)}), bf16[4,512,256]{2,1,0:T(8,128)(2,1)S(1)}, u32[]{:S(2)}, u32[]{:S(2)}) async-start(bf16[4,512,256]{2,1,0:T(8,128)(2,1)} %broadcast_in_dim.10), calls=%async_computation | async-start | bytes 2097152 | tf_op jit(solution)/shard_map/all_to_all | solution.py:213
  24.8 8.0 %collective-permute-start.10 = (bf16[512,256]{1,0:T(8,128)(2,1)S(1)}, bf16[512,256]{1,0:T(8,128)(2,1)S(1)}, u32[]{:S(2)}, u32[]{:S(2)}) collective-permute-start(bf16[512,256]{1,0:T(8,128)(2,1)S(1)} %copy-done), channel_id=1, source_target_pairs={{0,5},{1,4},{4,1},{5,0},{2,7},{3,6},{6,3},{7,2},{8,13},{9,12},{12,... | collective-permute-start | bytes 786440 | tf_op jit(solution)/shard_map/ppermute | solution.py:239
  27.2 8.1 %collective-permute-start.9 = (bf16[512,256]{1,0:T(8,128)(2,1)S(1)}, bf16[512,256]{1,0:T(8,128)(2,1)S(1)}, u32[]{:S(2)}, u32[]{:S(2)}) collective-permute-start(bf16[512,256]{1,0:T(8,128)(2,1)S(1)} %copy-done), channel_id=1, source_target_pairs={{0,4},{1,5},{4,0},{5,1},{2,6},{3,7},{6,2},{7,3},{8,12},{9,13},{12,... | collective-permute-start | bytes 786440 | tf_op jit(solution)/shard_map/ppermute | solution.py:239
  27.2 12.1 %collective-permute-start.8 = (bf16[512,256]{1,0:T(8,128)(2,1)S(1)}, bf16[512,256]{1,0:T(8,128)(2,1)S(1)}, u32[]{:S(2)}, u32[]{:S(2)}) collective-permute-start(bf16[512,256]{1,0:T(8,128)(2,1)S(1)} %copy-done), channel_id=1, source_target_pairs={{0,1},{1,0},{4,5},{5,4},{2,3},{3,2},{6,7},{7,6},{8,9},{9,8},{12,13... | collective-permute-start | bytes 786440 | tf_op jit(solution)/shard_map/ppermute | solution.py:239
  28.6 13.0 %collective-permute-start.11 = (bf16[512,256]{1,0:T(8,128)(2,1)S(1)}, bf16[512,256]{1,0:T(8,128)(2,1)S(1)}, u32[]{:S(2)}, u32[]{:S(2)}) collective-permute-start(bf16[512,256]{1,0:T(8,128)(2,1)S(1)} %copy-done), channel_id=1, source_target_pairs={{0,2},{2,0},{1,3},{3,1},{4,6},{6,4},{5,7},{7,5},{8,10},{10,8},{9,1... | collective-permute-start | bytes 786440 | tf_op jit(solution)/shard_map/ppermute | solution.py:217
  32.8 8.8 %collective-permute-start.14 = (bf16[512,256]{1,0:T(8,128)(2,1)S(1)}, bf16[512,256]{1,0:T(8,128)(2,1)S(1)}, u32[]{:S(2)}, u32[]{:S(2)}) collective-permute-start(bf16[512,256]{1,0:T(8,128)(2,1)S(1)} %collective-permute-done.10.refs_3_), channel_id=1, source_target_pairs={{0,2},{2,0},{1,3},{3,1},{4,6},{6,4},{5,7},{7,5},{8,10},{10,8},{9,1... | collective-permute-start | bytes 786440 | tf_op jit(solution)/shard_map/ppermute | solution.py:217
  46.1 40.8 %all-to-all-start.1 = ((f16[8,144,512]{2,1,0:T(8,128)(2,1)}), f16[8,144,512]{2,1,0:T(8,128)(2,1)S(1)}, u32[]{:S(2)}, u32[]{:S(2)}) async-start(f16[8,144,512]{2,1,0:T(8,128)(2,1)} %convert_element_type.95), calls=%async_computation.1 | async-start | bytes 2359296 | tf_op jit(solution)/shard_map/all_to_all | solution.py:270
  55.7 8.7 %collective-permute-start = (f16[144,640]{1,0:T(8,128)(2,1)S(1)}, f16[144,640]{1,0:T(8,128)(2,1)S(1)}, u32[]{:S(2)}, u32[]{:S(2)}) collective-permute-start(f16[144,640]{1,0:T(8,128)(2,1)S(1)} %concatenate.7), channel_id=1, source_target_pairs={{0,0},{1,2},{2,1},{3,3},{4,4},{5,6},{6,5},{7,7},{8,8},{9,10},{10,9... | collective-permute-start | bytes 552968 | tf_op jit(solution)/shard_map/ppermute | solution.py:249
  64.4 20.9 %collective-permute-start.5 = (f16[144,640]{1,0:T(8,128)(2,1)S(1)}, f16[144,640]{1,0:T(8,128)(2,1)S(1)}, u32[]{:S(2)}, u32[]{:S(2)}) collective-permute-start(f16[144,640]{1,0:T(8,128)(2,1)S(1)} %collective-permute-done), channel_id=1, source_target_pairs={{0,224},{32,0},{64,32},{96,64},{128,96},{160,128},{192,160},{224,1... | collective-permute-start | bytes 552968 | tf_op jit(solution)/shard_map/ppermute | solution.py:225
  67.1 19.7 %collective-permute-start.1 = (f16[144,640]{1,0:T(8,128)(2,1)S(1)}, f16[144,640]{1,0:T(8,128)(2,1)S(1)}, u32[]{:S(2)}, u32[]{:S(2)}) collective-permute-start(f16[144,640]{1,0:T(8,128)(2,1)S(1)} %collective-permute-done), channel_id=1, source_target_pairs={{0,32},{32,64},{64,96},{96,128},{128,160},{160,192},{192,224},{224... | collective-permute-start | bytes 552968 | tf_op jit(solution)/shard_map/ppermute | solution.py:223
  86.8 6.3 %collective-permute-start.2 = (f16[144,640]{1,0:T(8,128)(2,1)S(1)}, f16[144,640]{1,0:T(8,128)(2,1)S(1)}, u32[]{:S(2)}, u32[]{:S(2)}) collective-permute-start(f16[144,640]{1,0:T(8,128)(2,1)S(1)} %collective-permute-done.1), channel_id=1, source_target_pairs={{0,32},{32,64},{64,96},{96,128},{128,160},{160,192},{192,224},{224... | collective-permute-start | bytes 552968 | tf_op jit(solution)/shard_map/ppermute | solution.py:223
  90.0 19.8 %collective-permute-start.7 = (f16[144,640]{1,0:T(8,128)(2,1)S(1)}, f16[144,640]{1,0:T(8,128)(2,1)S(1)}, u32[]{:S(2)}, u32[]{:S(2)}) collective-permute-start(f16[144,640]{1,0:T(8,128)(2,1)S(1)} %collective-permute-done.6), channel_id=1, source_target_pairs={{0,224},{32,0},{64,32},{96,64},{128,96},{160,128},{192,160},{224,1... | collective-permute-start | bytes 552968 | tf_op jit(solution)/shard_map/ppermute | solution.py:225
  93.1 7.3 %collective-permute-start.17 = (bf16[2,128,512]{2,1,0:T(8,128)(2,1)S(1)}, bf16[2,128,512]{2,1,0:T(8,128)(2,1)S(1)}, u32[]{:S(2)}, u32[]{:S(2)}) collective-permute-start(bf16[2,128,512]{2,1,0:T(8,128)(2,1)S(1)} %maximum_select_fusion.g0), channel_id=1, source_target_pairs={{0,32},{2,226},{32,64},{34,2},{64,96},{66,34},{96,128},{98,66},{12... | collective-permute-start | bytes 786440 | tf_op jit(solution)/shard_map/ppermute | solution.py:282
  93.2 10.3 %collective-permute-start.3 = (f16[144,640]{1,0:T(8,128)(2,1)S(1)}, f16[144,640]{1,0:T(8,128)(2,1)S(1)}, u32[]{:S(2)}, u32[]{:S(2)}) collective-permute-start(f16[144,640]{1,0:T(8,128)(2,1)S(1)} %collective-permute-done.2), channel_id=1, source_target_pairs={{0,32},{32,64},{64,96},{96,128},{128,160},{160,192},{192,224},{224... | collective-permute-start | bytes 552968 | tf_op jit(solution)/shard_map/ppermute | solution.py:223
  100.3 6.4 %collective-permute-start.18 = (bf16[2,128,512]{2,1,0:T(8,128)(2,1)S(1)}, bf16[2,128,512]{2,1,0:T(8,128)(2,1)S(1)}, u32[]{:S(2)}, u32[]{:S(2)}) collective-permute-start(bf16[2,128,512]{2,1,0:T(8,128)(2,1)S(1)} %collective-permute-done.17.r1), channel_id=1, source_target_pairs={{0,32},{2,226},{32,64},{34,2},{64,96},{66,34},{96,128},{98,66},{12... | collective-permute-start | bytes 786440 | tf_op jit(solution)/shard_map/ppermute | solution.py:282
  103.5 17.5 %collective-permute-start.4 = (f16[144,640]{1,0:T(8,128)(2,1)S(1)}, f16[144,640]{1,0:T(8,128)(2,1)S(1)}, u32[]{:S(2)}, u32[]{:S(2)}) collective-permute-start(f16[144,640]{1,0:T(8,128)(2,1)S(1)} %collective-permute-done.3), channel_id=1, source_target_pairs={{0,32},{32,64},{64,96},{96,128},{128,160},{160,192},{192,224},{224... | collective-permute-start | bytes 552968 | tf_op jit(solution)/shard_map/ppermute | solution.py:223
  106.7 6.4 %collective-permute-start.19 = (bf16[2,128,512]{2,1,0:T(8,128)(2,1)S(1)}, bf16[2,128,512]{2,1,0:T(8,128)(2,1)S(1)}, u32[]{:S(2)}, u32[]{:S(2)}) collective-permute-start(bf16[2,128,512]{2,1,0:T(8,128)(2,1)S(1)} %collective-permute-done.18.r2), channel_id=1, source_target_pairs={{0,32},{2,226},{32,64},{34,2},{64,96},{66,34},{96,128},{98,66},{12... | collective-permute-start | bytes 786440 | tf_op jit(solution)/shard_map/ppermute | solution.py:282
  113.2 7.8 %collective-permute-start.20 = (bf16[2,64,512]{2,1,0:T(8,128)(2,1)S(1)}, bf16[2,64,512]{2,1,0:T(8,128)(2,1)S(1)}, u32[]{:S(2)}, u32[]{:S(2)}) collective-permute-start(bf16[2,64,512]{2,1,0:T(8,128)(2,1)S(1)} %constant_dynamic-slice_fusion), channel_id=1, source_target_pairs={{0,32},{2,226},{32,64},{34,2},{64,96},{66,34},{96,128},{98,66},{12... | collective-permute-start | bytes 393224 | tf_op jit(solution)/shard_map/ppermute | solution.py:282
  116.4 11.3 %collective-permute-start.21 = (bf16[2,128,512]{2,1,0:T(8,128)(2,1)S(1)}, bf16[2,128,512]{2,1,0:T(8,128)(2,1)S(1)}, u32[]{:S(2)}, u32[]{:S(2)}) collective-permute-start(bf16[2,128,512]{2,1,0:T(8,128)(2,1)S(1)} %collective-permute-done.17.r1), channel_id=1, source_target_pairs={{0,2},{2,0},{1,3},{3,1},{4,6},{6,4},{5,7},{7,5},{8,10},{10,8},{9,1... | collective-permute-start | bytes 786440 | tf_op jit(solution)/shard_map/ppermute | solution.py:217
  120.5 7.2 %collective-permute-start.22 = (bf16[2,128,512]{2,1,0:T(8,128)(2,1)S(1)}, bf16[2,128,512]{2,1,0:T(8,128)(2,1)S(1)}, u32[]{:S(2)}, u32[]{:S(2)}) collective-permute-start(bf16[2,128,512]{2,1,0:T(8,128)(2,1)S(1)} %collective-permute-done.18.r2), channel_id=1, source_target_pairs={{0,2},{2,0},{1,3},{3,1},{4,6},{6,4},{5,7},{7,5},{8,10},{10,8},{9,1... | collective-permute-start | bytes 786440 | tf_op jit(solution)/shard_map/ppermute | solution.py:217
  120.6 7.1 %collective-permute-start.23 = (bf16[2,128,512]{2,1,0:T(8,128)(2,1)S(1)}, bf16[2,128,512]{2,1,0:T(8,128)(2,1)S(1)}, u32[]{:S(2)}, u32[]{:S(2)}) collective-permute-start(bf16[2,128,512]{2,1,0:T(8,128)(2,1)S(1)} %collective-permute-done.19.r3), channel_id=1, source_target_pairs={{0,2},{2,0},{1,3},{3,1},{4,6},{6,4},{5,7},{7,5},{8,10},{10,8},{9,1... | collective-permute-start | bytes 786440 | tf_op jit(solution)/shard_map/ppermute | solution.py:217
  121.0 6.7 %collective-permute-start.24 = (bf16[2,64,512]{2,1,0:T(8,128)(2,1)S(1)}, bf16[2,64,512]{2,1,0:T(8,128)(2,1)S(1)}, u32[]{:S(2)}, u32[]{:S(2)}) collective-permute-start(bf16[2,64,512]{2,1,0:T(8,128)(2,1)S(1)} %collective-permute-done.20.r4), channel_id=1, source_target_pairs={{0,2},{2,0},{1,3},{3,1},{4,6},{6,4},{5,7},{7,5},{8,10},{10,8},{9,1... | collective-permute-start | bytes 393224 | tf_op jit(solution)/shard_map/ppermute | solution.py:217
  145.9 14.4 %collective-permute-start.27 = (f32[128,1024]{1,0:T(8,128)S(1)}, f32[128,1024]{1,0:T(8,128)S(1)}, u32[]{:S(2)}, u32[]{:S(2)}) collective-permute-start(f32[128,1024]{1,0:T(8,128)S(1)} %get-tuple-element.7), channel_id=1, source_target_pairs={{0,0},{1,2},{2,1},{3,3},{4,4},{5,6},{6,5},{7,7},{8,8},{9,10},{10,9... | collective-permute-start | bytes 1572872 | tf_op jit(solution)/shard_map/ppermute | solution.py:298
  156.8 7.8 %collective-permute-start.26 = (bf16[64,1024]{1,0:T(8,128)(2,1)S(1)}, bf16[64,1024]{1,0:T(8,128)(2,1)S(1)}, u32[]{:S(2)}, u32[]{:S(2)}) collective-permute-start(bf16[64,1024]{1,0:T(8,128)(2,1)S(1)} %update_rows.1), channel_id=1, source_target_pairs={{0,0},{1,2},{2,1},{3,3},{4,4},{5,6},{6,5},{7,7},{8,8},{9,10},{10,9... | collective-permute-start | bytes 393224 | tf_op jit(solution)/shard_map/ppermute | solution.py:308
  (8 other events, 59.8 us)
where the time goes:
time: 166 us; the launch traced here: 165 us
  starting transfers between devices  86.3 us (52%)
  waiting for transfers between devices  43.6 us (26%)
  Pallas kernels  28.1 us (17%)
  other arithmetic  3.79 us (2%)
  local copies, waits for them, and re-layouts  1.78 us (1%)
    ppermute x10, starting transfers between devices, sibling(): return lax.ppermute(x, 'co', [(0, 1), (1, 0)])  21.5 us
    all_to_all x1, starting transfers between devices, everyone(): lax.all_to_all(jnp.broadcast_to(x, (n, *x.shape)), axis, 0, 0, tiled=True)  21.3 us
    ppermute x3, waiting for transfers between devices, around(): lax.ppermute((down or [x])[-1], 'tok', [(i, (i - 1) % Z) for i in range(Z)])  18.8 us
    pallas_call x1, Pallas kernels, step(): pl.pallas_call(chain_kernel, out_shape=(sds((4, 1024, 256), BF16), sds((4...  18.1 us
    ppermute x4, waiting for transfers between devices, step(): runs.append(lax.ppermute(src, ('tok', 'co'), ring))  11.8 us
    ppermute x4, starting transfers between devices, step(): runs.append(lax.ppermute(src, ('tok', 'co'), ring))  9.47 us
    all_to_all x1, starting transfers between devices, step(): got = lax.all_to_all(partial.astype(F16), 'tok', 0, 0, tiled=True)  8.19 us
    ppermute x3, starting transfers between devices, around(): lax.ppermute((down or [x])[-1], 'tok', [(i, (i - 1) % Z) for i in range(Z)])  7.15 us
  transfers between devices with their start and end apart: 30, of which 11 were waited for; matrix products, arithmetic and copies ran while one was open for 2% of the time, Pallas kernels for 5%

commit v1 on v0

--- a/solution.py
+++ b/solution.py
@@ -40,31 +40,33 @@
     return lax.broadcasted_iota(jnp.int32, (n, n), 0) == lax.broadcasted_iota(jnp.int32, (n, n), 1)
 
 
-def partial_kernel(idx, *refs):
-    a_own, a_oth, (b, out, acc_s, top) = refs[:4], refs[4:8], refs[8:]
-    co, xl, pair = idx[0], idx[2], idx[3]
+def partial_kernel(idx, a_own, a_oth, b0, b1, b2, b3, out, acc_s, top):
+    co, y = idx[0], idx[2]
+    b = (b0, b1, b2, b3)
     top[...] = jnp.zeros(top.shape, F32)
     for h in range(2):
+        cb = (y >> 1) ^ h
         for ref, c in ((a_own, co), (a_oth, 1 - co)):
-            r = pl.multiple_of(256 * (2 * (xl ^ h) + c), 256)
-            for cb in range(2):
-                acc = (dot(ref[2 * h][...], b[2 * cb + pair], 0, 0)
-                       + dot(ref[2 * h + 1][...], b[2 * cb + 1 - pair], 0, 0))
-                acc_s[pl.ds(r, 256), 256 * cb:256 * (cb + 1)] = acc
+            for l in range(2):
+                r = pl.multiple_of(256 * (2 * l + c), 256)
+                acc = (dot(ref[2 * l + (y & 1)], b[2 * h][...], 0, 0)
+                       + dot(ref[2 * l + 1 - (y & 1)], b[2 * h + 1][...], 0, 0))
+                acc_s[cb, pl.ds(r, 256), :] = acc
                 top[...] = jnp.maximum(top[...], jnp.max(jnp.abs(acc), axis=0, keepdims=True))
     peak = jnp.max(top[...], axis=1, keepdims=True)
     power = jnp.floor(jnp.log2(jnp.maximum(peak, 1e-30)))
     up = jnp.exp2(14.0 - power)
 
     def body(k):
-        out[k, :128, :] = acc_s[pl.ds(pl.multiple_of(128 * k, 128), 128), :] * up
+        r = pl.multiple_of(128 * k, 128)
+        for cb in range(2):
+            out[k, :128, 256 * cb:256 * (cb + 1)] = acc_s[cb, pl.ds(r, 128), :] * up
         out[k, 128:, :] = jnp.broadcast_to(power, (16, 512))
 
     loop(Z, body)
 
 
-def assemble_kernel(idx, *refs):
-    pieces, s_out = refs[:Z], refs[Z]
+def assemble_kernel(idx, pieces, s_out):
     z = idx[0]
     for d in range(Z):
         rb = (z + Z - d) % Z
@@ -72,10 +74,20 @@
         for k in range(5):
             cb = (rb + k) % Z
             c = pl.multiple_of(cb * 128, 128)
-            blk = pieces[d][:, 128 * k:128 * (k + 1)]
+            blk = pieces[d, :, 128 * k:128 * (k + 1)]
             s_out[cb, pl.ds(r, 128), :] = blk
             if 0 < k < 4:
                 s_out[rb, pl.ds(c, 128), :] = blk.T
+
+
+def merge_kernel(idx, mine, theirs, out):
+    co = idx[1]
+    out[co] = mine[...]
+    out[1 - co] = theirs[...]
+
+
+def half_kernel(idx, src, out):
+    out[...] = src[:, pl.ds(pl.multiple_of(64 * idx[1], 64), 64), :]
 
 
 def chain_kernel(idx, st, g0, r1, r2, r3, r4, o1, o2, o3, o4,
@@ -229,58 +241,63 @@
 def step(inputs, output_grads, statistics):
     z = lax.axis_index("tok")
     co = lax.axis_index("co")
-    idx1 = jnp.stack([co, z, lax.axis_index("xl"), lax.axis_index("pair")]).astype(jnp.int32)
+    idx1 = jnp.stack([co, z, lax.axis_index("y")]).astype(jnp.int32)
     idx2 = jnp.stack([z, co]).astype(jnp.int32)
 
     table = [(yy * 4 + xx, xx * 4 + yy) for yy in range(4) for xx in range(4)]
-    cot = lax.ppermute(output_grads, ("y", "xl", "pair"), table)
-    a_own = [inputs]
+    cot = [lax.ppermute(output_grads, ("y", "xl", "pair"), table)]
+    a_own = everyone(inputs, ("xl", "pair"), 4)
     for d in range(1, 4):
-        a_own.append(lax.ppermute(inputs, ("xl", "pair"), [(i, i ^ d) for i in range(4)]))
-    b = everyone(cot, "y", 4)
-    a_oth = []
-    for d in range(4):
-        a_oth.append(sibling(a_own[d]))
+        cot.append(lax.ppermute(cot[0], "y", [(i, i ^ d) for i in range(4)]))
+    a_oth = sibling(a_own)
 
     stat = statistics.reshape(128, 1024)
     wide = jnp.concatenate([stat, stat[:, :512]], axis=1)
     part = lax.dynamic_slice(wide, (0, z * 128), (128, 640))
     part = pack(part, jnp.max(jnp.abs(stat)))
-    part = lax.ppermute(part, ("co", "pair"), SWAP)
-    st = around(part)
+    st = jnp.stack(around(part))
+    st = lax.ppermute(st, ("co", "pair"), SWAP)
     st = pl.pallas_call(
         assemble_kernel,
         out_shape=sds((8, 1024, 128), F32),
-        in_specs=[SMEM] + [VMEM] * Z,
+        in_specs=[SMEM, VMEM],
         out_specs=VMEM,
         compiler_params=params(10),
         name="assemble",
-    )(idx2, *[0.9 * unpack(p) for p in st])
+    )(idx2, 0.9 * unpack(st))
 
     partial = pl.pallas_call(
         partial_kernel,
         out_shape=sds((Z, 144, 512), F32),
-        in_specs=[SMEM] + [VMEM] * 9,
+        in_specs=[SMEM] + [VMEM] * 6,
         out_specs=VMEM,
-        scratch_shapes=[pltpu.VMEM((1024, 512), F32), pltpu.VMEM((1, 256), F32)],
+        scratch_shapes=[pltpu.VMEM((2, 1024, 256), F32), pltpu.VMEM((1, 256), F32)],
         compiler_params=params(14),
         name="partial_gradient",
-    )(idx1, *a_own, *a_oth, b)
+    )(idx1, a_own, a_oth, *cot)
 
     got = lax.all_to_all(partial.astype(F16), "tok", 0, 0, tiled=True)
     mine = jnp.sum(unpack(got), axis=0).astype(BF16)
     theirs = sibling(mine)
-    piece = jnp.where(co == 0, jnp.stack([mine, theirs]), jnp.stack([theirs, mine]))
-    ring = []
-    for i in range(Z):
-        ring += [(2 * i, 2 * ((i + 1) % Z)), (2 * i + 1, 2 * ((i - 1) % Z) + 1)]
-    runs, others = [piece], []
-    for s in range(1, 5):
-        src = runs[-1]
-        if s == 4:
-            src = lax.dynamic_slice_in_dim(src, co * 64, 64, 1)
-        runs.append(lax.ppermute(src, ("tok", "co"), ring))
-        others.append(sibling(runs[-1]))
+    piece = pl.pallas_call(
+        merge_kernel, out_shape=sds((2, 128, 512), BF16), in_specs=[SMEM, VMEM, VMEM], out_specs=VMEM,
+        compiler_params=params(2), name="merge",
+    )(idx2, mine, theirs)
+
+    def pass_on(x, n):
+        perm = []
+        for i in range(Z):
+            perm += [(2 * i, 2 * ((i + n) % Z)), (2 * i + 1, 2 * ((i - n) % Z) + 1)]
+        return lax.ppermute(x, ("tok", "co"), perm)
+
+    two = pass_on(piece, 2)
+    one = pass_on(piece, 1)
+    half = pl.pallas_call(
+        half_kernel, out_shape=sds((2, 64, 512), BF16), in_specs=[SMEM, VMEM], out_specs=VMEM,
+        compiler_params=params(2), name="half",
+    )(idx2, two)
+    runs = [piece, one, two, pass_on(two, 1), pass_on(half, 2)]
+    others = [sibling(r) for r in runs[1:]]
 
     root, grad, rows = pl.pallas_call(
         chain_kernel,

time: 166 us -> 176 us (1.060)
  the two profiles are of different devices: /device:TPU:1 before, /device:TPU:35 now
where the time goes in v1:
time: 176 us
  waiting for transfers between devices  58.8 us (33%)
  starting transfers between devices  55 us (31%)
  Pallas kernels  29.2 us (17%)
  blocking collectives  16.4 us (9%)
  local copies, waits for them, and re-layouts  10.9 us (6%)
  other arithmetic  3.64 us (2%)
    ppermute x4, waiting for transfers between devices, around(): up.append(lax.ppermute(up[-1], 'tok', [(i, (i + 1) % Z) for i in range(Z)]))  28.3 us
    pallas_call x1, Pallas kernels, step(): pl.pallas_call(chain_kernel, out_shape=(sds((4, 1024, 256), BF16), sds((4...  18.1 us
    all_to_all x1, blocking collectives, everyone(): lax.all_to_all(jnp.broadcast_to(x, (n, *x.shape)), axis, 0, 0, tiled=True)  16.4 us
    ppermute x4, starting transfers between devices, pass_on(): return lax.ppermute(x, ('tok', 'co'), perm)  9.23 us
    all_to_all x1, starting transfers between devices, step(): got = lax.all_to_all(partial.astype(F16), 'tok', 0, 0, tiled=True)  8.62 us
    ppermute x7, starting transfers between devices, sibling(): return lax.ppermute(x, 'co', [(0, 1), (1, 0)])  8.52 us
    unnamed x14, local copies, waits for them, and re-layouts  8.4 us
    ppermute x1, waiting for transfers between devices, step(): cot = [lax.ppermute(output_grads, ('y', 'xl', 'pair'), table)]  7.54 us
  transfers between devices with their start and end apart: 26, of which 13 were waited for; matrix products, arithmetic and copies ran while one was open for 7% of the time, Pallas kernels for 6%

profile of v1, /device:TPU:35, one launch (start us, length us, event | category | flops | bytes accessed | tf_op | source)
XLA Modules:
  0.0 175.6 jit_solution(12545081442194151264)
XLA Ops:
  1.7 16.4 %all_to_all.10.a_own = bf16[4,512,256]{2,1,0:T(8,128)(2,1)S(1)} all-to-all(bf16[4,512,256]{2,1,0:T(8,128)(2,1)S(1)} %broadcast_in_dim.10), channel_id=1, replica_groups=mesh['tok'=8,'y'=4,'xl'=2,'co'=2,'pair'=2] {'xl','pair'}, dimensions={0} | all-to-all | bytes 2097152 | tf_op jit(solution)/shard_map/all_to_all | solution.py:225
  18.1 2.2 %collective-permute-start.8 = (bf16[4,512,256]{2,1,0:T(8,128)(2,1)S(1)}, bf16[4,512,256]{2,1,0:T(8,128)(2,1)S(1)}, u32[]{:S(2)}, u32[]{:S(2)}) collective-permute-start(bf16[4,512,256]{2,1,0:T(8,128)(2,1)S(1)} %all_to_all.10.a_own), channel_id=1, source_target_pairs={{0,2},{2,0},{1,3},{3,1},{4,6},{6,4},{5,7},{7,5},{8,10},{10,8},{9,1... | collective-permute-start | bytes 3145736 | tf_op jit(solution)/shard_map/ppermute | solution.py:229
  20.3 5.8 %collective-permute-start.9 = (bf16[512,256]{1,0:T(8,128)(2,1)}, bf16[512,256]{1,0:T(8,128)(2,1)S(1)}, u32[]{:S(2)}, u32[]{:S(2)}) collective-permute-start(bf16[512,256]{1,0:T(8,128)(2,1)} %param.4), channel_id=1, source_target_pairs={{0,0},{1,8},{4,16},{5,24},{8,1},{9,9},{12,17},{13,25},{16,4},{17,1... | collective-permute-start | bytes 786440 | tf_op jit(solution)/shard_map/ppermute | solution.py:248
  29.9 7.5 %collective-permute-done.9.b0 = bf16[512,256]{1,0:T(8,128)(2,1)S(1)} collective-permute-done((bf16[512,256]{1,0:T(8,128)(2,1)}, bf16[512,256]{1,0:T(8,128)(2,1)S(1)}, u32[]{:S(2)}, u32[]{:S(2)}) %collective-permute-start.9) | collective-permute-done | bytes 262176 | tf_op jit(solution)/shard_map/ppermute | solution.py:248
  38.5 2.2 %collective-permute-start.10 = (bf16[512,256]{1,0:T(8,128)(2,1)S(1)}, bf16[512,256]{1,0:T(8,128)(2,1)S(1)}, u32[]{:S(2)}, u32[]{:S(2)}) collective-permute-start(bf16[512,256]{1,0:T(8,128)(2,1)S(1)} %collective-permute-done.9.b0), channel_id=1, source_target_pairs={{0,8},{8,0},{16,24},{24,16},{1,9},{9,1},{17,25},{25,17},{2,10},{10... | collective-permute-start | bytes 786440 | tf_op jit(solution)/shard_map/ppermute | solution.py:251
  41.5 4.3 %collective-permute-done.4 = f16[144,640]{1,0:T(8,128)(2,1)S(1)} collective-permute-done((f16[144,640]{1,0:T(8,128)(2,1)}, f16[144,640]{1,0:T(8,128)(2,1)S(1)}, u32[]{:S(2)}, u32[]{:S(2)}) %collective-permute-start.4) | collective-permute-done | bytes 184352 | tf_op jit(solution)/shard_map/ppermute | solution.py:237
  47.5 4.0 %collective-permute-done.12.b3 = bf16[512,256]{1,0:T(8,128)(2,1)S(1)} collective-permute-done((bf16[512,256]{1,0:T(8,128)(2,1)S(1)}, bf16[512,256]{1,0:T(8,128)(2,1)S(1)}, u32[]{:S(2)}, u32[]{:S(2)}) %collective-permute-start.12) | collective-permute-done | bytes 262176 | tf_op jit(solution)/shard_map/ppermute | solution.py:251
  51.7 2.1 %partial_gradient.1 = f32[8,144,512]{2,1,0:T(8,128)S(1)} custom-call(s32[3]{0:T(128)S(1)} %pad_add_fusion.1.idx, bf16[4,512,256]{2,1,0:T(8,128)(2,1)S(1)} %all_to_all.10.a_own, bf16[4,512,256]{2,1,0:T(8,128)(2,1)S(1)} %collective-permute-done.8.a_oth, bf16[512,256]{1,0:T(8,128)(2,1)S(1)} %collective-permute-done.9.b0, ...), custom_call_target="tpu_custom_call" | custom-call | tf_op jit(solution)/shard_map/partial_gradient/pallas_call | solution.py:269
  55.2 8.6 %all-to-all-start.1 = ((f16[8,144,512]{2,1,0:T(8,128)(2,1)}), f16[8,144,512]{2,1,0:T(8,128)(2,1)S(1)}, u32[]{:S(2)}, u32[]{:S(2)}) async-start(f16[8,144,512]{2,1,0:T(8,128)(2,1)} %convert_element_type.29), calls=%async_computation.1 | async-start | bytes 2359296 | tf_op jit(solution)/shard_map/all_to_all | solution.py:279
  68.5 24.9 %collective-permute-done.2 = f16[144,640]{1,0:T(8,128)(2,1)S(1)} collective-permute-done((f16[144,640]{1,0:T(8,128)(2,1)}, f16[144,640]{1,0:T(8,128)(2,1)S(1)}, u32[]{:S(2)}, u32[]{:S(2)}) %collective-permute-start.2) | collective-permute-done | bytes 184352 | tf_op jit(solution)/shard_map/ppermute | solution.py:235
  93.4 2.3 %collective-permute-start.3 = (f16[144,640]{1,0:T(8,128)(2,1)S(1)}, f16[144,640]{1,0:T(8,128)(2,1)S(1)}, u32[]{:S(2)}, u32[]{:S(2)}) collective-permute-start(f16[144,640]{1,0:T(8,128)(2,1)S(1)} %collective-permute-done.2), channel_id=1, source_target_pairs={{0,32},{32,64},{64,96},{96,128},{128,160},{160,192},{192,224},{224... | collective-permute-start | bytes 552968 | tf_op jit(solution)/shard_map/ppermute | solution.py:235
  96.4 3.5 %collective-permute-done.3 = f16[144,640]{1,0:T(8,128)(2,1)S(1)} collective-permute-done((f16[144,640]{1,0:T(8,128)(2,1)S(1)}, f16[144,640]{1,0:T(8,128)(2,1)S(1)}, u32[]{:S(2)}, u32[]{:S(2)}) %collective-permute-start.3) | collective-permute-done | bytes 184352 | tf_op jit(solution)/shard_map/ppermute | solution.py:235
  103.6 7.4 %collective-permute-start.7 = (f16[8,144,640]{2,1,0:T(8,128)(2,1)}, f16[8,144,640]{2,1,0:T(8,128)(2,1)S(1)}, u32[]{:S(2)}, u32[]{:S(2)}) collective-permute-start(f16[8,144,640]{2,1,0:T(8,128)(2,1)} %bitcast_dynamic-update-slice_fusion), channel_id=1, source_target_pairs={{0,0},{1,2},{2,1},{3,3},{4,4},{5,6},{6,5},{7,7},{8,8},{9,10},{10,9... | collective-permute-start | bytes 4423688 | tf_op jit(solution)/shard_map/ppermute | solution.py:259
  113.3 2.6 %collective-permute-start.15 = (bf16[2,128,512]{2,1,0:T(8,128)(2,1)S(1)}, bf16[2,128,512]{2,1,0:T(8,128)(2,1)S(1)}, u32[]{:S(2)}, u32[]{:S(2)}) collective-permute-start(bf16[2,128,512]{2,1,0:T(8,128)(2,1)S(1)} %merge.1.g0), channel_id=1, source_target_pairs={{0,64},{2,194},{32,96},{34,226},{64,128},{66,2},{96,160},{98,34},{... | collective-permute-start | bytes 786440 | tf_op jit(solution)/shard_map/ppermute | solution.py:291
  117.6 4.4 %collective-permute-done.15.src.r2 = bf16[2,128,512]{2,1,0:T(8,128)(2,1)S(1)} collective-permute-done((bf16[2,128,512]{2,1,0:T(8,128)(2,1)S(1)}, bf16[2,128,512]{2,1,0:T(8,128)(2,1)S(1)}, u32[]{:S(2)}, u32[]{:S(2)}) %collective-permute-start.15) | collective-permute-done | bytes 262176 | tf_op jit(solution)/shard_map/ppermute | solution.py:291
  124.4 3.1 %collective-permute-start.17 = (bf16[2,64,512]{2,1,0:T(8,128)(2,1)S(1)}, bf16[2,64,512]{2,1,0:T(8,128)(2,1)S(1)}, u32[]{:S(2)}, u32[]{:S(2)}) collective-permute-start(bf16[2,64,512]{2,1,0:T(8,128)(2,1)S(1)} %half.1), channel_id=1, source_target_pairs={{0,64},{2,194},{32,96},{34,226},{64,128},{66,2},{96,160},{98,34},{... | collective-permute-start | bytes 393224 | tf_op jit(solution)/shard_map/ppermute | solution.py:291
  128.3 2.1 %collective-permute-start.19 = (bf16[2,128,512]{2,1,0:T(8,128)(2,1)S(1)}, bf16[2,128,512]{2,1,0:T(8,128)(2,1)S(1)}, u32[]{:S(2)}, u32[]{:S(2)}) collective-permute-start(bf16[2,128,512]{2,1,0:T(8,128)(2,1)S(1)} %collective-permute-done.15.src.r2), channel_id=1, source_target_pairs={{0,2},{2,0},{1,3},{3,1},{4,6},{6,4},{5,7},{7,5},{8,10},{10,8},{9,1... | collective-permute-start | bytes 786440 | tf_op jit(solution)/shard_map/ppermute | solution.py:229
  130.6 2.0 %collective-permute-done.17.r4 = bf16[2,64,512]{2,1,0:T(8,128)(2,1)S(1)} collective-permute-done((bf16[2,64,512]{2,1,0:T(8,128)(2,1)S(1)}, bf16[2,64,512]{2,1,0:T(8,128)(2,1)S(1)}, u32[]{:S(2)}, u32[]{:S(2)}) %collective-permute-start.17) | collective-permute-done | bytes 131104 | tf_op jit(solution)/shard_map/ppermute | solution.py:291
  132.6 3.9 %collective-permute-start.21 = (bf16[2,64,512]{2,1,0:T(8,128)(2,1)S(1)}, bf16[2,64,512]{2,1,0:T(8,128)(2,1)S(1)}, u32[]{:S(2)}, u32[]{:S(2)}) collective-permute-start(bf16[2,64,512]{2,1,0:T(8,128)(2,1)S(1)} %collective-permute-done.17.r4), channel_id=1, source_target_pairs={{0,2},{2,0},{1,3},{3,1},{4,6},{6,4},{5,7},{7,5},{8,10},{10,8},{9,1... | collective-permute-start | bytes 393224 | tf_op jit(solution)/shard_map/ppermute | solution.py:229
  138.1 18.1 %inverse_root.1 = (bf16[4,1024,256]{2,1,0:T(8,128)(2,1)S(1)}, bf16[4,1024,256]{2,1,0:T(8,128)(2,1)S(1)}, f32[128,1024]{1,0:T(8,128)S(1)}) custom-call(s32[2]{0:T(128)S(1)} %pad_add_fusion.idx, f32[8,1024,128]{2,1,0:T(8,128)S(1)} %assemble.1.st, bf16[2,128,512]{2,1,0:T(8,128)(2,1)S(1)} %merge.1.g0, bf16[2,128,512]{2,1,0:T(8,128)(2,1)S(1)} %collective-permute-done.14.r1, ...), custom_call_target="tpu_custom_call" | custom-call | tf_op jit(solution)/shard_map/inverse_root/pallas_call | solution.py:302
  156.2 2.3 %collective-permute-start.24 = (f32[128,1024]{1,0:T(8,128)S(1)}, f32[128,1024]{1,0:T(8,128)S(1)}, u32[]{:S(2)}, u32[]{:S(2)}) collective-permute-start(f32[128,1024]{1,0:T(8,128)S(1)} %get-tuple-element.7), channel_id=1, source_target_pairs={{0,0},{1,2},{2,1},{3,3},{4,4},{5,6},{6,5},{7,7},{8,8},{9,10},{10,9... | collective-permute-start | bytes 1572872 | tf_op jit(solution)/shard_map/ppermute | solution.py:315
  160.4 6.8 %update_rows.1 = bf16[64,1024]{1,0:T(8,128)(2,1)S(1)} custom-call(s32[2]{0:T(128)S(1)} %pad_add_fusion.idx, bf16[4,1024,256]{2,1,0:T(8,128)(2,1)S(1)} %get-tuple-element.5.own, bf16[4,1024,256]{2,1,0:T(8,128)(2,1)S(1)} %collective-permute-done.22.other, bf16[4,1024,256]{2,1,0:T(8,128)(2,1)S(1)} %get-tuple-element.6.grad), custom_call_target="tpu_custom_call" | custom-call | tf_op jit(solution)/shard_map/update_rows/pallas_call | solution.py:316
  167.2 3.0 %collective-permute-start.23 = (bf16[64,1024]{1,0:T(8,128)(2,1)S(1)}, bf16[64,1024]{1,0:T(8,128)(2,1)S(1)}, u32[]{:S(2)}, u32[]{:S(2)}) collective-permute-start(bf16[64,1024]{1,0:T(8,128)(2,1)S(1)} %update_rows.1), channel_id=1, source_target_pairs={{0,0},{1,2},{2,1},{3,3},{4,4},{5,6},{6,5},{7,7},{8,8},{9,10},{10,9... | collective-permute-start | bytes 393224 | tf_op jit(solution)/shard_map/ppermute | solution.py:325
  171.0 3.9 %collective-permute-done.23 = bf16[64,1024]{1,0:T(8,128)(2,1)S(1)} collective-permute-done((bf16[64,1024]{1,0:T(8,128)(2,1)S(1)}, bf16[64,1024]{1,0:T(8,128)(2,1)S(1)}, u32[]{:S(2)}, u32[]{:S(2)}) %collective-permute-start.23) | collective-permute-done | bytes 131104 | tf_op jit(solution)/shard_map/ppermute | solution.py:325
  (63 shorter events, 30.6 us)
Async XLA Ops:
  18.1 33.6 %collective-permute-start.8 = (bf16[4,512,256]{2,1,0:T(8,128)(2,1)S(1)}, bf16[4,512,256]{2,1,0:T(8,128)(2,1)S(1)}, u32[]{:S(2)}, u32[]{:S(2)}) collective-permute-start(bf16[4,512,256]{2,1,0:T(8,128)(2,1)S(1)} %all_to_all.10.a_own), channel_id=1, source_target_pairs={{0,2},{2,0},{1,3},{3,1},{4,6},{6,4},{5,7},{7,5},{8,10},{10,8},{9,1... | collective-permute-start | bytes 3145736 | tf_op jit(solution)/shard_map/ppermute | solution.py:229
  20.3 17.2 %collective-permute-start.9 = (bf16[512,256]{1,0:T(8,128)(2,1)}, bf16[512,256]{1,0:T(8,128)(2,1)S(1)}, u32[]{:S(2)}, u32[]{:S(2)}) collective-permute-start(bf16[512,256]{1,0:T(8,128)(2,1)} %param.4), channel_id=1, source_target_pairs={{0,0},{1,8},{4,16},{5,24},{8,1},{9,9},{12,17},{13,25},{16,4},{17,1... | collective-permute-start | bytes 786440 | tf_op jit(solution)/shard_map/ppermute | solution.py:248
  28.3 12.4 %collective-permute-start = (f16[144,640]{1,0:T(8,128)(2,1)}, f16[144,640]{1,0:T(8,128)(2,1)}, u32[]{:S(2)}, u32[]{:S(2)}) collective-permute-start(f16[144,640]{1,0:T(8,128)(2,1)} %concatenate.7), channel_id=1, source_target_pairs={{0,32},{32,64},{64,96},{96,128},{128,160},{160,192},{192,224},{224... | collective-permute-start | bytes 552968 | tf_op jit(solution)/shard_map/ppermute | solution.py:235
  37.5 14.0 %collective-permute-start.12 = (bf16[512,256]{1,0:T(8,128)(2,1)S(1)}, bf16[512,256]{1,0:T(8,128)(2,1)S(1)}, u32[]{:S(2)}, u32[]{:S(2)}) collective-permute-start(bf16[512,256]{1,0:T(8,128)(2,1)S(1)} %collective-permute-done.9.b0), channel_id=1, source_target_pairs={{0,24},{8,16},{16,8},{24,0},{1,25},{9,17},{17,9},{25,1},{2,26},{10... | collective-permute-start | bytes 786440 | tf_op jit(solution)/shard_map/ppermute | solution.py:251
  38.3 13.2 %collective-permute-start.11 = (bf16[512,256]{1,0:T(8,128)(2,1)S(1)}, bf16[512,256]{1,0:T(8,128)(2,1)S(1)}, u32[]{:S(2)}, u32[]{:S(2)}) collective-permute-start(bf16[512,256]{1,0:T(8,128)(2,1)S(1)} %collective-permute-done.9.b0), channel_id=1, source_target_pairs={{0,16},{8,24},{16,0},{24,8},{1,17},{9,25},{17,1},{25,9},{2,18},{10... | collective-permute-start | bytes 786440 | tf_op jit(solution)/shard_map/ppermute | solution.py:251
  38.5 13.2 %collective-permute-start.10 = (bf16[512,256]{1,0:T(8,128)(2,1)S(1)}, bf16[512,256]{1,0:T(8,128)(2,1)S(1)}, u32[]{:S(2)}, u32[]{:S(2)}) collective-permute-start(bf16[512,256]{1,0:T(8,128)(2,1)S(1)} %collective-permute-done.9.b0), channel_id=1, source_target_pairs={{0,8},{8,0},{16,24},{24,16},{1,9},{9,1},{17,25},{25,17},{2,10},{10... | collective-permute-start | bytes 786440 | tf_op jit(solution)/shard_map/ppermute | solution.py:251
  40.7 5.1 %collective-permute-start.4 = (f16[144,640]{1,0:T(8,128)(2,1)}, f16[144,640]{1,0:T(8,128)(2,1)S(1)}, u32[]{:S(2)}, u32[]{:S(2)}) collective-permute-start(f16[144,640]{1,0:T(8,128)(2,1)} %concatenate.7), channel_id=1, source_target_pairs={{0,224},{32,0},{64,32},{96,64},{128,96},{160,128},{192,160},{224,1... | collective-permute-start | bytes 552968 | tf_op jit(solution)/shard_map/ppermute | solution.py:237
  45.8 19.6 %collective-permute-start.1 = (f16[144,640]{1,0:T(8,128)(2,1)}, f16[144,640]{1,0:T(8,128)(2,1)}, u32[]{:S(2)}, u32[]{:S(2)}) collective-permute-start(f16[144,640]{1,0:T(8,128)(2,1)} %collective-permute-done), channel_id=1, source_target_pairs={{0,32},{32,64},{64,96},{96,128},{128,160},{160,192},{192,224},{224... | collective-permute-start | bytes 552968 | tf_op jit(solution)/shard_map/ppermute | solution.py:235
  51.4 15.2 %collective-permute-start.5 = (f16[144,640]{1,0:T(8,128)(2,1)S(1)}, f16[144,640]{1,0:T(8,128)(2,1)}, u32[]{:S(2)}, u32[]{:S(2)}) collective-permute-start(f16[144,640]{1,0:T(8,128)(2,1)S(1)} %collective-permute-done.4), channel_id=1, source_target_pairs={{0,224},{32,0},{64,32},{96,64},{128,96},{160,128},{192,160},{224,1... | collective-permute-start | bytes 552968 | tf_op jit(solution)/shard_map/ppermute | solution.py:237
  55.2 55.9 %all-to-all-start.1 = ((f16[8,144,512]{2,1,0:T(8,128)(2,1)}), f16[8,144,512]{2,1,0:T(8,128)(2,1)S(1)}, u32[]{:S(2)}, u32[]{:S(2)}) async-start(f16[8,144,512]{2,1,0:T(8,128)(2,1)} %convert_element_type.29), calls=%async_computation.1 | async-start | bytes 2359296 | tf_op jit(solution)/shard_map/all_to_all | solution.py:279
  65.4 28.0 %collective-permute-start.2 = (f16[144,640]{1,0:T(8,128)(2,1)}, f16[144,640]{1,0:T(8,128)(2,1)S(1)}, u32[]{:S(2)}, u32[]{:S(2)}) collective-permute-start(f16[144,640]{1,0:T(8,128)(2,1)} %collective-permute-done.1), channel_id=1, source_target_pairs={{0,32},{32,64},{64,96},{96,128},{128,160},{160,192},{192,224},{224... | collective-permute-start | bytes 552968 | tf_op jit(solution)/shard_map/ppermute | solution.py:235
  66.6 33.9 %collective-permute-start.6 = (f16[144,640]{1,0:T(8,128)(2,1)}, f16[144,640]{1,0:T(8,128)(2,1)S(1)}, u32[]{:S(2)}, u32[]{:S(2)}) collective-permute-start(f16[144,640]{1,0:T(8,128)(2,1)} %collective-permute-done.5), channel_id=1, source_target_pairs={{0,224},{32,0},{64,32},{96,64},{128,96},{160,128},{192,160},{224,1... | collective-permute-start | bytes 552968 | tf_op jit(solution)/shard_map/ppermute | solution.py:237
  93.4 6.4 %collective-permute-start.3 = (f16[144,640]{1,0:T(8,128)(2,1)S(1)}, f16[144,640]{1,0:T(8,128)(2,1)S(1)}, u32[]{:S(2)}, u32[]{:S(2)}) collective-permute-start(f16[144,640]{1,0:T(8,128)(2,1)S(1)} %collective-permute-done.2), channel_id=1, source_target_pairs={{0,32},{32,64},{64,96},{96,128},{128,160},{160,192},{192,224},{224... | collective-permute-start | bytes 552968 | tf_op jit(solution)/shard_map/ppermute | solution.py:235
  103.6 24.7 %collective-permute-start.7 = (f16[8,144,640]{2,1,0:T(8,128)(2,1)}, f16[8,144,640]{2,1,0:T(8,128)(2,1)S(1)}, u32[]{:S(2)}, u32[]{:S(2)}) collective-permute-start(f16[8,144,640]{2,1,0:T(8,128)(2,1)} %bitcast_dynamic-update-slice_fusion), channel_id=1, source_target_pairs={{0,0},{1,2},{2,1},{3,3},{4,4},{5,6},{6,5},{7,7},{8,8},{9,10},{10,9... | collective-permute-start | bytes 4423688 | tf_op jit(solution)/shard_map/ppermute | solution.py:259
  113.3 8.7 %collective-permute-start.15 = (bf16[2,128,512]{2,1,0:T(8,128)(2,1)S(1)}, bf16[2,128,512]{2,1,0:T(8,128)(2,1)S(1)}, u32[]{:S(2)}, u32[]{:S(2)}) collective-permute-start(bf16[2,128,512]{2,1,0:T(8,128)(2,1)S(1)} %merge.1.g0), channel_id=1, source_target_pairs={{0,64},{2,194},{32,96},{34,226},{64,128},{66,2},{96,160},{98,34},{... | collective-permute-start | bytes 786440 | tf_op jit(solution)/shard_map/ppermute | solution.py:291
  115.9 14.6 %collective-permute-start.14 = (bf16[2,128,512]{2,1,0:T(8,128)(2,1)S(1)}, bf16[2,128,512]{2,1,0:T(8,128)(2,1)S(1)}, u32[]{:S(2)}, u32[]{:S(2)}) collective-permute-start(bf16[2,128,512]{2,1,0:T(8,128)(2,1)S(1)} %merge.1.g0), channel_id=1, source_target_pairs={{0,32},{2,226},{32,64},{34,2},{64,96},{66,34},{96,128},{98,66},{12... | collective-permute-start | bytes 786440 | tf_op jit(solution)/shard_map/ppermute | solution.py:291
  122.0 14.5 %collective-permute-start.16 = (bf16[2,128,512]{2,1,0:T(8,128)(2,1)S(1)}, bf16[2,128,512]{2,1,0:T(8,128)(2,1)S(1)}, u32[]{:S(2)}, u32[]{:S(2)}) collective-permute-start(bf16[2,128,512]{2,1,0:T(8,128)(2,1)S(1)} %collective-permute-done.15.src.r2), channel_id=1, source_target_pairs={{0,32},{2,226},{32,64},{34,2},{64,96},{66,34},{96,128},{98,66},{12... | collective-permute-start | bytes 786440 | tf_op jit(solution)/shard_map/ppermute | solution.py:291
  124.4 8.2 %collective-permute-start.17 = (bf16[2,64,512]{2,1,0:T(8,128)(2,1)S(1)}, bf16[2,64,512]{2,1,0:T(8,128)(2,1)S(1)}, u32[]{:S(2)}, u32[]{:S(2)}) collective-permute-start(bf16[2,64,512]{2,1,0:T(8,128)(2,1)S(1)} %half.1), channel_id=1, source_target_pairs={{0,64},{2,194},{32,96},{34,226},{64,128},{66,2},{96,160},{98,34},{... | collective-permute-start | bytes 393224 | tf_op jit(solution)/shard_map/ppermute | solution.py:291
  128.3 9.7 %collective-permute-start.19 = (bf16[2,128,512]{2,1,0:T(8,128)(2,1)S(1)}, bf16[2,128,512]{2,1,0:T(8,128)(2,1)S(1)}, u32[]{:S(2)}, u32[]{:S(2)}) collective-permute-start(bf16[2,128,512]{2,1,0:T(8,128)(2,1)S(1)} %collective-permute-done.15.src.r2), channel_id=1, source_target_pairs={{0,2},{2,0},{1,3},{3,1},{4,6},{6,4},{5,7},{7,5},{8,10},{10,8},{9,1... | collective-permute-start | bytes 786440 | tf_op jit(solution)/shard_map/ppermute | solution.py:229
  130.5 7.6 %collective-permute-start.18 = (bf16[2,128,512]{2,1,0:T(8,128)(2,1)S(1)}, bf16[2,128,512]{2,1,0:T(8,128)(2,1)S(1)}, u32[]{:S(2)}, u32[]{:S(2)}) collective-permute-start(bf16[2,128,512]{2,1,0:T(8,128)(2,1)S(1)} %collective-permute-done.14.r1), channel_id=1, source_target_pairs={{0,2},{2,0},{1,3},{3,1},{4,6},{6,4},{5,7},{7,5},{8,10},{10,8},{9,1... | collective-permute-start | bytes 786440 | tf_op jit(solution)/shard_map/ppermute | solution.py:229
  132.6 5.4 %collective-permute-start.21 = (bf16[2,64,512]{2,1,0:T(8,128)(2,1)S(1)}, bf16[2,64,512]{2,1,0:T(8,128)(2,1)S(1)}, u32[]{:S(2)}, u32[]{:S(2)}) collective-permute-start(bf16[2,64,512]{2,1,0:T(8,128)(2,1)S(1)} %collective-permute-done.17.r4), channel_id=1, source_target_pairs={{0,2},{2,0},{1,3},{3,1},{4,6},{6,4},{5,7},{7,5},{8,10},{10,8},{9,1... | collective-permute-start | bytes 393224 | tf_op jit(solution)/shard_map/ppermute | solution.py:229
  156.1 4.2 %collective-permute-start.22 = (bf16[4,1024,256]{2,1,0:T(8,128)(2,1)S(1)}, bf16[4,1024,256]{2,1,0:T(8,128)(2,1)S(1)}, u32[]{:S(2)}, u32[]{:S(2)}) collective-permute-start(bf16[4,1024,256]{2,1,0:T(8,128)(2,1)S(1)} %get-tuple-element.5.own), channel_id=1, source_target_pairs={{0,2},{2,0},{1,3},{3,1},{4,6},{6,4},{5,7},{7,5},{8,10},{10,8},{9,1... | collective-permute-start | bytes 6291464 | tf_op jit(solution)/shard_map/ppermute | solution.py:229
  156.2 13.9 %collective-permute-start.24 = (f32[128,1024]{1,0:T(8,128)S(1)}, f32[128,1024]{1,0:T(8,128)S(1)}, u32[]{:S(2)}, u32[]{:S(2)}) collective-permute-start(f32[128,1024]{1,0:T(8,128)S(1)} %get-tuple-element.7), channel_id=1, source_target_pairs={{0,0},{1,2},{2,1},{3,3},{4,4},{5,6},{6,5},{7,7},{8,8},{9,10},{10,9... | collective-permute-start | bytes 1572872 | tf_op jit(solution)/shard_map/ppermute | solution.py:315
  167.2 7.8 %collective-permute-start.23 = (bf16[64,1024]{1,0:T(8,128)(2,1)S(1)}, bf16[64,1024]{1,0:T(8,128)(2,1)S(1)}, u32[]{:S(2)}, u32[]{:S(2)}) collective-permute-start(bf16[64,1024]{1,0:T(8,128)(2,1)S(1)} %update_rows.1), channel_id=1, source_target_pairs={{0,0},{1,2},{2,1},{3,3},{4,4},{5,6},{6,5},{7,7},{8,8},{9,10},{10,9... | collective-permute-start | bytes 393224 | tf_op jit(solution)/shard_map/ppermute | solution.py:325
  (4 other events, 38.2 us)

commit v2 on v1

--- a/solution.py
+++ b/solution.py
@@ -11,7 +11,6 @@
 F16 = jnp.float16
 VMEM = pl.BlockSpec(memory_space=pltpu.VMEM)
 SMEM = pl.BlockSpec(memory_space=pltpu.SMEM)
-HBM = pl.BlockSpec(memory_space=pltpu.HBM)
 Z = 8
 SWAP = [(0, 0), (1, 2), (2, 1), (3, 3)]
 
@@ -91,10 +90,8 @@
 
 
 def chain_kernel(idx, st, g0, r1, r2, r3, r4, o1, o2, o3, o4,
-                 root, grad, rows, s_s, x_s, before, f0, f1, t0, t1, sem):
+                 root, grad, rows, sq, s_s, x_s, f0, f1, t0, t1):
     z, co = idx[0], idx[1]
-    fetch = pltpu.make_async_copy(st, s_s, sem)
-    fetch.start()
     step = 1 - 2 * co
     pieces = [(g0, z, 0), (r1, z - step, 0), (r2, z - 2 * step, 0), (r3, z - 3 * step, 0),
               (o1, z + step, 0), (o2, z + 2 * step, 0), (o3, z + 3 * step, 0),
@@ -122,26 +119,25 @@
 
         loop(Z, body)
 
-    fetch.wait()
     zr = pl.multiple_of(z * 128, 128)
-    for j in range(Z):
-        before[:, 128 * j:128 * (j + 1)] = s_s[j, pl.ds(zr, 128), :]
-
-    def product(j):
+
+    def product(j, carry):
+        top, acc = carry
         r = pl.multiple_of(j * 256, 256)
         p = dot(cat(x_s), jnp.concatenate([x_s[k, pl.ds(r, 256), :] for k in range(Z)], axis=1), 1, 1)
-        s_s[2 * j] = s_s[2 * j] + 0.1 * p[:, :128]
-        s_s[2 * j + 1] = s_s[2 * j + 1] + 0.1 * p[:, 128:]
-
-    loop(4, product)
+        for h in range(2):
+            u = st[2 * j + h] + 0.1 * p[:, 128 * h:128 * (h + 1)]
+            s_s[2 * j + h] = u
+            top = jnp.maximum(top, jnp.sum(jnp.abs(u), axis=0, keepdims=True))
+        v = grad[j].astype(F32)
+        return top, acc + jnp.sum(v * v, axis=0, keepdims=True)
+
+    top, acc = lax.fori_loop(0, 4, product, (jnp.zeros((1, 128), F32), jnp.zeros((1, 256), F32)))
+    sq[...] = jnp.broadcast_to(jnp.sum(acc, axis=1, keepdims=True), sq.shape)
 
     for j in range(Z):
         c = slice(128 * j, 128 * (j + 1))
-        rows[:, c] = s_s[j, pl.ds(zr, 128), :] - before[:, c]
-    top = None
-    for j in range(Z):
-        m = jnp.sum(jnp.abs(s_s[j]), axis=0, keepdims=True)
-        top = m if top is None else jnp.maximum(top, m)
+        rows[:, c] = s_s[j, pl.ds(zr, 128), :] - st[j, pl.ds(zr, 128), :]
     bound = jnp.max(top, axis=1, keepdims=True)
     inv = 1.0 / (1.1 * bound)
     ridge = jnp.where(diagonal(128), 0.1 * bound, 0.0)
@@ -179,7 +175,7 @@
     mul(root, f0, t0)
 
 
-def update_kernel(idx, own, other, grad, out, mix, r_s, keep):
+def update_kernel(idx, own, other, grad, grad_sq, out, mix, r_s, keep):
     z, co = idx[0], idx[1]
     zr = pl.multiple_of(z * 128 + co * 64, 64)
 
@@ -197,12 +193,7 @@
 
         update_sq = jnp.sum(lax.fori_loop(0, 4, raw, jnp.zeros((1, 256), F32)), axis=1, keepdims=True)
 
-        def square(j, acc):
-            v = grad[j].astype(F32)
-            return acc + jnp.sum(v * v, axis=0, keepdims=True)
-
-        grad_sq = jnp.sum(lax.fori_loop(0, 4, square, jnp.zeros((1, 256), F32)), axis=1, keepdims=True)
-        ratio = jnp.sqrt(grad_sq / (update_sq + 1e-6))
+        ratio = jnp.sqrt(grad_sq[:1, :1] / (update_sq + 1e-6))
         for j in range(4):
             out[:, 256 * j:256 * (j + 1)] = (keep[j] * ratio).astype(BF16)
 
@@ -229,13 +220,8 @@
     return lax.ppermute(x, "co", [(0, 1), (1, 0)])
 
 
-def around(x):
-    up, down = [x], []
-    for k in range(1, 5):
-        up.append(lax.ppermute(up[-1], "tok", [(i, (i + 1) % Z) for i in range(Z)]))
-        if k < 4:
-            down.append(lax.ppermute((down or [x])[-1], "tok", [(i, (i - 1) % Z) for i in range(Z)]))
-    return up + down[::-1]
+def along(x, d):
+    return lax.ppermute(x, "tok", [(i, (i + d) % Z) for i in range(Z)])
 
 
 def step(inputs, output_grads, statistics):
@@ -255,7 +241,22 @@
     wide = jnp.concatenate([stat, stat[:, :512]], axis=1)
     part = lax.dynamic_slice(wide, (0, z * 128), (128, 640))
     part = pack(part, jnp.max(jnp.abs(stat)))
-    st = jnp.stack(around(part))
+    up2, down2 = along(part, 2), along(part, -2)
+    up1, down1 = along(part, 1), along(part, -1)
+
+    partial = pl.pallas_call(
+        partial_kernel,
+        out_shape=sds((Z, 144, 512), F32),
+        in_specs=[SMEM] + [VMEM] * 6,
+        out_specs=VMEM,
+        scratch_shapes=[pltpu.VMEM((2, 1024, 256), F32), pltpu.VMEM((1, 256), F32)],
+        compiler_params=params(14),
+        name="partial_gradient",
+    )(idx1, a_own, a_oth, *cot)
+
+    near = lax.optimization_barrier((partial[0, 128:136, :128], part, up1, up2, down2, down1))[1:]
+    far = [along(up2, 1), along(up2, 2), along(down2, -1)]
+    st = jnp.stack([*near[:3], *far, *near[3:]])
     st = lax.ppermute(st, ("co", "pair"), SWAP)
     st = pl.pallas_call(
         assemble_kernel,
@@ -266,16 +267,6 @@
         name="assemble",
     )(idx2, 0.9 * unpack(st))
 
-    partial = pl.pallas_call(
-        partial_kernel,
-        out_shape=sds((Z, 144, 512), F32),
-        in_specs=[SMEM] + [VMEM] * 6,
-        out_specs=VMEM,
-        scratch_shapes=[pltpu.VMEM((2, 1024, 256), F32), pltpu.VMEM((1, 256), F32)],
-        compiler_params=params(14),
-        name="partial_gradient",
-    )(idx1, a_own, a_oth, *cot)
-
     got = lax.all_to_all(partial.astype(F16), "tok", 0, 0, tiled=True)
     mine = jnp.sum(unpack(got), axis=0).astype(BF16)
     theirs = sibling(mine)
@@ -299,14 +290,13 @@
     runs = [piece, one, two, pass_on(two, 1), pass_on(half, 2)]
     others = [sibling(r) for r in runs[1:]]
 
-    root, grad, rows = pl.pallas_call(
+    root, grad, rows, grad_sq = pl.pallas_call(
         chain_kernel,
-        out_shape=(sds((4, 1024, 256), BF16), sds((4, 1024, 256), BF16), sds((128, 1024), F32)),
-        in_specs=[SMEM, HBM] + [VMEM] * 9,
-        out_specs=(VMEM,) * 3,
-        scratch_shapes=[pltpu.VMEM((8, 1024, 128), F32), pltpu.VMEM((8, 1024, 128), BF16),
-                        pltpu.VMEM((128, 1024), F32)] + [pltpu.VMEM((4, 1024, 256), BF16)] * 4
-        + [pltpu.SemaphoreType.DMA],
+        out_shape=(sds((4, 1024, 256), BF16), sds((4, 1024, 256), BF16), sds((128, 1024), F32), sds((8, 128), F32)),
+        in_specs=[SMEM] + [VMEM] * 10,
+        out_specs=(VMEM,) * 4,
+        scratch_shapes=[pltpu.VMEM((8, 1024, 128), F32), pltpu.VMEM((8, 1024, 128), BF16)]
+        + [pltpu.VMEM((4, 1024, 256), BF16)] * 4,
         compiler_params=params(22),
         name="inverse_root",
     )(idx2, st, *runs, *others)
@@ -316,12 +306,12 @@
     final = pl.pallas_call(
         update_kernel,
         out_shape=sds((64, 1024), BF16),
-        in_specs=[SMEM] + [VMEM] * 3,
+        in_specs=[SMEM] + [VMEM] * 4,
         out_specs=VMEM,
         scratch_shapes=[pltpu.VMEM((4, 1024, 256), BF16), pltpu.VMEM((1024, 256), F32), pltpu.VMEM((4, 64, 256), F32)],
         compiler_params=params(16),
         name="update_rows",
-    )(idx2, root, other_root, grad)
+    )(idx2, root, other_root, grad, grad_sq)
     update = lax.ppermute(final, ("co", "pair"), SWAP)
     new_rows = 0.9 * stat + back
     return update[None], new_rows[None, None]

time: 176 us -> 188 us (1.068)
  the two profiles are of different devices: /device:TPU:35 before, /device:TPU:33 now
where the time goes in v2:
time: 188 us; the launch traced here: 186 us
  starting transfers between devices  70.6 us (38%)
  waiting for transfers between devices  53.1 us (28%)
  Pallas kernels  28.2 us (15%)
  blocking collectives  17.8 us (9%)
  local copies, waits for them, and re-layouts  9.3 us (5%)
  other arithmetic  5.9 us (3%)
    ppermute x7, waiting for transfers between devices, along(): return lax.ppermute(x, 'tok', [(i, (i + d) % Z) for i in range(Z)])  31.3 us
    ppermute x7, starting transfers between devices, sibling(): return lax.ppermute(x, 'co', [(0, 1), (1, 0)])  19 us
    all_to_all x1, blocking collectives, everyone(): lax.all_to_all(jnp.broadcast_to(x, (n, *x.shape)), axis, 0, 0, tiled=True)  17.8 us
    pallas_call x1, Pallas kernels, step(): pl.pallas_call(chain_kernel, out_shape=(sds((4, 1024, 256), BF16), sds((4...  17.4 us
    ppermute x7, starting transfers between devices, along(): return lax.ppermute(x, 'tok', [(i, (i + d) % Z) for i in range(Z)])  12.3 us
    ppermute x3, starting transfers between devices, step(): cot.append(lax.ppermute(cot[0], 'y', [(i, i ^ d) for i in range(4)]))  10.7 us
    ppermute x3, waiting for transfers between devices, step(): cot.append(lax.ppermute(cot[0], 'y', [(i, i ^ d) for i in range(4)]))  9.15 us
    ppermute x4, starting transfers between devices, pass_on(): return lax.ppermute(x, ('tok', 'co'), perm)  8.94 us
  transfers between devices with their start and end apart: 26, of which 10 were waited for; matrix products, arithmetic and copies ran while one was open for 6% of the time, Pallas kernels for 5%

profile of v2, /device:TPU:33, one launch (start us, length us, event | category | flops | bytes accessed | tf_op | source)
XLA Modules:
  0.0 186.5 jit_solution(5439602863383285006)
XLA Ops:
  1.7 17.8 %all_to_all.10.a_own = bf16[4,512,256]{2,1,0:T(8,128)(2,1)S(1)} all-to-all(bf16[4,512,256]{2,1,0:T(8,128)(2,1)S(1)} %broadcast_in_dim.10), channel_id=1, replica_groups=mesh['tok'=8,'y'=4,'xl'=2,'co'=2,'pair'=2] {'xl','pair'}, dimensions={0} | all-to-all | bytes 2097152 | tf_op jit(solution)/shard_map/all_to_all | solution.py:216
  19.5 1.8 collective-permute-start.8
  24.5 5.8 %collective-permute-start.2 = (f16[144,640]{1,0:T(8,128)(2,1)S(1)}, f16[144,640]{1,0:T(8,128)(2,1)S(1)}, u32[]{:S(2)}, u32[]{:S(2)}) collective-permute-start(f16[144,640]{1,0:T(8,128)(2,1)S(1)} %concatenate.7), channel_id=1, source_target_pairs={{0,192},{32,224},{64,0},{96,32},{128,64},{160,96},{192,128},{224,1... | collective-permute-start | bytes 552968 | tf_op jit(solution)/shard_map/ppermute | solution.py:224
  32.7 9.5 %collective-permute-start.12 = (bf16[512,256]{1,0:T(8,128)(2,1)S(1)}, bf16[512,256]{1,0:T(8,128)(2,1)S(1)}, u32[]{:S(2)}, u32[]{:S(2)}) collective-permute-start(bf16[512,256]{1,0:T(8,128)(2,1)S(1)} %collective-permute-done.9.b0), channel_id=1, source_target_pairs={{0,24},{8,16},{16,8},{24,0},{1,25},{9,17},{17,9},{25,1},{2,26},{10... | collective-permute-start | bytes 786440 | tf_op jit(solution)/shard_map/ppermute | solution.py:237
  45.2 8.8 %collective-permute-done.12.b3 = bf16[512,256]{1,0:T(8,128)(2,1)S(1)} collective-permute-done((bf16[512,256]{1,0:T(8,128)(2,1)S(1)}, bf16[512,256]{1,0:T(8,128)(2,1)S(1)}, u32[]{:S(2)}, u32[]{:S(2)}) %collective-permute-start.12) | collective-permute-done | bytes 262176 | tf_op jit(solution)/shard_map/ppermute | solution.py:237
  54.4 2.1 %partial_gradient.1 = f32[8,144,512]{2,1,0:T(8,128)S(1)} custom-call(s32[3]{0:T(128)S(1)} %pad_add_fusion.1.idx, bf16[4,512,256]{2,1,0:T(8,128)(2,1)S(1)} %all_to_all.10.a_own, bf16[4,512,256]{2,1,0:T(8,128)(2,1)S(1)} %collective-permute-done.8.a_oth, bf16[512,256]{1,0:T(8,128)(2,1)S(1)} %collective-permute-done.9.b0, ...), custom_call_target="tpu_custom_call" | custom-call | tf_op jit(solution)/shard_map/partial_gradient/pallas_call | solution.py:247
  57.9 7.8 %all-to-all-start.1 = ((f16[8,144,512]{2,1,0:T(8,128)(2,1)}), f16[8,144,512]{2,1,0:T(8,128)(2,1)S(1)}, u32[]{:S(2)}, u32[]{:S(2)}) async-start(f16[8,144,512]{2,1,0:T(8,128)(2,1)} %convert_element_type.29), calls=%async_computation.1 | async-start | bytes 2359296 | tf_op jit(solution)/shard_map/all_to_all | solution.py:270
  67.3 2.4 %collective-permute-start.5 = (f16[144,640]{1,0:T(8,128)(2,1)}, f16[144,640]{1,0:T(8,128)(2,1)S(1)}, u32[]{:S(2)}, u32[]{:S(2)}) collective-permute-start(f16[144,640]{1,0:T(8,128)(2,1)} %collective-permute-done.1), channel_id=1, source_target_pairs={{0,64},{32,96},{64,128},{96,160},{128,192},{160,224},{192,0},{224,... | collective-permute-start | bytes 552968 | tf_op jit(solution)/shard_map/ppermute | solution.py:224
  69.7 2.4 %collective-permute-start.4 = (f16[144,640]{1,0:T(8,128)(2,1)}, f16[144,640]{1,0:T(8,128)(2,1)S(1)}, u32[]{:S(2)}, u32[]{:S(2)}) collective-permute-start(f16[144,640]{1,0:T(8,128)(2,1)} %collective-permute-done.1), channel_id=1, source_target_pairs={{0,32},{32,64},{64,96},{96,128},{128,160},{160,192},{192,224},{224... | collective-permute-start | bytes 552968 | tf_op jit(solution)/shard_map/ppermute | solution.py:224
  72.1 1.7 bitcast_dynamic-update-slice_fusion.5
  73.7 29.6 %collective-permute-done.4 = f16[144,640]{1,0:T(8,128)(2,1)S(1)} collective-permute-done((f16[144,640]{1,0:T(8,128)(2,1)}, f16[144,640]{1,0:T(8,128)(2,1)S(1)}, u32[]{:S(2)}, u32[]{:S(2)}) %collective-permute-start.4) | collective-permute-done | bytes 184352 | tf_op jit(solution)/shard_map/ppermute | solution.py:224
  106.8 5.4 %collective-permute-start.7 = (f16[8,144,640]{2,1,0:T(8,128)(2,1)}, f16[8,144,640]{2,1,0:T(8,128)(2,1)}, u32[]{:S(2)}, u32[]{:S(2)}) collective-permute-start(f16[8,144,640]{2,1,0:T(8,128)(2,1)} %bitcast_dynamic-update-slice_fusion), channel_id=1, source_target_pairs={{0,0},{1,2},{2,1},{3,3},{4,4},{5,6},{6,5},{7,7},{8,8},{9,10},{10,9... | collective-permute-start | bytes 4423688 | tf_op jit(solution)/shard_map/ppermute | solution.py:260
  112.5 8.7 %collective-permute-start.13 = (bf16[128,512]{1,0:T(8,128)(2,1)S(1)}, bf16[128,512]{1,0:T(8,128)(2,1)S(1)}, u32[]{:S(2)}, u32[]{:S(2)}) collective-permute-start(bf16[128,512]{1,0:T(8,128)(2,1)S(1)} %multiply_reduce_fusion.mine), channel_id=1, source_target_pairs={{0,2},{2,0},{1,3},{3,1},{4,6},{6,4},{5,7},{7,5},{8,10},{10,8},{9,1... | collective-permute-start | bytes 393224 | tf_op jit(solution)/shard_map/ppermute | solution.py:220
  122.8 3.7 %collective-permute-start.15 = (bf16[2,128,512]{2,1,0:T(8,128)(2,1)S(1)}, bf16[2,128,512]{2,1,0:T(8,128)(2,1)S(1)}, u32[]{:S(2)}, u32[]{:S(2)}) collective-permute-start(bf16[2,128,512]{2,1,0:T(8,128)(2,1)S(1)} %merge.1.g0), channel_id=1, source_target_pairs={{0,64},{2,194},{32,96},{34,226},{64,128},{66,2},{96,160},{98,34},{... | collective-permute-start | bytes 786440 | tf_op jit(solution)/shard_map/ppermute | solution.py:282
  127.5 5.0 %collective-permute-done.15.src.r2 = bf16[2,128,512]{2,1,0:T(8,128)(2,1)S(1)} collective-permute-done((bf16[2,128,512]{2,1,0:T(8,128)(2,1)S(1)}, bf16[2,128,512]{2,1,0:T(8,128)(2,1)S(1)}, u32[]{:S(2)}, u32[]{:S(2)}) %collective-permute-start.15) | collective-permute-done | bytes 262176 | tf_op jit(solution)/shard_map/ppermute | solution.py:282
  133.8 3.4 %collective-permute-start.17 = (bf16[2,64,512]{2,1,0:T(8,128)(2,1)S(1)}, bf16[2,64,512]{2,1,0:T(8,128)(2,1)S(1)}, u32[]{:S(2)}, u32[]{:S(2)}) collective-permute-start(bf16[2,64,512]{2,1,0:T(8,128)(2,1)S(1)} %half.1), channel_id=1, source_target_pairs={{0,64},{2,194},{32,96},{34,226},{64,128},{66,2},{96,160},{98,34},{... | collective-permute-start | bytes 393224 | tf_op jit(solution)/shard_map/ppermute | solution.py:282
  138.2 3.1 %collective-permute-start.19 = (bf16[2,128,512]{2,1,0:T(8,128)(2,1)S(1)}, bf16[2,128,512]{2,1,0:T(8,128)(2,1)S(1)}, u32[]{:S(2)}, u32[]{:S(2)}) collective-permute-start(bf16[2,128,512]{2,1,0:T(8,128)(2,1)S(1)} %collective-permute-done.15.src.r2), channel_id=1, source_target_pairs={{0,2},{2,0},{1,3},{3,1},{4,6},{6,4},{5,7},{7,5},{8,10},{10,8},{9,1... | collective-permute-start | bytes 786440 | tf_op jit(solution)/shard_map/ppermute | solution.py:220
  141.9 5.2 %collective-permute-start.21 = (bf16[2,64,512]{2,1,0:T(8,128)(2,1)S(1)}, bf16[2,64,512]{2,1,0:T(8,128)(2,1)S(1)}, u32[]{:S(2)}, u32[]{:S(2)}) collective-permute-start(bf16[2,64,512]{2,1,0:T(8,128)(2,1)S(1)} %collective-permute-done.17.r4), channel_id=1, source_target_pairs={{0,2},{2,0},{1,3},{3,1},{4,6},{6,4},{5,7},{7,5},{8,10},{10,8},{9,1... | collective-permute-start | bytes 393224 | tf_op jit(solution)/shard_map/ppermute | solution.py:220
  149.9 17.4 %inverse_root.1 = (bf16[4,1024,256]{2,1,0:T(8,128)(2,1)S(1)}, bf16[4,1024,256]{2,1,0:T(8,128)(2,1)S(1)}, f32[128,1024]{1,0:T(8,128)S(1)}, f32[8,128]{1,0:T(8,128)S(1)}) custom-call(s32[2]{0:T(128)S(1)} %pad_add_fusion.idx, f32[8,1024,128]{2,1,0:T(8,128)S(1)} %assemble.1.st, bf16[2,128,512]{2,1,0:T(8,128)(2,1)S(1)} %merge.1.g0, ...), custom_call_target="tpu_custom_call" | custom-call | tf_op jit(solution)/shard_map/inverse_root/pallas_call | solution.py:293
  167.5 1.9 %collective-permute-start.24 = (f32[128,1024]{1,0:T(8,128)S(1)}, f32[128,1024]{1,0:T(8,128)S(1)}, u32[]{:S(2)}, u32[]{:S(2)}) collective-permute-start(f32[128,1024]{1,0:T(8,128)S(1)} %get-tuple-element.19), channel_id=1, source_target_pairs={{0,0},{1,2},{2,1},{3,3},{4,4},{5,6},{6,5},{7,7},{8,8},{9,10},{10,9... | collective-permute-start | bytes 1572872 | tf_op jit(solution)/shard_map/ppermute | solution.py:305
  169.4 2.2 %collective-permute-done.22.other = bf16[4,1024,256]{2,1,0:T(8,128)(2,1)S(1)} collective-permute-done((bf16[4,1024,256]{2,1,0:T(8,128)(2,1)S(1)}, bf16[4,1024,256]{2,1,0:T(8,128)(2,1)S(1)}, u32[]{:S(2)}, u32[]{:S(2)}) %collective-permute-start.22) | collective-permute-done | bytes 2097184 | tf_op jit(solution)/shard_map/ppermute | solution.py:220
  171.6 6.4 %update_rows.1 = bf16[64,1024]{1,0:T(8,128)(2,1)S(1)} custom-call(s32[2]{0:T(128)S(1)} %pad_add_fusion.idx, bf16[4,1024,256]{2,1,0:T(8,128)(2,1)S(1)} %get-tuple-element.16.own, bf16[4,1024,256]{2,1,0:T(8,128)(2,1)S(1)} %collective-permute-done.22.other, bf16[4,1024,256]{2,1,0:T(8,128)(2,1)S(1)} %get-tuple-element.17.grad, ...), custom_call_target="tpu_custom_call" | custom-call | tf_op jit(solution)/shard_map/update_rows/pallas_call | solution.py:306
  178.0 2.9 %collective-permute-start.23 = (bf16[64,1024]{1,0:T(8,128)(2,1)S(1)}, bf16[64,1024]{1,0:T(8,128)(2,1)S(1)}, u32[]{:S(2)}, u32[]{:S(2)}) collective-permute-start(bf16[64,1024]{1,0:T(8,128)(2,1)S(1)} %update_rows.1), channel_id=1, source_target_pairs={{0,0},{1,2},{2,1},{3,3},{4,4},{5,6},{6,5},{7,7},{8,8},{9,10},{10,9... | collective-permute-start | bytes 393224 | tf_op jit(solution)/shard_map/ppermute | solution.py:315
  181.9 4.0 %collective-permute-done.23 = bf16[64,1024]{1,0:T(8,128)(2,1)S(1)} collective-permute-done((bf16[64,1024]{1,0:T(8,128)(2,1)S(1)}, bf16[64,1024]{1,0:T(8,128)(2,1)S(1)}, u32[]{:S(2)}, u32[]{:S(2)}) %collective-permute-start.23) | collective-permute-done | bytes 131104 | tf_op jit(solution)/shard_map/ppermute | solution.py:315
  (61 shorter events, 25.8 us)
Async XLA Ops:
  19.5 34.9 %collective-permute-start.8 = (bf16[4,512,256]{2,1,0:T(8,128)(2,1)S(1)}, bf16[4,512,256]{2,1,0:T(8,128)(2,1)S(1)}, u32[]{:S(2)}, u32[]{:S(2)}) collective-permute-start(bf16[4,512,256]{2,1,0:T(8,128)(2,1)S(1)} %all_to_all.10.a_own), channel_id=1, source_target_pairs={{0,2},{2,0},{1,3},{3,1},{4,6},{6,4},{5,7},{7,5},{8,10},{10,8},{9,1... | collective-permute-start | bytes 3145736 | tf_op jit(solution)/shard_map/ppermute | solution.py:220
  21.3 11.4 %collective-permute-start.9 = (bf16[512,256]{1,0:T(8,128)(2,1)}, bf16[512,256]{1,0:T(8,128)(2,1)S(1)}, u32[]{:S(2)}, u32[]{:S(2)}) collective-permute-start(bf16[512,256]{1,0:T(8,128)(2,1)} %param.4), channel_id=1, source_target_pairs={{0,0},{1,8},{4,16},{5,24},{8,1},{9,9},{12,17},{13,25},{16,4},{17,1... | collective-permute-start | bytes 786440 | tf_op jit(solution)/shard_map/ppermute | solution.py:234
  24.4 6.6 %collective-permute-start.3 = (f16[144,640]{1,0:T(8,128)(2,1)S(1)}, f16[144,640]{1,0:T(8,128)(2,1)S(1)}, u32[]{:S(2)}, u32[]{:S(2)}) collective-permute-start(f16[144,640]{1,0:T(8,128)(2,1)S(1)} %concatenate.7), channel_id=1, source_target_pairs={{0,224},{32,0},{64,32},{96,64},{128,96},{160,128},{192,160},{224,1... | collective-permute-start | bytes 552968 | tf_op jit(solution)/shard_map/ppermute | solution.py:224
  24.5 17.7 %collective-permute-start.2 = (f16[144,640]{1,0:T(8,128)(2,1)S(1)}, f16[144,640]{1,0:T(8,128)(2,1)S(1)}, u32[]{:S(2)}, u32[]{:S(2)}) collective-permute-start(f16[144,640]{1,0:T(8,128)(2,1)S(1)} %concatenate.7), channel_id=1, source_target_pairs={{0,192},{32,224},{64,0},{96,32},{128,64},{160,96},{192,128},{224,1... | collective-permute-start | bytes 552968 | tf_op jit(solution)/shard_map/ppermute | solution.py:224
  30.4 11.8 %collective-permute-start.1 = (f16[144,640]{1,0:T(8,128)(2,1)S(1)}, f16[144,640]{1,0:T(8,128)(2,1)}, u32[]{:S(2)}, u32[]{:S(2)}) collective-permute-start(f16[144,640]{1,0:T(8,128)(2,1)S(1)} %concatenate.7), channel_id=1, source_target_pairs={{0,64},{32,96},{64,128},{96,160},{128,192},{160,224},{192,0},{224,... | collective-permute-start | bytes 552968 | tf_op jit(solution)/shard_map/ppermute | solution.py:224
  31.1 13.5 %collective-permute-start = (f16[144,640]{1,0:T(8,128)(2,1)S(1)}, f16[144,640]{1,0:T(8,128)(2,1)}, u32[]{:S(2)}, u32[]{:S(2)}) collective-permute-start(f16[144,640]{1,0:T(8,128)(2,1)S(1)} %concatenate.7), channel_id=1, source_target_pairs={{0,32},{32,64},{64,96},{96,128},{128,160},{160,192},{192,224},{224... | collective-permute-start | bytes 552968 | tf_op jit(solution)/shard_map/ppermute | solution.py:224
  32.7 21.4 %collective-permute-start.12 = (bf16[512,256]{1,0:T(8,128)(2,1)S(1)}, bf16[512,256]{1,0:T(8,128)(2,1)S(1)}, u32[]{:S(2)}, u32[]{:S(2)}) collective-permute-start(bf16[512,256]{1,0:T(8,128)(2,1)S(1)} %collective-permute-done.9.b0), channel_id=1, source_target_pairs={{0,24},{8,16},{16,8},{24,0},{1,25},{9,17},{17,9},{25,1},{2,26},{10... | collective-permute-start | bytes 786440 | tf_op jit(solution)/shard_map/ppermute | solution.py:237
  42.2 11.9 %collective-permute-start.11 = (bf16[512,256]{1,0:T(8,128)(2,1)S(1)}, bf16[512,256]{1,0:T(8,128)(2,1)S(1)}, u32[]{:S(2)}, u32[]{:S(2)}) collective-permute-start(bf16[512,256]{1,0:T(8,128)(2,1)S(1)} %collective-permute-done.9.b0), channel_id=1, source_target_pairs={{0,16},{8,24},{16,0},{24,8},{1,17},{9,25},{17,1},{25,9},{2,18},{10... | collective-permute-start | bytes 786440 | tf_op jit(solution)/shard_map/ppermute | solution.py:237
  42.2 12.2 %collective-permute-start.10 = (bf16[512,256]{1,0:T(8,128)(2,1)S(1)}, bf16[512,256]{1,0:T(8,128)(2,1)S(1)}, u32[]{:S(2)}, u32[]{:S(2)}) collective-permute-start(bf16[512,256]{1,0:T(8,128)(2,1)S(1)} %collective-permute-done.9.b0), channel_id=1, source_target_pairs={{0,8},{8,0},{16,24},{24,16},{1,9},{9,1},{17,25},{25,17},{2,10},{10... | collective-permute-start | bytes 786440 | tf_op jit(solution)/shard_map/ppermute | solution.py:237
  57.9 54.3 %all-to-all-start.1 = ((f16[8,144,512]{2,1,0:T(8,128)(2,1)}), f16[8,144,512]{2,1,0:T(8,128)(2,1)S(1)}, u32[]{:S(2)}, u32[]{:S(2)}) async-start(f16[8,144,512]{2,1,0:T(8,128)(2,1)} %convert_element_type.29), calls=%async_computation.1 | async-start | bytes 2359296 | tf_op jit(solution)/shard_map/all_to_all | solution.py:270
  67.3 37.4 %collective-permute-start.6 = (f16[144,640]{1,0:T(8,128)(2,1)S(1)}, f16[144,640]{1,0:T(8,128)(2,1)S(1)}, u32[]{:S(2)}, u32[]{:S(2)}) collective-permute-start(f16[144,640]{1,0:T(8,128)(2,1)S(1)} %collective-permute-done.2), channel_id=1, source_target_pairs={{0,224},{32,0},{64,32},{96,64},{128,96},{160,128},{192,160},{224,1... | collective-permute-start | bytes 552968 | tf_op jit(solution)/shard_map/ppermute | solution.py:224
  67.3 36.7 %collective-permute-start.5 = (f16[144,640]{1,0:T(8,128)(2,1)}, f16[144,640]{1,0:T(8,128)(2,1)S(1)}, u32[]{:S(2)}, u32[]{:S(2)}) collective-permute-start(f16[144,640]{1,0:T(8,128)(2,1)} %collective-permute-done.1), channel_id=1, source_target_pairs={{0,64},{32,96},{64,128},{96,160},{128,192},{160,224},{192,0},{224,... | collective-permute-start | bytes 552968 | tf_op jit(solution)/shard_map/ppermute | solution.py:224
  69.7 33.6 %collective-permute-start.4 = (f16[144,640]{1,0:T(8,128)(2,1)}, f16[144,640]{1,0:T(8,128)(2,1)S(1)}, u32[]{:S(2)}, u32[]{:S(2)}) collective-permute-start(f16[144,640]{1,0:T(8,128)(2,1)} %collective-permute-done.1), channel_id=1, source_target_pairs={{0,32},{32,64},{64,96},{96,128},{128,160},{160,192},{192,224},{224... | collective-permute-start | bytes 552968 | tf_op jit(solution)/shard_map/ppermute | solution.py:224
  106.8 30.5 %collective-permute-start.7 = (f16[8,144,640]{2,1,0:T(8,128)(2,1)}, f16[8,144,640]{2,1,0:T(8,128)(2,1)}, u32[]{:S(2)}, u32[]{:S(2)}) collective-permute-start(f16[8,144,640]{2,1,0:T(8,128)(2,1)} %bitcast_dynamic-update-slice_fusion), channel_id=1, source_target_pairs={{0,0},{1,2},{2,1},{3,3},{4,4},{5,6},{6,5},{7,7},{8,8},{9,10},{10,9... | collective-permute-start | bytes 4423688 | tf_op jit(solution)/shard_map/ppermute | solution.py:260
  112.5 9.7 %collective-permute-start.13 = (bf16[128,512]{1,0:T(8,128)(2,1)S(1)}, bf16[128,512]{1,0:T(8,128)(2,1)S(1)}, u32[]{:S(2)}, u32[]{:S(2)}) collective-permute-start(bf16[128,512]{1,0:T(8,128)(2,1)S(1)} %multiply_reduce_fusion.mine), channel_id=1, source_target_pairs={{0,2},{2,0},{1,3},{3,1},{4,6},{6,4},{5,7},{7,5},{8,10},{10,8},{9,1... | collective-permute-start | bytes 393224 | tf_op jit(solution)/shard_map/ppermute | solution.py:220
  122.8 9.8 %collective-permute-start.15 = (bf16[2,128,512]{2,1,0:T(8,128)(2,1)S(1)}, bf16[2,128,512]{2,1,0:T(8,128)(2,1)S(1)}, u32[]{:S(2)}, u32[]{:S(2)}) collective-permute-start(bf16[2,128,512]{2,1,0:T(8,128)(2,1)S(1)} %merge.1.g0), channel_id=1, source_target_pairs={{0,64},{2,194},{32,96},{34,226},{64,128},{66,2},{96,160},{98,34},{... | collective-permute-start | bytes 786440 | tf_op jit(solution)/shard_map/ppermute | solution.py:282
  126.4 14.9 %collective-permute-start.14 = (bf16[2,128,512]{2,1,0:T(8,128)(2,1)S(1)}, bf16[2,128,512]{2,1,0:T(8,128)(2,1)S(1)}, u32[]{:S(2)}, u32[]{:S(2)}) collective-permute-start(bf16[2,128,512]{2,1,0:T(8,128)(2,1)S(1)} %merge.1.g0), channel_id=1, source_target_pairs={{0,32},{2,226},{32,64},{34,2},{64,96},{66,34},{96,128},{98,66},{12... | collective-permute-start | bytes 786440 | tf_op jit(solution)/shard_map/ppermute | solution.py:282
  132.6 14.5 %collective-permute-start.16 = (bf16[2,128,512]{2,1,0:T(8,128)(2,1)S(1)}, bf16[2,128,512]{2,1,0:T(8,128)(2,1)S(1)}, u32[]{:S(2)}, u32[]{:S(2)}) collective-permute-start(bf16[2,128,512]{2,1,0:T(8,128)(2,1)S(1)} %collective-permute-done.15.src.r2), channel_id=1, source_target_pairs={{0,32},{2,226},{32,64},{34,2},{64,96},{66,34},{96,128},{98,66},{12... | collective-permute-start | bytes 786440 | tf_op jit(solution)/shard_map/ppermute | solution.py:282
  133.8 8.0 %collective-permute-start.17 = (bf16[2,64,512]{2,1,0:T(8,128)(2,1)S(1)}, bf16[2,64,512]{2,1,0:T(8,128)(2,1)S(1)}, u32[]{:S(2)}, u32[]{:S(2)}) collective-permute-start(bf16[2,64,512]{2,1,0:T(8,128)(2,1)S(1)} %half.1), channel_id=1, source_target_pairs={{0,64},{2,194},{32,96},{34,226},{64,128},{66,2},{96,160},{98,34},{... | collective-permute-start | bytes 393224 | tf_op jit(solution)/shard_map/ppermute | solution.py:282
  138.2 11.7 %collective-permute-start.19 = (bf16[2,128,512]{2,1,0:T(8,128)(2,1)S(1)}, bf16[2,128,512]{2,1,0:T(8,128)(2,1)S(1)}, u32[]{:S(2)}, u32[]{:S(2)}) collective-permute-start(bf16[2,128,512]{2,1,0:T(8,128)(2,1)S(1)} %collective-permute-done.15.src.r2), channel_id=1, source_target_pairs={{0,2},{2,0},{1,3},{3,1},{4,6},{6,4},{5,7},{7,5},{8,10},{10,8},{9,1... | collective-permute-start | bytes 786440 | tf_op jit(solution)/shard_map/ppermute | solution.py:220
  141.3 8.6 %collective-permute-start.18 = (bf16[2,128,512]{2,1,0:T(8,128)(2,1)S(1)}, bf16[2,128,512]{2,1,0:T(8,128)(2,1)S(1)}, u32[]{:S(2)}, u32[]{:S(2)}) collective-permute-start(bf16[2,128,512]{2,1,0:T(8,128)(2,1)S(1)} %collective-permute-done.14.r1), channel_id=1, source_target_pairs={{0,2},{2,0},{1,3},{3,1},{4,6},{6,4},{5,7},{7,5},{8,10},{10,8},{9,1... | collective-permute-start | bytes 786440 | tf_op jit(solution)/shard_map/ppermute | solution.py:220
  141.9 8.0 %collective-permute-start.21 = (bf16[2,64,512]{2,1,0:T(8,128)(2,1)S(1)}, bf16[2,64,512]{2,1,0:T(8,128)(2,1)S(1)}, u32[]{:S(2)}, u32[]{:S(2)}) collective-permute-start(bf16[2,64,512]{2,1,0:T(8,128)(2,1)S(1)} %collective-permute-done.17.r4), channel_id=1, source_target_pairs={{0,2},{2,0},{1,3},{3,1},{4,6},{6,4},{5,7},{7,5},{8,10},{10,8},{9,1... | collective-permute-start | bytes 393224 | tf_op jit(solution)/shard_map/ppermute | solution.py:220
  167.5 13.5 %collective-permute-start.24 = (f32[128,1024]{1,0:T(8,128)S(1)}, f32[128,1024]{1,0:T(8,128)S(1)}, u32[]{:S(2)}, u32[]{:S(2)}) collective-permute-start(f32[128,1024]{1,0:T(8,128)S(1)} %get-tuple-element.19), channel_id=1, source_target_pairs={{0,0},{1,2},{2,1},{3,3},{4,4},{5,6},{6,5},{7,7},{8,8},{9,10},{10,9... | collective-permute-start | bytes 1572872 | tf_op jit(solution)/shard_map/ppermute | solution.py:305
  178.0 7.8 %collective-permute-start.23 = (bf16[64,1024]{1,0:T(8,128)(2,1)S(1)}, bf16[64,1024]{1,0:T(8,128)(2,1)S(1)}, u32[]{:S(2)}, u32[]{:S(2)}) collective-permute-start(bf16[64,1024]{1,0:T(8,128)(2,1)S(1)} %update_rows.1), channel_id=1, source_target_pairs={{0,0},{1,2},{2,1},{3,3},{4,4},{5,6},{6,5},{7,7},{8,8},{9,10},{10,9... | collective-permute-start | bytes 393224 | tf_op jit(solution)/shard_map/ppermute | solution.py:315
  (3 other events, 29.3 us)

commit v3 on v2

--- a/solution.py
+++ b/solution.py
@@ -31,8 +31,8 @@
     return jnp.concatenate([ref[k] for k in range(ref.shape[0])], axis=1)
 
 
-def loop(n, body):
-    lax.fori_loop(0, n, lambda j, c: (body(j), c)[1], 0)
+def loop(n, body, unroll=1):
+    lax.fori_loop(0, n, lambda j, c: (body(j), c)[1], 0, unroll=unroll)
 
 
 def diagonal(n):
@@ -60,7 +60,7 @@
         r = pl.multiple_of(128 * k, 128)
         for cb in range(2):
             out[k, :128, 256 * cb:256 * (cb + 1)] = acc_s[cb, pl.ds(r, 128), :] * up
-        out[k, 128:, :] = jnp.broadcast_to(power, (16, 512))
+        out[k, 128:, :] = jnp.broadcast_to(power, (8, 512))
 
     loop(Z, body)
 
@@ -159,7 +159,7 @@
         def body(j):
             dst[j] = dot(cat(a), b[j]).astype(BF16)
 
-        loop(4, body)
+        loop(4, body, 2)
 
     mul(t0, f0, f0)
     mul(f1, t0, t0)
@@ -204,12 +204,12 @@
 def pack(x, peak):
     power = jnp.floor(jnp.log2(jnp.maximum(peak, 1e-30)))
     scaled = (x * jnp.exp2(14.0 - power)).astype(F16)
-    label = jnp.broadcast_to(power, (*x.shape[:-2], 16, x.shape[-1])).astype(F16)
+    label = jnp.broadcast_to(power, (*x.shape[:-2], 8, x.shape[-1])).astype(F16)
     return jnp.concatenate([scaled, label], axis=-2)
 
 
 def unpack(x):
-    return x[..., :-16, :].astype(F32) * jnp.exp2(x[..., -16:-15, :].astype(F32) - 14.0)
+    return x[..., :-8, :].astype(F32) * jnp.exp2(x[..., -8:-7, :].astype(F32) - 14.0)
 
 
 def everyone(x, axis, n):
@@ -241,12 +241,15 @@
     wide = jnp.concatenate([stat, stat[:, :512]], axis=1)
     part = lax.dynamic_slice(wide, (0, z * 128), (128, 640))
     part = pack(part, jnp.max(jnp.abs(stat)))
-    up2, down2 = along(part, 2), along(part, -2)
-    up1, down1 = along(part, 1), along(part, -1)
+    up, down = [part], [part]
+    for k in range(1, 5):
+        up.append(along(up[-1], 1))
+        if k < 4:
+            down.append(along(down[-1], -1))
 
     partial = pl.pallas_call(
         partial_kernel,
-        out_shape=sds((Z, 144, 512), F32),
+        out_shape=sds((Z, 136, 512), F32),
         in_specs=[SMEM] + [VMEM] * 6,
         out_specs=VMEM,
         scratch_shapes=[pltpu.VMEM((2, 1024, 256), F32), pltpu.VMEM((1, 256), F32)],
@@ -254,9 +257,8 @@
         name="partial_gradient",
     )(idx1, a_own, a_oth, *cot)
 
-    near = lax.optimization_barrier((partial[0, 128:136, :128], part, up1, up2, down2, down1))[1:]
-    far = [along(up2, 1), along(up2, 2), along(down2, -1)]
-    st = jnp.stack([*near[:3], *far, *near[3:]])
+    near = lax.optimization_barrier((partial[0, 128:136, :128], *up[:4], *down[1:]))[1:]
+    st = jnp.stack([*near[:4], up[4], *near[:3:-1]])
     st = lax.ppermute(st, ("co", "pair"), SWAP)
     st = pl.pallas_call(
         assemble_kernel,

time: 188 us -> 187 us (level)
  starting transfers between devices: 70.6 us -> 68.4 us
    ppermute x1, starting transfers between devices: 5.4 us -> 2.16 us  [step(): st = lax.ppermute(st, ('co', 'pair'), SWAP)]
    ppermute x7, starting transfers between devices: 19 us -> 22.2 us  [sibling(): return lax.ppermute(x, 'co', [(0, 1), (1, 0)])]
    ppermute x7, starting transfers between devices: 12.3 us -> 9.25 us  [along(): return lax.ppermute(x, 'tok', [(i, (i + d) % Z) for i in range(Z)])]
    unnamed x12 -> x16, local copies, waits for them, and re-layouts: 7.47 us -> 8.32 us
  transfers between devices with their start and end apart: 26 -> 26, of which waited for: 10 -> 11; matrix products, arithmetic and copies ran while one was open for 6% -> 7% of each run, Pallas kernels for 5% -> 5%
where the time goes in v3:
time: 187 us; the launch traced here: 185 us
  starting transfers between devices  68.4 us (37%)
  waiting for transfers between devices  54.5 us (29%)
  Pallas kernels  27.2 us (15%)
  blocking collectives  17.8 us (10%)
  local copies, waits for them, and re-layouts  10.2 us (5%)
  other arithmetic  5.83 us (3%)
    ppermute x7, waiting for transfers between devices, along(): return lax.ppermute(x, 'tok', [(i, (i + d) % Z) for i in range(Z)])  31.1 us
    ppermute x7, starting transfers between devices, sibling(): return lax.ppermute(x, 'co', [(0, 1), (1, 0)])  22.2 us
    all_to_all x1, blocking collectives, everyone(): lax.all_to_all(jnp.broadcast_to(x, (n, *x.shape)), axis, 0, 0, tiled=True)  17.8 us
    pallas_call x1, Pallas kernels, step(): pl.pallas_call(chain_kernel, out_shape=(sds((4, 1024, 256), BF16), sds((4...  16.4 us
    ppermute x3, starting transfers between devices, step(): cot.append(lax.ppermute(cot[0], 'y', [(i, i ^ d) for i in range(4)]))  12.5 us
    ppermute x3, waiting for transfers between devices, step(): cot.append(lax.ppermute(cot[0], 'y', [(i, i ^ d) for i in range(4)]))  10.7 us
    ppermute x7, starting transfers between devices, along(): return lax.ppermute(x, 'tok', [(i, (i + d) % Z) for i in range(Z)])  9.25 us
    ppermute x4, starting transfers between devices, pass_on(): return lax.ppermute(x, ('tok', 'co'), perm)  8.91 us
  transfers between devices with their start and end apart: 26, of which 11 were waited for; matrix products, arithmetic and copies ran while one was open for 7% of the time, Pallas kernels for 5%

profile of v3, /device:TPU:33, one launch (start us, length us, event | category | flops | bytes accessed | tf_op | source)
XLA Modules:
  0.0 185.5 jit_solution(17323935082927736431)
XLA Ops:
  1.7 17.8 %all_to_all.10.a_own = bf16[4,512,256]{2,1,0:T(8,128)(2,1)S(1)} all-to-all(bf16[4,512,256]{2,1,0:T(8,128)(2,1)S(1)} %broadcast_in_dim.10), channel_id=1, replica_groups=mesh['tok'=8,'y'=4,'xl'=2,'co'=2,'pair'=2] {'xl','pair'}, dimensions={0} | all-to-all | bytes 2097152 | tf_op jit(solution)/shard_map/all_to_all | solution.py:216
  19.5 1.8 collective-permute-start.8
  24.6 4.6 %collective-permute-done.3 = f16[136,640]{1,0:T(8,128)(2,1)S(1)} collective-permute-done((f16[136,640]{1,0:T(8,128)(2,1)S(1)}, f16[136,640]{1,0:T(8,128)(2,1)S(1)}, u32[]{:S(2)}, u32[]{:S(2)}) %collective-permute-start.3) | collective-permute-done | bytes 174112 | tf_op jit(solution)/shard_map/ppermute | solution.py:224
  29.2 2.9 %collective-permute-start.4 = (f16[136,640]{1,0:T(8,128)(2,1)S(1)}, f16[136,640]{1,0:T(8,128)(2,1)S(1)}, u32[]{:S(2)}, u32[]{:S(2)}) collective-permute-start(f16[136,640]{1,0:T(8,128)(2,1)S(1)} %collective-permute-done.3), channel_id=1, source_target_pairs={{0,224},{32,0},{64,32},{96,64},{128,96},{160,128},{192,160},{224,1... | collective-permute-start | bytes 522248 | tf_op jit(solution)/shard_map/ppermute | solution.py:224
  35.0 3.4 %collective-permute-start.5 = (f16[136,640]{1,0:T(8,128)(2,1)S(1)}, f16[136,640]{1,0:T(8,128)(2,1)}, u32[]{:S(2)}, u32[]{:S(2)}) collective-permute-start(f16[136,640]{1,0:T(8,128)(2,1)S(1)} %collective-permute-done.4), channel_id=1, source_target_pairs={{0,224},{32,0},{64,32},{96,64},{128,96},{160,128},{192,160},{224,1... | collective-permute-start | bytes 522248 | tf_op jit(solution)/shard_map/ppermute | solution.py:224
  38.4 2.4 %collective-permute-done.1 = f16[136,640]{1,0:T(8,128)(2,1)} collective-permute-done((f16[136,640]{1,0:T(8,128)(2,1)S(1)}, f16[136,640]{1,0:T(8,128)(2,1)}, u32[]{:S(2)}, u32[]{:S(2)}) %collective-permute-start.1) | collective-permute-done | bytes 174112 | tf_op jit(solution)/shard_map/ppermute | solution.py:224
  40.9 12.0 %collective-permute-start.12 = (bf16[512,256]{1,0:T(8,128)(2,1)S(1)}, bf16[512,256]{1,0:T(8,128)(2,1)S(1)}, u32[]{:S(2)}, u32[]{:S(2)}) collective-permute-start(bf16[512,256]{1,0:T(8,128)(2,1)S(1)} %collective-permute-done.9.b0), channel_id=1, source_target_pairs={{0,24},{8,16},{16,8},{24,0},{1,25},{9,17},{17,9},{25,1},{2,26},{10... | collective-permute-start | bytes 786440 | tf_op jit(solution)/shard_map/ppermute | solution.py:237
  54.2 10.3 %collective-permute-done.12.b3 = bf16[512,256]{1,0:T(8,128)(2,1)S(1)} collective-permute-done((bf16[512,256]{1,0:T(8,128)(2,1)S(1)}, bf16[512,256]{1,0:T(8,128)(2,1)S(1)}, u32[]{:S(2)}, u32[]{:S(2)}) %collective-permute-start.12) | collective-permute-done | bytes 262176 | tf_op jit(solution)/shard_map/ppermute | solution.py:237
  64.9 2.1 %partial_gradient.1 = f32[8,136,512]{2,1,0:T(8,128)S(1)} custom-call(s32[3]{0:T(128)S(1)} %pad_add_fusion.1.idx, bf16[4,512,256]{2,1,0:T(8,128)(2,1)S(1)} %all_to_all.10.a_own, bf16[4,512,256]{2,1,0:T(8,128)(2,1)S(1)} %collective-permute-done.8.a_oth, bf16[512,256]{1,0:T(8,128)(2,1)S(1)} %collective-permute-done.9.b0, ...), custom_call_target="tpu_custom_call" | custom-call | tf_op jit(solution)/shard_map/partial_gradient/pallas_call | solution.py:250
  68.3 7.0 %all-to-all-start.1 = ((f16[8,136,512]{2,1,0:T(8,128)(2,1)}), f16[8,136,512]{2,1,0:T(8,128)(2,1)S(1)}, u32[]{:S(2)}, u32[]{:S(2)}) async-start(f16[8,136,512]{2,1,0:T(8,128)(2,1)} %convert_element_type.29), calls=%async_computation.1 | async-start | bytes 2228224 | tf_op jit(solution)/shard_map/all_to_all | solution.py:272
  80.5 22.7 %collective-permute-done.6 = f16[136,640]{1,0:T(8,128)(2,1)S(1)} collective-permute-done((f16[136,640]{1,0:T(8,128)(2,1)}, f16[136,640]{1,0:T(8,128)(2,1)S(1)}, u32[]{:S(2)}, u32[]{:S(2)}) %collective-permute-start.6) | collective-permute-done | bytes 174112 | tf_op jit(solution)/shard_map/ppermute | solution.py:224
  106.9 2.2 %collective-permute-start.7 = (f16[8,136,640]{2,1,0:T(8,128)(2,1)}, f16[8,136,640]{2,1,0:T(8,128)(2,1)}, u32[]{:S(2)}, u32[]{:S(2)}) collective-permute-start(f16[8,136,640]{2,1,0:T(8,128)(2,1)} %bitcast_dynamic-update-slice_fusion), channel_id=1, source_target_pairs={{0,0},{1,2},{2,1},{3,3},{4,4},{5,6},{6,5},{7,7},{8,8},{9,10},{10,9... | collective-permute-start | bytes 4177928 | tf_op jit(solution)/shard_map/ppermute | solution.py:262
  109.4 11.8 %collective-permute-start.13 = (bf16[128,512]{1,0:T(8,128)(2,1)S(1)}, bf16[128,512]{1,0:T(8,128)(2,1)S(1)}, u32[]{:S(2)}, u32[]{:S(2)}) collective-permute-start(bf16[128,512]{1,0:T(8,128)(2,1)S(1)} %multiply_reduce_fusion.mine), channel_id=1, source_target_pairs={{0,2},{2,0},{1,3},{3,1},{4,6},{6,4},{5,7},{7,5},{8,10},{10,8},{9,1... | collective-permute-start | bytes 393224 | tf_op jit(solution)/shard_map/ppermute | solution.py:220
  122.8 3.7 %collective-permute-start.15 = (bf16[2,128,512]{2,1,0:T(8,128)(2,1)S(1)}, bf16[2,128,512]{2,1,0:T(8,128)(2,1)S(1)}, u32[]{:S(2)}, u32[]{:S(2)}) collective-permute-start(bf16[2,128,512]{2,1,0:T(8,128)(2,1)S(1)} %merge.1.g0), channel_id=1, source_target_pairs={{0,64},{2,194},{32,96},{34,226},{64,128},{66,2},{96,160},{98,34},{... | collective-permute-start | bytes 786440 | tf_op jit(solution)/shard_map/ppermute | solution.py:284
  127.5 5.1 %collective-permute-done.15.src.r2 = bf16[2,128,512]{2,1,0:T(8,128)(2,1)S(1)} collective-permute-done((bf16[2,128,512]{2,1,0:T(8,128)(2,1)S(1)}, bf16[2,128,512]{2,1,0:T(8,128)(2,1)S(1)}, u32[]{:S(2)}, u32[]{:S(2)}) %collective-permute-start.15) | collective-permute-done | bytes 262176 | tf_op jit(solution)/shard_map/ppermute | solution.py:284
  133.9 3.5 %collective-permute-start.17 = (bf16[2,64,512]{2,1,0:T(8,128)(2,1)S(1)}, bf16[2,64,512]{2,1,0:T(8,128)(2,1)S(1)}, u32[]{:S(2)}, u32[]{:S(2)}) collective-permute-start(bf16[2,64,512]{2,1,0:T(8,128)(2,1)S(1)} %half.1), channel_id=1, source_target_pairs={{0,64},{2,194},{32,96},{34,226},{64,128},{66,2},{96,160},{98,34},{... | collective-permute-start | bytes 393224 | tf_op jit(solution)/shard_map/ppermute | solution.py:284
  138.3 3.1 %collective-permute-start.19 = (bf16[2,128,512]{2,1,0:T(8,128)(2,1)S(1)}, bf16[2,128,512]{2,1,0:T(8,128)(2,1)S(1)}, u32[]{:S(2)}, u32[]{:S(2)}) collective-permute-start(bf16[2,128,512]{2,1,0:T(8,128)(2,1)S(1)} %collective-permute-done.15.src.r2), channel_id=1, source_target_pairs={{0,2},{2,0},{1,3},{3,1},{4,6},{6,4},{5,7},{7,5},{8,10},{10,8},{9,1... | collective-permute-start | bytes 786440 | tf_op jit(solution)/shard_map/ppermute | solution.py:220
  141.9 5.3 %collective-permute-start.21 = (bf16[2,64,512]{2,1,0:T(8,128)(2,1)S(1)}, bf16[2,64,512]{2,1,0:T(8,128)(2,1)S(1)}, u32[]{:S(2)}, u32[]{:S(2)}) collective-permute-start(bf16[2,64,512]{2,1,0:T(8,128)(2,1)S(1)} %collective-permute-done.17.r4), channel_id=1, source_target_pairs={{0,2},{2,0},{1,3},{3,1},{4,6},{6,4},{5,7},{7,5},{8,10},{10,8},{9,1... | collective-permute-start | bytes 393224 | tf_op jit(solution)/shard_map/ppermute | solution.py:220
  149.9 16.4 %inverse_root.1 = (bf16[4,1024,256]{2,1,0:T(8,128)(2,1)S(1)}, bf16[4,1024,256]{2,1,0:T(8,128)(2,1)S(1)}, f32[128,1024]{1,0:T(8,128)S(1)}, f32[8,128]{1,0:T(8,128)S(1)}) custom-call(s32[2]{0:T(128)S(1)} %pad_add_fusion.idx, f32[8,1024,128]{2,1,0:T(8,128)S(1)} %assemble.1.st, bf16[2,128,512]{2,1,0:T(8,128)(2,1)S(1)} %merge.1.g0, ...), custom_call_target="tpu_custom_call" | custom-call | tf_op jit(solution)/shard_map/inverse_root/pallas_call | solution.py:295
  166.4 1.9 %collective-permute-start.24 = (f32[128,1024]{1,0:T(8,128)S(1)}, f32[128,1024]{1,0:T(8,128)S(1)}, u32[]{:S(2)}, u32[]{:S(2)}) collective-permute-start(f32[128,1024]{1,0:T(8,128)S(1)} %get-tuple-element.23), channel_id=1, source_target_pairs={{0,0},{1,2},{2,1},{3,3},{4,4},{5,6},{6,5},{7,7},{8,8},{9,10},{10,9... | collective-permute-start | bytes 1572872 | tf_op jit(solution)/shard_map/ppermute | solution.py:307
  168.3 2.2 %collective-permute-done.22.other = bf16[4,1024,256]{2,1,0:T(8,128)(2,1)S(1)} collective-permute-done((bf16[4,1024,256]{2,1,0:T(8,128)(2,1)S(1)}, bf16[4,1024,256]{2,1,0:T(8,128)(2,1)S(1)}, u32[]{:S(2)}, u32[]{:S(2)}) %collective-permute-start.22) | collective-permute-done | bytes 2097184 | tf_op jit(solution)/shard_map/ppermute | solution.py:220
  170.6 6.4 %update_rows.1 = bf16[64,1024]{1,0:T(8,128)(2,1)S(1)} custom-call(s32[2]{0:T(128)S(1)} %pad_add_fusion.idx, bf16[4,1024,256]{2,1,0:T(8,128)(2,1)S(1)} %get-tuple-element.20.own, bf16[4,1024,256]{2,1,0:T(8,128)(2,1)S(1)} %collective-permute-done.22.other, bf16[4,1024,256]{2,1,0:T(8,128)(2,1)S(1)} %get-tuple-element.21.grad, ...), custom_call_target="tpu_custom_call" | custom-call | tf_op jit(solution)/shard_map/update_rows/pallas_call | solution.py:308
  177.0 2.9 %collective-permute-start.23 = (bf16[64,1024]{1,0:T(8,128)(2,1)S(1)}, bf16[64,1024]{1,0:T(8,128)(2,1)S(1)}, u32[]{:S(2)}, u32[]{:S(2)}) collective-permute-start(bf16[64,1024]{1,0:T(8,128)(2,1)S(1)} %update_rows.1), channel_id=1, source_target_pairs={{0,0},{1,2},{2,1},{3,3},{4,4},{5,6},{6,5},{7,7},{8,8},{9,10},{10,9... | collective-permute-start | bytes 393224 | tf_op jit(solution)/shard_map/ppermute | solution.py:317
  180.8 4.0 %collective-permute-done.23 = bf16[64,1024]{1,0:T(8,128)(2,1)S(1)} collective-permute-done((bf16[64,1024]{1,0:T(8,128)(2,1)S(1)}, bf16[64,1024]{1,0:T(8,128)(2,1)S(1)}, u32[]{:S(2)}, u32[]{:S(2)}) %collective-permute-start.23) | collective-permute-done | bytes 131104 | tf_op jit(solution)/shard_map/ppermute | solution.py:317
  (65 shorter events, 28.5 us)
Async XLA Ops:
  19.5 45.4 %collective-permute-start.8 = (bf16[4,512,256]{2,1,0:T(8,128)(2,1)S(1)}, bf16[4,512,256]{2,1,0:T(8,128)(2,1)S(1)}, u32[]{:S(2)}, u32[]{:S(2)}) collective-permute-start(bf16[4,512,256]{2,1,0:T(8,128)(2,1)S(1)} %all_to_all.10.a_own), channel_id=1, source_target_pairs={{0,2},{2,0},{1,3},{3,1},{4,6},{6,4},{5,7},{7,5},{8,10},{10,8},{9,1... | collective-permute-start | bytes 3145736 | tf_op jit(solution)/shard_map/ppermute | solution.py:220
  22.8 6.4 %collective-permute-start.3 = (f16[136,640]{1,0:T(8,128)(2,1)S(1)}, f16[136,640]{1,0:T(8,128)(2,1)S(1)}, u32[]{:S(2)}, u32[]{:S(2)}) collective-permute-start(f16[136,640]{1,0:T(8,128)(2,1)S(1)} %concatenate.7), channel_id=1, source_target_pairs={{0,224},{32,0},{64,32},{96,64},{128,96},{160,128},{192,160},{224,1... | collective-permute-start | bytes 522248 | tf_op jit(solution)/shard_map/ppermute | solution.py:224
  22.9 10.8 %collective-permute-start = (f16[136,640]{1,0:T(8,128)(2,1)S(1)}, f16[136,640]{1,0:T(8,128)(2,1)S(1)}, u32[]{:S(2)}, u32[]{:S(2)}) collective-permute-start(f16[136,640]{1,0:T(8,128)(2,1)S(1)} %concatenate.7), channel_id=1, source_target_pairs={{0,32},{32,64},{64,96},{96,128},{128,160},{160,192},{192,224},{224... | collective-permute-start | bytes 522248 | tf_op jit(solution)/shard_map/ppermute | solution.py:224
  29.2 5.8 %collective-permute-start.4 = (f16[136,640]{1,0:T(8,128)(2,1)S(1)}, f16[136,640]{1,0:T(8,128)(2,1)S(1)}, u32[]{:S(2)}, u32[]{:S(2)}) collective-permute-start(f16[136,640]{1,0:T(8,128)(2,1)S(1)} %collective-permute-done.3), channel_id=1, source_target_pairs={{0,224},{32,0},{64,32},{96,64},{128,96},{160,128},{192,160},{224,1... | collective-permute-start | bytes 522248 | tf_op jit(solution)/shard_map/ppermute | solution.py:224
  32.1 8.8 %collective-permute-start.9 = (bf16[512,256]{1,0:T(8,128)(2,1)}, bf16[512,256]{1,0:T(8,128)(2,1)S(1)}, u32[]{:S(2)}, u32[]{:S(2)}) collective-permute-start(bf16[512,256]{1,0:T(8,128)(2,1)} %param.4), channel_id=1, source_target_pairs={{0,0},{1,8},{4,16},{5,24},{8,1},{9,9},{12,17},{13,25},{16,4},{17,1... | collective-permute-start | bytes 786440 | tf_op jit(solution)/shard_map/ppermute | solution.py:234
  33.7 7.2 %collective-permute-start.1 = (f16[136,640]{1,0:T(8,128)(2,1)S(1)}, f16[136,640]{1,0:T(8,128)(2,1)}, u32[]{:S(2)}, u32[]{:S(2)}) collective-permute-start(f16[136,640]{1,0:T(8,128)(2,1)S(1)} %collective-permute-done), channel_id=1, source_target_pairs={{0,32},{32,64},{64,96},{96,128},{128,160},{160,192},{192,224},{224... | collective-permute-start | bytes 522248 | tf_op jit(solution)/shard_map/ppermute | solution.py:224
  35.0 17.8 %collective-permute-start.5 = (f16[136,640]{1,0:T(8,128)(2,1)S(1)}, f16[136,640]{1,0:T(8,128)(2,1)}, u32[]{:S(2)}, u32[]{:S(2)}) collective-permute-start(f16[136,640]{1,0:T(8,128)(2,1)S(1)} %collective-permute-done.4), channel_id=1, source_target_pairs={{0,224},{32,0},{64,32},{96,64},{128,96},{160,128},{192,160},{224,1... | collective-permute-start | bytes 522248 | tf_op jit(solution)/shard_map/ppermute | solution.py:224
  40.9 12.6 %collective-permute-start.2 = (f16[136,640]{1,0:T(8,128)(2,1)}, f16[136,640]{1,0:T(8,128)(2,1)}, u32[]{:S(2)}, u32[]{:S(2)}) collective-permute-start(f16[136,640]{1,0:T(8,128)(2,1)} %collective-permute-done.1), channel_id=1, source_target_pairs={{0,32},{32,64},{64,96},{96,128},{128,160},{160,192},{192,224},{224... | collective-permute-start | bytes 522248 | tf_op jit(solution)/shard_map/ppermute | solution.py:224
  40.9 23.7 %collective-permute-start.12 = (bf16[512,256]{1,0:T(8,128)(2,1)S(1)}, bf16[512,256]{1,0:T(8,128)(2,1)S(1)}, u32[]{:S(2)}, u32[]{:S(2)}) collective-permute-start(bf16[512,256]{1,0:T(8,128)(2,1)S(1)} %collective-permute-done.9.b0), channel_id=1, source_target_pairs={{0,24},{8,16},{16,8},{24,0},{1,25},{9,17},{17,9},{25,1},{2,26},{10... | collective-permute-start | bytes 786440 | tf_op jit(solution)/shard_map/ppermute | solution.py:237
  52.8 11.7 %collective-permute-start.11 = (bf16[512,256]{1,0:T(8,128)(2,1)S(1)}, bf16[512,256]{1,0:T(8,128)(2,1)S(1)}, u32[]{:S(2)}, u32[]{:S(2)}) collective-permute-start(bf16[512,256]{1,0:T(8,128)(2,1)S(1)} %collective-permute-done.9.b0), channel_id=1, source_target_pairs={{0,16},{8,24},{16,0},{24,8},{1,17},{9,25},{17,1},{25,9},{2,18},{10... | collective-permute-start | bytes 786440 | tf_op jit(solution)/shard_map/ppermute | solution.py:237
  52.8 12.1 %collective-permute-start.10 = (bf16[512,256]{1,0:T(8,128)(2,1)S(1)}, bf16[512,256]{1,0:T(8,128)(2,1)S(1)}, u32[]{:S(2)}, u32[]{:S(2)}) collective-permute-start(bf16[512,256]{1,0:T(8,128)(2,1)S(1)} %collective-permute-done.9.b0), channel_id=1, source_target_pairs={{0,8},{8,0},{16,24},{24,16},{1,9},{9,1},{17,25},{25,17},{2,10},{10... | collective-permute-start | bytes 786440 | tf_op jit(solution)/shard_map/ppermute | solution.py:237
  68.3 40.8 %all-to-all-start.1 = ((f16[8,136,512]{2,1,0:T(8,128)(2,1)}), f16[8,136,512]{2,1,0:T(8,128)(2,1)S(1)}, u32[]{:S(2)}, u32[]{:S(2)}) async-start(f16[8,136,512]{2,1,0:T(8,128)(2,1)} %convert_element_type.29), calls=%async_computation.1 | async-start | bytes 2228224 | tf_op jit(solution)/shard_map/all_to_all | solution.py:272
  76.1 27.2 %collective-permute-start.6 = (f16[136,640]{1,0:T(8,128)(2,1)}, f16[136,640]{1,0:T(8,128)(2,1)S(1)}, u32[]{:S(2)}, u32[]{:S(2)}) collective-permute-start(f16[136,640]{1,0:T(8,128)(2,1)} %collective-permute-done.2), channel_id=1, source_target_pairs={{0,32},{32,64},{64,96},{96,128},{128,160},{160,192},{192,224},{224... | collective-permute-start | bytes 522248 | tf_op jit(solution)/shard_map/ppermute | solution.py:224
  106.9 30.4 %collective-permute-start.7 = (f16[8,136,640]{2,1,0:T(8,128)(2,1)}, f16[8,136,640]{2,1,0:T(8,128)(2,1)}, u32[]{:S(2)}, u32[]{:S(2)}) collective-permute-start(f16[8,136,640]{2,1,0:T(8,128)(2,1)} %bitcast_dynamic-update-slice_fusion), channel_id=1, source_target_pairs={{0,0},{1,2},{2,1},{3,3},{4,4},{5,6},{6,5},{7,7},{8,8},{9,10},{10,9... | collective-permute-start | bytes 4177928 | tf_op jit(solution)/shard_map/ppermute | solution.py:262
  109.4 12.8 %collective-permute-start.13 = (bf16[128,512]{1,0:T(8,128)(2,1)S(1)}, bf16[128,512]{1,0:T(8,128)(2,1)S(1)}, u32[]{:S(2)}, u32[]{:S(2)}) collective-permute-start(bf16[128,512]{1,0:T(8,128)(2,1)S(1)} %multiply_reduce_fusion.mine), channel_id=1, source_target_pairs={{0,2},{2,0},{1,3},{3,1},{4,6},{6,4},{5,7},{7,5},{8,10},{10,8},{9,1... | collective-permute-start | bytes 393224 | tf_op jit(solution)/shard_map/ppermute | solution.py:220
  122.8 9.8 %collective-permute-start.15 = (bf16[2,128,512]{2,1,0:T(8,128)(2,1)S(1)}, bf16[2,128,512]{2,1,0:T(8,128)(2,1)S(1)}, u32[]{:S(2)}, u32[]{:S(2)}) collective-permute-start(bf16[2,128,512]{2,1,0:T(8,128)(2,1)S(1)} %merge.1.g0), channel_id=1, source_target_pairs={{0,64},{2,194},{32,96},{34,226},{64,128},{66,2},{96,160},{98,34},{... | collective-permute-start | bytes 786440 | tf_op jit(solution)/shard_map/ppermute | solution.py:284
  126.4 14.9 %collective-permute-start.14 = (bf16[2,128,512]{2,1,0:T(8,128)(2,1)S(1)}, bf16[2,128,512]{2,1,0:T(8,128)(2,1)S(1)}, u32[]{:S(2)}, u32[]{:S(2)}) collective-permute-start(bf16[2,128,512]{2,1,0:T(8,128)(2,1)S(1)} %merge.1.g0), channel_id=1, source_target_pairs={{0,32},{2,226},{32,64},{34,2},{64,96},{66,34},{96,128},{98,66},{12... | collective-permute-start | bytes 786440 | tf_op jit(solution)/shard_map/ppermute | solution.py:284
  132.6 14.5 %collective-permute-start.16 = (bf16[2,128,512]{2,1,0:T(8,128)(2,1)S(1)}, bf16[2,128,512]{2,1,0:T(8,128)(2,1)S(1)}, u32[]{:S(2)}, u32[]{:S(2)}) collective-permute-start(bf16[2,128,512]{2,1,0:T(8,128)(2,1)S(1)} %collective-permute-done.15.src.r2), channel_id=1, source_target_pairs={{0,32},{2,226},{32,64},{34,2},{64,96},{66,34},{96,128},{98,66},{12... | collective-permute-start | bytes 786440 | tf_op jit(solution)/shard_map/ppermute | solution.py:284
  133.9 8.0 %collective-permute-start.17 = (bf16[2,64,512]{2,1,0:T(8,128)(2,1)S(1)}, bf16[2,64,512]{2,1,0:T(8,128)(2,1)S(1)}, u32[]{:S(2)}, u32[]{:S(2)}) collective-permute-start(bf16[2,64,512]{2,1,0:T(8,128)(2,1)S(1)} %half.1), channel_id=1, source_target_pairs={{0,64},{2,194},{32,96},{34,226},{64,128},{66,2},{96,160},{98,34},{... | collective-permute-start | bytes 393224 | tf_op jit(solution)/shard_map/ppermute | solution.py:284
  138.3 11.7 %collective-permute-start.19 = (bf16[2,128,512]{2,1,0:T(8,128)(2,1)S(1)}, bf16[2,128,512]{2,1,0:T(8,128)(2,1)S(1)}, u32[]{:S(2)}, u32[]{:S(2)}) collective-permute-start(bf16[2,128,512]{2,1,0:T(8,128)(2,1)S(1)} %collective-permute-done.15.src.r2), channel_id=1, source_target_pairs={{0,2},{2,0},{1,3},{3,1},{4,6},{6,4},{5,7},{7,5},{8,10},{10,8},{9,1... | collective-permute-start | bytes 786440 | tf_op jit(solution)/shard_map/ppermute | solution.py:220
  141.3 8.6 %collective-permute-start.18 = (bf16[2,128,512]{2,1,0:T(8,128)(2,1)S(1)}, bf16[2,128,512]{2,1,0:T(8,128)(2,1)S(1)}, u32[]{:S(2)}, u32[]{:S(2)}) collective-permute-start(bf16[2,128,512]{2,1,0:T(8,128)(2,1)S(1)} %collective-permute-done.14.r1), channel_id=1, source_target_pairs={{0,2},{2,0},{1,3},{3,1},{4,6},{6,4},{5,7},{7,5},{8,10},{10,8},{9,1... | collective-permute-start | bytes 786440 | tf_op jit(solution)/shard_map/ppermute | solution.py:220
  141.9 8.0 %collective-permute-start.21 = (bf16[2,64,512]{2,1,0:T(8,128)(2,1)S(1)}, bf16[2,64,512]{2,1,0:T(8,128)(2,1)S(1)}, u32[]{:S(2)}, u32[]{:S(2)}) collective-permute-start(bf16[2,64,512]{2,1,0:T(8,128)(2,1)S(1)} %collective-permute-done.17.r4), channel_id=1, source_target_pairs={{0,2},{2,0},{1,3},{3,1},{4,6},{6,4},{5,7},{7,5},{8,10},{10,8},{9,1... | collective-permute-start | bytes 393224 | tf_op jit(solution)/shard_map/ppermute | solution.py:220
  166.4 13.5 %collective-permute-start.24 = (f32[128,1024]{1,0:T(8,128)S(1)}, f32[128,1024]{1,0:T(8,128)S(1)}, u32[]{:S(2)}, u32[]{:S(2)}) collective-permute-start(f32[128,1024]{1,0:T(8,128)S(1)} %get-tuple-element.23), channel_id=1, source_target_pairs={{0,0},{1,2},{2,1},{3,3},{4,4},{5,6},{6,5},{7,7},{8,8},{9,10},{10,9... | collective-permute-start | bytes 1572872 | tf_op jit(solution)/shard_map/ppermute | solution.py:307
  177.0 7.8 %collective-permute-start.23 = (bf16[64,1024]{1,0:T(8,128)(2,1)S(1)}, bf16[64,1024]{1,0:T(8,128)(2,1)S(1)}, u32[]{:S(2)}, u32[]{:S(2)}) collective-permute-start(bf16[64,1024]{1,0:T(8,128)(2,1)S(1)} %update_rows.1), channel_id=1, source_target_pairs={{0,0},{1,2},{2,1},{3,3},{4,4},{5,6},{6,5},{7,7},{8,8},{9,10},{10,9... | collective-permute-start | bytes 393224 | tf_op jit(solution)/shard_map/ppermute | solution.py:317
  (5 other events, 36.0 us)

commit v4 on v3

--- a/solution.py
+++ b/solution.py
@@ -132,7 +132,7 @@
         v = grad[j].astype(F32)
         return top, acc + jnp.sum(v * v, axis=0, keepdims=True)
 
-    top, acc = lax.fori_loop(0, 4, product, (jnp.zeros((1, 128), F32), jnp.zeros((1, 256), F32)))
+    top, acc = lax.fori_loop(0, 4, product, (jnp.zeros((1, 128), F32), jnp.zeros((1, 256), F32)), unroll=2)
     sq[...] = jnp.broadcast_to(jnp.sum(acc, axis=1, keepdims=True), sq.shape)
 
     for j in range(Z):
@@ -159,7 +159,7 @@
         def body(j):
             dst[j] = dot(cat(a), b[j]).astype(BF16)
 
-        loop(4, body, 2)
+        loop(4, body, 4)
 
     mul(t0, f0, f0)
     mul(f1, t0, t0)
@@ -171,7 +171,7 @@
         t0[j] = t0[j] * jnp.asarray(-0.25, BF16)
         t0[j, pl.ds(r, 256), :] = diag
 
-    loop(4, second)
+    loop(4, second, 4)
     mul(root, f0, t0)
 
 
@@ -183,7 +183,7 @@
         def mixed(j):
             mix[j] = dot(cat(left), grad[j]).astype(BF16)
 
-        loop(4, mixed)
+        loop(4, mixed, 2)
 
         def raw(j, acc):
             r = dot(cat(mix), right[j])
@@ -191,11 +191,11 @@
             keep[j] = r_s[pl.ds(zr, 64), :]
             return acc + jnp.sum(r * r, axis=0, keepdims=True)
 
-        update_sq = jnp.sum(lax.fori_loop(0, 4, raw, jnp.zeros((1, 256), F32)), axis=1, keepdims=True)
+        update_sq = jnp.sum(lax.fori_loop(0, 4, raw, jnp.zeros((1, 256), F32), unroll=2), axis=1, keepdims=True)
 
         ratio = jnp.sqrt(grad_sq[:1, :1] / (update_sq + 1e-6))
         for j in range(4):
-            out[:, 256 * j:256 * (j + 1)] = (keep[j] * ratio).astype(BF16)
+            out[0, :, 256 * j:256 * (j + 1)] = (keep[j] * ratio).astype(BF16)
 
     pl.when(co == 0)(lambda: run(own, other))
     pl.when(co == 1)(lambda: run(other, own))
@@ -227,10 +227,10 @@
 def step(inputs, output_grads, statistics):
     z = lax.axis_index("tok")
     co = lax.axis_index("co")
-    idx1 = jnp.stack([co, z, lax.axis_index("y")]).astype(jnp.int32)
+    idx1 = jnp.stack([co, z, lax.axis_index("y") ^ lax.axis_index(("xl", "pair"))]).astype(jnp.int32)
     idx2 = jnp.stack([z, co]).astype(jnp.int32)
 
-    table = [(yy * 4 + xx, xx * 4 + yy) for yy in range(4) for xx in range(4)]
+    table = [(yy * 4 + xx, (xx ^ yy) * 4 + yy) for yy in range(4) for xx in range(4)]
     cot = [lax.ppermute(output_grads, ("y", "xl", "pair"), table)]
     a_own = everyone(inputs, ("xl", "pair"), 4)
     for d in range(1, 4):
@@ -307,7 +307,7 @@
     back = lax.ppermute(rows, ("co", "pair"), SWAP)
     final = pl.pallas_call(
         update_kernel,
-        out_shape=sds((64, 1024), BF16),
+        out_shape=sds((1, 64, 1024), BF16),
         in_specs=[SMEM] + [VMEM] * 4,
         out_specs=VMEM,
         scratch_shapes=[pltpu.VMEM((4, 1024, 256), BF16), pltpu.VMEM((1024, 256), F32), pltpu.VMEM((4, 64, 256), F32)],
@@ -316,7 +316,7 @@
     )(idx2, root, other_root, grad, grad_sq)
     update = lax.ppermute(final, ("co", "pair"), SWAP)
     new_rows = 0.9 * stat + back
-    return update[None], new_rows[None, None]
+    return update, new_rows[None, None]
 
 
 def solution(mesh):

time: 187 us -> 184 us (0.984)
  Pallas kernels: 27.2 us -> 24.4 us
    ppermute x1, starting transfers between devices: 2.16 us -> 4.83 us  [step(): st = lax.ppermute(st, ('co', 'pair'), SWAP)]
    ppermute x7, starting transfers between devices: 22.2 us -> 19.7 us  [sibling(): return lax.ppermute(x, 'co', [(0, 1), (1, 0)])]
    pallas_call x1, Pallas kernels: 16.4 us -> 14.1 us  [step(): pl.pallas_call(chain_kernel, out_shape=(sds((4, 1024, 256), BF16), sds((4...]
  transfers between devices with their start and end apart: 26 -> 26, of which waited for: 11 -> 11; matrix products, arithmetic and copies ran while one was open for 7% -> 7% of each run, Pallas kernels for 5% -> 4%
where the time goes in v4:
time: 184 us; the launch traced here: 183 us
  starting transfers between devices  68.7 us (37%)
  waiting for transfers between devices  54.5 us (30%)
  Pallas kernels  24.4 us (13%)
  blocking collectives  17.8 us (10%)
  local copies, waits for them, and re-layouts  10.2 us (6%)
  other arithmetic  5.82 us (3%)
    ppermute x7, waiting for transfers between devices, along(): return lax.ppermute(x, 'tok', [(i, (i + d) % Z) for i in range(Z)])  31.1 us
    ppermute x7, starting transfers between devices, sibling(): return lax.ppermute(x, 'co', [(0, 1), (1, 0)])  19.7 us
    all_to_all x1, blocking collectives, everyone(): lax.all_to_all(jnp.broadcast_to(x, (n, *x.shape)), axis, 0, 0, tiled=True)  17.8 us
    pallas_call x1, Pallas kernels, step(): pl.pallas_call(chain_kernel, out_shape=(sds((4, 1024, 256), BF16), sds((4...  14.1 us
    ppermute x3, starting transfers between devices, step(): cot.append(lax.ppermute(cot[0], 'y', [(i, i ^ d) for i in range(4)]))  12.5 us
    ppermute x3, waiting for transfers between devices, step(): cot.append(lax.ppermute(cot[0], 'y', [(i, i ^ d) for i in range(4)]))  10.7 us
    ppermute x7, starting transfers between devices, along(): return lax.ppermute(x, 'tok', [(i, (i + d) % Z) for i in range(Z)])  9.25 us
    ppermute x4, starting transfers between devices, pass_on(): return lax.ppermute(x, ('tok', 'co'), perm)  8.91 us
  transfers between devices with their start and end apart: 26, of which 11 were waited for; matrix products, arithmetic and copies ran while one was open for 7% of the time, Pallas kernels for 4%

profile of v4, /device:TPU:33, one launch (start us, length us, event | category | flops | bytes accessed | tf_op | source)
XLA Modules:
  0.0 182.9 jit_solution(17679853821785575868)
XLA Ops:
  1.7 17.8 %all_to_all.10.a_own = bf16[4,512,256]{2,1,0:T(8,128)(2,1)S(1)} all-to-all(bf16[4,512,256]{2,1,0:T(8,128)(2,1)S(1)} %broadcast_in_dim.7), channel_id=1, replica_groups=mesh['tok'=8,'y'=4,'xl'=2,'co'=2,'pair'=2] {'xl','pair'}, dimensions={0} | all-to-all | bytes 2097152 | tf_op jit(solution)/shard_map/all_to_all | solution.py:216
  19.5 1.8 collective-permute-start.8
  24.6 4.6 %collective-permute-done.3 = f16[136,640]{1,0:T(8,128)(2,1)S(1)} collective-permute-done((f16[136,640]{1,0:T(8,128)(2,1)S(1)}, f16[136,640]{1,0:T(8,128)(2,1)S(1)}, u32[]{:S(2)}, u32[]{:S(2)}) %collective-permute-start.3) | collective-permute-done | bytes 174112 | tf_op jit(solution)/shard_map/ppermute | solution.py:224
  29.2 2.9 %collective-permute-start.4 = (f16[136,640]{1,0:T(8,128)(2,1)S(1)}, f16[136,640]{1,0:T(8,128)(2,1)S(1)}, u32[]{:S(2)}, u32[]{:S(2)}) collective-permute-start(f16[136,640]{1,0:T(8,128)(2,1)S(1)} %collective-permute-done.3), channel_id=1, source_target_pairs={{0,224},{32,0},{64,32},{96,64},{128,96},{160,128},{192,160},{224,1... | collective-permute-start | bytes 522248 | tf_op jit(solution)/shard_map/ppermute | solution.py:224
  35.0 3.4 %collective-permute-start.5 = (f16[136,640]{1,0:T(8,128)(2,1)S(1)}, f16[136,640]{1,0:T(8,128)(2,1)}, u32[]{:S(2)}, u32[]{:S(2)}) collective-permute-start(f16[136,640]{1,0:T(8,128)(2,1)S(1)} %collective-permute-done.4), channel_id=1, source_target_pairs={{0,224},{32,0},{64,32},{96,64},{128,96},{160,128},{192,160},{224,1... | collective-permute-start | bytes 522248 | tf_op jit(solution)/shard_map/ppermute | solution.py:224
  38.4 2.4 %collective-permute-done.1 = f16[136,640]{1,0:T(8,128)(2,1)} collective-permute-done((f16[136,640]{1,0:T(8,128)(2,1)S(1)}, f16[136,640]{1,0:T(8,128)(2,1)}, u32[]{:S(2)}, u32[]{:S(2)}) %collective-permute-start.1) | collective-permute-done | bytes 174112 | tf_op jit(solution)/shard_map/ppermute | solution.py:224
  40.9 12.0 %collective-permute-start.12 = (bf16[512,256]{1,0:T(8,128)(2,1)S(1)}, bf16[512,256]{1,0:T(8,128)(2,1)S(1)}, u32[]{:S(2)}, u32[]{:S(2)}) collective-permute-start(bf16[512,256]{1,0:T(8,128)(2,1)S(1)} %collective-permute-done.9.b0), channel_id=1, source_target_pairs={{0,24},{8,16},{16,8},{24,0},{1,25},{9,17},{17,9},{25,1},{2,26},{10... | collective-permute-start | bytes 786440 | tf_op jit(solution)/shard_map/ppermute | solution.py:237
  54.2 10.3 %collective-permute-done.12.b3 = bf16[512,256]{1,0:T(8,128)(2,1)S(1)} collective-permute-done((bf16[512,256]{1,0:T(8,128)(2,1)S(1)}, bf16[512,256]{1,0:T(8,128)(2,1)S(1)}, u32[]{:S(2)}, u32[]{:S(2)}) %collective-permute-start.12) | collective-permute-done | bytes 262176 | tf_op jit(solution)/shard_map/ppermute | solution.py:237
  64.9 2.1 %partial_gradient.1 = f32[8,136,512]{2,1,0:T(8,128)S(1)} custom-call(s32[3]{0:T(128)S(1)} %pad_add_fusion.1.idx, bf16[4,512,256]{2,1,0:T(8,128)(2,1)S(1)} %all_to_all.10.a_own, bf16[4,512,256]{2,1,0:T(8,128)(2,1)S(1)} %collective-permute-done.8.a_oth, bf16[512,256]{1,0:T(8,128)(2,1)S(1)} %collective-permute-done.9.b0, ...), custom_call_target="tpu_custom_call" | custom-call | tf_op jit(solution)/shard_map/partial_gradient/pallas_call | solution.py:250
  68.3 7.0 %all-to-all-start.1 = ((f16[8,136,512]{2,1,0:T(8,128)(2,1)}), f16[8,136,512]{2,1,0:T(8,128)(2,1)S(1)}, u32[]{:S(2)}, u32[]{:S(2)}) async-start(f16[8,136,512]{2,1,0:T(8,128)(2,1)} %convert_element_type.29), calls=%async_computation.1 | async-start | bytes 2228224 | tf_op jit(solution)/shard_map/all_to_all | solution.py:272
  80.5 22.7 %collective-permute-done.6 = f16[136,640]{1,0:T(8,128)(2,1)S(1)} collective-permute-done((f16[136,640]{1,0:T(8,128)(2,1)}, f16[136,640]{1,0:T(8,128)(2,1)S(1)}, u32[]{:S(2)}, u32[]{:S(2)}) %collective-permute-start.6) | collective-permute-done | bytes 174112 | tf_op jit(solution)/shard_map/ppermute | solution.py:224
  106.9 4.8 %collective-permute-start.7 = (f16[8,136,640]{2,1,0:T(8,128)(2,1)}, f16[8,136,640]{2,1,0:T(8,128)(2,1)}, u32[]{:S(2)}, u32[]{:S(2)}) collective-permute-start(f16[8,136,640]{2,1,0:T(8,128)(2,1)} %bitcast_dynamic-update-slice_fusion), channel_id=1, source_target_pairs={{0,0},{1,2},{2,1},{3,3},{4,4},{5,6},{6,5},{7,7},{8,8},{9,10},{10,9... | collective-permute-start | bytes 4177928 | tf_op jit(solution)/shard_map/ppermute | solution.py:262
  112.0 9.1 %collective-permute-start.13 = (bf16[128,512]{1,0:T(8,128)(2,1)S(1)}, bf16[128,512]{1,0:T(8,128)(2,1)S(1)}, u32[]{:S(2)}, u32[]{:S(2)}) collective-permute-start(bf16[128,512]{1,0:T(8,128)(2,1)S(1)} %multiply_reduce_fusion.mine), channel_id=1, source_target_pairs={{0,2},{2,0},{1,3},{3,1},{4,6},{6,4},{5,7},{7,5},{8,10},{10,8},{9,1... | collective-permute-start | bytes 393224 | tf_op jit(solution)/shard_map/ppermute | solution.py:220
  122.7 3.7 %collective-permute-start.15 = (bf16[2,128,512]{2,1,0:T(8,128)(2,1)S(1)}, bf16[2,128,512]{2,1,0:T(8,128)(2,1)S(1)}, u32[]{:S(2)}, u32[]{:S(2)}) collective-permute-start(bf16[2,128,512]{2,1,0:T(8,128)(2,1)S(1)} %merge.1.g0), channel_id=1, source_target_pairs={{0,64},{2,194},{32,96},{34,226},{64,128},{66,2},{96,160},{98,34},{... | collective-permute-start | bytes 786440 | tf_op jit(solution)/shard_map/ppermute | solution.py:284
  127.5 5.1 %collective-permute-done.15.src.r2 = bf16[2,128,512]{2,1,0:T(8,128)(2,1)S(1)} collective-permute-done((bf16[2,128,512]{2,1,0:T(8,128)(2,1)S(1)}, bf16[2,128,512]{2,1,0:T(8,128)(2,1)S(1)}, u32[]{:S(2)}, u32[]{:S(2)}) %collective-permute-start.15) | collective-permute-done | bytes 262176 | tf_op jit(solution)/shard_map/ppermute | solution.py:284
  133.8 3.5 %collective-permute-start.17 = (bf16[2,64,512]{2,1,0:T(8,128)(2,1)S(1)}, bf16[2,64,512]{2,1,0:T(8,128)(2,1)S(1)}, u32[]{:S(2)}, u32[]{:S(2)}) collective-permute-start(bf16[2,64,512]{2,1,0:T(8,128)(2,1)S(1)} %half.1), channel_id=1, source_target_pairs={{0,64},{2,194},{32,96},{34,226},{64,128},{66,2},{96,160},{98,34},{... | collective-permute-start | bytes 393224 | tf_op jit(solution)/shard_map/ppermute | solution.py:284
  138.2 3.1 %collective-permute-start.19 = (bf16[2,128,512]{2,1,0:T(8,128)(2,1)S(1)}, bf16[2,128,512]{2,1,0:T(8,128)(2,1)S(1)}, u32[]{:S(2)}, u32[]{:S(2)}) collective-permute-start(bf16[2,128,512]{2,1,0:T(8,128)(2,1)S(1)} %collective-permute-done.15.src.r2), channel_id=1, source_target_pairs={{0,2},{2,0},{1,3},{3,1},{4,6},{6,4},{5,7},{7,5},{8,10},{10,8},{9,1... | collective-permute-start | bytes 786440 | tf_op jit(solution)/shard_map/ppermute | solution.py:220
  141.9 5.2 %collective-permute-start.21 = (bf16[2,64,512]{2,1,0:T(8,128)(2,1)S(1)}, bf16[2,64,512]{2,1,0:T(8,128)(2,1)S(1)}, u32[]{:S(2)}, u32[]{:S(2)}) collective-permute-start(bf16[2,64,512]{2,1,0:T(8,128)(2,1)S(1)} %collective-permute-done.17.r4), channel_id=1, source_target_pairs={{0,2},{2,0},{1,3},{3,1},{4,6},{6,4},{5,7},{7,5},{8,10},{10,8},{9,1... | collective-permute-start | bytes 393224 | tf_op jit(solution)/shard_map/ppermute | solution.py:220
  149.9 14.1 %inverse_root.1 = (bf16[4,1024,256]{2,1,0:T(8,128)(2,1)S(1)}, bf16[4,1024,256]{2,1,0:T(8,128)(2,1)S(1)}, f32[128,1024]{1,0:T(8,128)S(1)}, f32[8,128]{1,0:T(8,128)S(1)}) custom-call(s32[2]{0:T(128)S(1)} %pad_add_fusion.idx, f32[8,1024,128]{2,1,0:T(8,128)S(1)} %assemble.1.st, bf16[2,128,512]{2,1,0:T(8,128)(2,1)S(1)} %merge.1.g0, ...), custom_call_target="tpu_custom_call" | custom-call | tf_op jit(solution)/shard_map/inverse_root/pallas_call | solution.py:295
  164.4 1.9 %collective-permute-start.24 = (f32[128,1024]{1,0:T(8,128)S(1)}, f32[128,1024]{1,0:T(8,128)S(1)}, u32[]{:S(2)}, u32[]{:S(2)}) collective-permute-start(f32[128,1024]{1,0:T(8,128)S(1)} %get-tuple-element.23), channel_id=1, source_target_pairs={{0,0},{1,2},{2,1},{3,3},{4,4},{5,6},{6,5},{7,7},{8,8},{9,10},{10,9... | collective-permute-start | bytes 1572872 | tf_op jit(solution)/shard_map/ppermute | solution.py:307
  166.3 2.2 %collective-permute-done.22.other = bf16[4,1024,256]{2,1,0:T(8,128)(2,1)S(1)} collective-permute-done((bf16[4,1024,256]{2,1,0:T(8,128)(2,1)S(1)}, bf16[4,1024,256]{2,1,0:T(8,128)(2,1)S(1)}, u32[]{:S(2)}, u32[]{:S(2)}) %collective-permute-start.22) | collective-permute-done | bytes 2097184 | tf_op jit(solution)/shard_map/ppermute | solution.py:220
  168.5 5.8 %update_rows.1 = bf16[1,64,1024]{2,1,0:T(8,128)(2,1)S(1)} custom-call(s32[2]{0:T(128)S(1)} %pad_add_fusion.idx, bf16[4,1024,256]{2,1,0:T(8,128)(2,1)S(1)} %get-tuple-element.20.own, bf16[4,1024,256]{2,1,0:T(8,128)(2,1)S(1)} %collective-permute-done.22.other, bf16[4,1024,256]{2,1,0:T(8,128)(2,1)S(1)} %get-tuple-element.21.grad, ...), custom_call_target="tpu_custom_call" | custom-call | tf_op jit(solution)/shard_map/update_rows/pallas_call | solution.py:308
  174.4 2.9 %collective-permute-start.23 = (bf16[1,64,1024]{2,1,0:T(8,128)(2,1)S(1)}, bf16[1,64,1024]{2,1,0:T(8,128)(2,1)S(1)}, u32[]{:S(2)}, u32[]{:S(2)}) collective-permute-start(bf16[1,64,1024]{2,1,0:T(8,128)(2,1)S(1)} %update_rows.1), channel_id=1, source_target_pairs={{0,0},{1,2},{2,1},{3,3},{4,4},{5,6},{6,5},{7,7},{8,8},{9,10},{10,9... | collective-permute-start | bytes 393224 | tf_op jit(solution)/shard_map/ppermute | solution.py:317
  178.2 4.0 %collective-permute-done.23 = bf16[1,64,1024]{2,1,0:T(8,128)(2,1)S(1)} collective-permute-done((bf16[1,64,1024]{2,1,0:T(8,128)(2,1)S(1)}, bf16[1,64,1024]{2,1,0:T(8,128)(2,1)S(1)}, u32[]{:S(2)}, u32[]{:S(2)}) %collective-permute-start.23) | collective-permute-done | bytes 131104 | tf_op jit(solution)/shard_map/ppermute | solution.py:317
  (65 shorter events, 28.7 us)
Async XLA Ops:
  19.5 45.4 %collective-permute-start.8 = (bf16[4,512,256]{2,1,0:T(8,128)(2,1)S(1)}, bf16[4,512,256]{2,1,0:T(8,128)(2,1)S(1)}, u32[]{:S(2)}, u32[]{:S(2)}) collective-permute-start(bf16[4,512,256]{2,1,0:T(8,128)(2,1)S(1)} %all_to_all.10.a_own), channel_id=1, source_target_pairs={{0,2},{2,0},{1,3},{3,1},{4,6},{6,4},{5,7},{7,5},{8,10},{10,8},{9,1... | collective-permute-start | bytes 3145736 | tf_op jit(solution)/shard_map/ppermute | solution.py:220
  22.8 6.4 %collective-permute-start.3 = (f16[136,640]{1,0:T(8,128)(2,1)S(1)}, f16[136,640]{1,0:T(8,128)(2,1)S(1)}, u32[]{:S(2)}, u32[]{:S(2)}) collective-permute-start(f16[136,640]{1,0:T(8,128)(2,1)S(1)} %concatenate.7), channel_id=1, source_target_pairs={{0,224},{32,0},{64,32},{96,64},{128,96},{160,128},{192,160},{224,1... | collective-permute-start | bytes 522248 | tf_op jit(solution)/shard_map/ppermute | solution.py:224
  22.9 10.8 %collective-permute-start = (f16[136,640]{1,0:T(8,128)(2,1)S(1)}, f16[136,640]{1,0:T(8,128)(2,1)S(1)}, u32[]{:S(2)}, u32[]{:S(2)}) collective-permute-start(f16[136,640]{1,0:T(8,128)(2,1)S(1)} %concatenate.7), channel_id=1, source_target_pairs={{0,32},{32,64},{64,96},{96,128},{128,160},{160,192},{192,224},{224... | collective-permute-start | bytes 522248 | tf_op jit(solution)/shard_map/ppermute | solution.py:224
  29.2 5.8 %collective-permute-start.4 = (f16[136,640]{1,0:T(8,128)(2,1)S(1)}, f16[136,640]{1,0:T(8,128)(2,1)S(1)}, u32[]{:S(2)}, u32[]{:S(2)}) collective-permute-start(f16[136,640]{1,0:T(8,128)(2,1)S(1)} %collective-permute-done.3), channel_id=1, source_target_pairs={{0,224},{32,0},{64,32},{96,64},{128,96},{160,128},{192,160},{224,1... | collective-permute-start | bytes 522248 | tf_op jit(solution)/shard_map/ppermute | solution.py:224
  32.1 8.8 %collective-permute-start.9 = (bf16[512,256]{1,0:T(8,128)(2,1)}, bf16[512,256]{1,0:T(8,128)(2,1)S(1)}, u32[]{:S(2)}, u32[]{:S(2)}) collective-permute-start(bf16[512,256]{1,0:T(8,128)(2,1)} %param.4), channel_id=1, source_target_pairs={{0,0},{1,8},{4,16},{5,24},{8,9},{9,1},{12,25},{13,17},{16,20},{17,... | collective-permute-start | bytes 786440 | tf_op jit(solution)/shard_map/ppermute | solution.py:234
  33.7 7.2 %collective-permute-start.1 = (f16[136,640]{1,0:T(8,128)(2,1)S(1)}, f16[136,640]{1,0:T(8,128)(2,1)}, u32[]{:S(2)}, u32[]{:S(2)}) collective-permute-start(f16[136,640]{1,0:T(8,128)(2,1)S(1)} %collective-permute-done), channel_id=1, source_target_pairs={{0,32},{32,64},{64,96},{96,128},{128,160},{160,192},{192,224},{224... | collective-permute-start | bytes 522248 | tf_op jit(solution)/shard_map/ppermute | solution.py:224
  35.0 17.8 %collective-permute-start.5 = (f16[136,640]{1,0:T(8,128)(2,1)S(1)}, f16[136,640]{1,0:T(8,128)(2,1)}, u32[]{:S(2)}, u32[]{:S(2)}) collective-permute-start(f16[136,640]{1,0:T(8,128)(2,1)S(1)} %collective-permute-done.4), channel_id=1, source_target_pairs={{0,224},{32,0},{64,32},{96,64},{128,96},{160,128},{192,160},{224,1... | collective-permute-start | bytes 522248 | tf_op jit(solution)/shard_map/ppermute | solution.py:224
  40.9 12.6 %collective-permute-start.2 = (f16[136,640]{1,0:T(8,128)(2,1)}, f16[136,640]{1,0:T(8,128)(2,1)}, u32[]{:S(2)}, u32[]{:S(2)}) collective-permute-start(f16[136,640]{1,0:T(8,128)(2,1)} %collective-permute-done.1), channel_id=1, source_target_pairs={{0,32},{32,64},{64,96},{96,128},{128,160},{160,192},{192,224},{224... | collective-permute-start | bytes 522248 | tf_op jit(solution)/shard_map/ppermute | solution.py:224
  40.9 23.7 %collective-permute-start.12 = (bf16[512,256]{1,0:T(8,128)(2,1)S(1)}, bf16[512,256]{1,0:T(8,128)(2,1)S(1)}, u32[]{:S(2)}, u32[]{:S(2)}) collective-permute-start(bf16[512,256]{1,0:T(8,128)(2,1)S(1)} %collective-permute-done.9.b0), channel_id=1, source_target_pairs={{0,24},{8,16},{16,8},{24,0},{1,25},{9,17},{17,9},{25,1},{2,26},{10... | collective-permute-start | bytes 786440 | tf_op jit(solution)/shard_map/ppermute | solution.py:237
  52.8 11.7 %collective-permute-start.11 = (bf16[512,256]{1,0:T(8,128)(2,1)S(1)}, bf16[512,256]{1,0:T(8,128)(2,1)S(1)}, u32[]{:S(2)}, u32[]{:S(2)}) collective-permute-start(bf16[512,256]{1,0:T(8,128)(2,1)S(1)} %collective-permute-done.9.b0), channel_id=1, source_target_pairs={{0,16},{8,24},{16,0},{24,8},{1,17},{9,25},{17,1},{25,9},{2,18},{10... | collective-permute-start | bytes 786440 | tf_op jit(solution)/shard_map/ppermute | solution.py:237
  52.8 12.1 %collective-permute-start.10 = (bf16[512,256]{1,0:T(8,128)(2,1)S(1)}, bf16[512,256]{1,0:T(8,128)(2,1)S(1)}, u32[]{:S(2)}, u32[]{:S(2)}) collective-permute-start(bf16[512,256]{1,0:T(8,128)(2,1)S(1)} %collective-permute-done.9.b0), channel_id=1, source_target_pairs={{0,8},{8,0},{16,24},{24,16},{1,9},{9,1},{17,25},{25,17},{2,10},{10... | collective-permute-start | bytes 786440 | tf_op jit(solution)/shard_map/ppermute | solution.py:237
  68.3 43.4 %all-to-all-start.1 = ((f16[8,136,512]{2,1,0:T(8,128)(2,1)}), f16[8,136,512]{2,1,0:T(8,128)(2,1)S(1)}, u32[]{:S(2)}, u32[]{:S(2)}) async-start(f16[8,136,512]{2,1,0:T(8,128)(2,1)} %convert_element_type.29), calls=%async_computation.1 | async-start | bytes 2228224 | tf_op jit(solution)/shard_map/all_to_all | solution.py:272
  76.0 27.2 %collective-permute-start.6 = (f16[136,640]{1,0:T(8,128)(2,1)}, f16[136,640]{1,0:T(8,128)(2,1)S(1)}, u32[]{:S(2)}, u32[]{:S(2)}) collective-permute-start(f16[136,640]{1,0:T(8,128)(2,1)} %collective-permute-done.2), channel_id=1, source_target_pairs={{0,32},{32,64},{64,96},{96,128},{128,160},{160,192},{192,224},{224... | collective-permute-start | bytes 522248 | tf_op jit(solution)/shard_map/ppermute | solution.py:224
  106.9 30.4 %collective-permute-start.7 = (f16[8,136,640]{2,1,0:T(8,128)(2,1)}, f16[8,136,640]{2,1,0:T(8,128)(2,1)}, u32[]{:S(2)}, u32[]{:S(2)}) collective-permute-start(f16[8,136,640]{2,1,0:T(8,128)(2,1)} %bitcast_dynamic-update-slice_fusion), channel_id=1, source_target_pairs={{0,0},{1,2},{2,1},{3,3},{4,4},{5,6},{6,5},{7,7},{8,8},{9,10},{10,9... | collective-permute-start | bytes 4177928 | tf_op jit(solution)/shard_map/ppermute | solution.py:262
  112.0 10.1 %collective-permute-start.13 = (bf16[128,512]{1,0:T(8,128)(2,1)S(1)}, bf16[128,512]{1,0:T(8,128)(2,1)S(1)}, u32[]{:S(2)}, u32[]{:S(2)}) collective-permute-start(bf16[128,512]{1,0:T(8,128)(2,1)S(1)} %multiply_reduce_fusion.mine), channel_id=1, source_target_pairs={{0,2},{2,0},{1,3},{3,1},{4,6},{6,4},{5,7},{7,5},{8,10},{10,8},{9,1... | collective-permute-start | bytes 393224 | tf_op jit(solution)/shard_map/ppermute | solution.py:220
  122.7 9.8 %collective-permute-start.15 = (bf16[2,128,512]{2,1,0:T(8,128)(2,1)S(1)}, bf16[2,128,512]{2,1,0:T(8,128)(2,1)S(1)}, u32[]{:S(2)}, u32[]{:S(2)}) collective-permute-start(bf16[2,128,512]{2,1,0:T(8,128)(2,1)S(1)} %merge.1.g0), channel_id=1, source_target_pairs={{0,64},{2,194},{32,96},{34,226},{64,128},{66,2},{96,160},{98,34},{... | collective-permute-start | bytes 786440 | tf_op jit(solution)/shard_map/ppermute | solution.py:284
  126.4 14.9 %collective-permute-start.14 = (bf16[2,128,512]{2,1,0:T(8,128)(2,1)S(1)}, bf16[2,128,512]{2,1,0:T(8,128)(2,1)S(1)}, u32[]{:S(2)}, u32[]{:S(2)}) collective-permute-start(bf16[2,128,512]{2,1,0:T(8,128)(2,1)S(1)} %merge.1.g0), channel_id=1, source_target_pairs={{0,32},{2,226},{32,64},{34,2},{64,96},{66,34},{96,128},{98,66},{12... | collective-permute-start | bytes 786440 | tf_op jit(solution)/shard_map/ppermute | solution.py:284
  132.6 14.5 %collective-permute-start.16 = (bf16[2,128,512]{2,1,0:T(8,128)(2,1)S(1)}, bf16[2,128,512]{2,1,0:T(8,128)(2,1)S(1)}, u32[]{:S(2)}, u32[]{:S(2)}) collective-permute-start(bf16[2,128,512]{2,1,0:T(8,128)(2,1)S(1)} %collective-permute-done.15.src.r2), channel_id=1, source_target_pairs={{0,32},{2,226},{32,64},{34,2},{64,96},{66,34},{96,128},{98,66},{12... | collective-permute-start | bytes 786440 | tf_op jit(solution)/shard_map/ppermute | solution.py:284
  133.8 8.0 %collective-permute-start.17 = (bf16[2,64,512]{2,1,0:T(8,128)(2,1)S(1)}, bf16[2,64,512]{2,1,0:T(8,128)(2,1)S(1)}, u32[]{:S(2)}, u32[]{:S(2)}) collective-permute-start(bf16[2,64,512]{2,1,0:T(8,128)(2,1)S(1)} %half.1), channel_id=1, source_target_pairs={{0,64},{2,194},{32,96},{34,226},{64,128},{66,2},{96,160},{98,34},{... | collective-permute-start | bytes 393224 | tf_op jit(solution)/shard_map/ppermute | solution.py:284
  138.2 11.7 %collective-permute-start.19 = (bf16[2,128,512]{2,1,0:T(8,128)(2,1)S(1)}, bf16[2,128,512]{2,1,0:T(8,128)(2,1)S(1)}, u32[]{:S(2)}, u32[]{:S(2)}) collective-permute-start(bf16[2,128,512]{2,1,0:T(8,128)(2,1)S(1)} %collective-permute-done.15.src.r2), channel_id=1, source_target_pairs={{0,2},{2,0},{1,3},{3,1},{4,6},{6,4},{5,7},{7,5},{8,10},{10,8},{9,1... | collective-permute-start | bytes 786440 | tf_op jit(solution)/shard_map/ppermute | solution.py:220
  141.3 8.6 %collective-permute-start.18 = (bf16[2,128,512]{2,1,0:T(8,128)(2,1)S(1)}, bf16[2,128,512]{2,1,0:T(8,128)(2,1)S(1)}, u32[]{:S(2)}, u32[]{:S(2)}) collective-permute-start(bf16[2,128,512]{2,1,0:T(8,128)(2,1)S(1)} %collective-permute-done.14.r1), channel_id=1, source_target_pairs={{0,2},{2,0},{1,3},{3,1},{4,6},{6,4},{5,7},{7,5},{8,10},{10,8},{9,1... | collective-permute-start | bytes 786440 | tf_op jit(solution)/shard_map/ppermute | solution.py:220
  141.9 8.0 %collective-permute-start.21 = (bf16[2,64,512]{2,1,0:T(8,128)(2,1)S(1)}, bf16[2,64,512]{2,1,0:T(8,128)(2,1)S(1)}, u32[]{:S(2)}, u32[]{:S(2)}) collective-permute-start(bf16[2,64,512]{2,1,0:T(8,128)(2,1)S(1)} %collective-permute-done.17.r4), channel_id=1, source_target_pairs={{0,2},{2,0},{1,3},{3,1},{4,6},{6,4},{5,7},{7,5},{8,10},{10,8},{9,1... | collective-permute-start | bytes 393224 | tf_op jit(solution)/shard_map/ppermute | solution.py:220
  164.4 13.0 %collective-permute-start.24 = (f32[128,1024]{1,0:T(8,128)S(1)}, f32[128,1024]{1,0:T(8,128)S(1)}, u32[]{:S(2)}, u32[]{:S(2)}) collective-permute-start(f32[128,1024]{1,0:T(8,128)S(1)} %get-tuple-element.23), channel_id=1, source_target_pairs={{0,0},{1,2},{2,1},{3,3},{4,4},{5,6},{6,5},{7,7},{8,8},{9,10},{10,9... | collective-permute-start | bytes 1572872 | tf_op jit(solution)/shard_map/ppermute | solution.py:307
  174.4 7.8 %collective-permute-start.23 = (bf16[1,64,1024]{2,1,0:T(8,128)(2,1)S(1)}, bf16[1,64,1024]{2,1,0:T(8,128)(2,1)S(1)}, u32[]{:S(2)}, u32[]{:S(2)}) collective-permute-start(bf16[1,64,1024]{2,1,0:T(8,128)(2,1)S(1)} %update_rows.1), channel_id=1, source_target_pairs={{0,0},{1,2},{2,1},{3,3},{4,4},{5,6},{6,5},{7,7},{8,8},{9,10},{10,9... | collective-permute-start | bytes 393224 | tf_op jit(solution)/shard_map/ppermute | solution.py:317
  (5 other events, 36.3 us)

commit v5 on v4

--- a/solution.py
+++ b/solution.py
@@ -132,7 +132,7 @@
         v = grad[j].astype(F32)
         return top, acc + jnp.sum(v * v, axis=0, keepdims=True)
 
-    top, acc = lax.fori_loop(0, 4, product, (jnp.zeros((1, 128), F32), jnp.zeros((1, 256), F32)), unroll=2)
+    top, acc = lax.fori_loop(0, 4, product, (jnp.zeros((1, 128), F32), jnp.zeros((1, 256), F32)), unroll=4)
     sq[...] = jnp.broadcast_to(jnp.sum(acc, axis=1, keepdims=True), sq.shape)
 
     for j in range(Z):
@@ -183,7 +183,7 @@
         def mixed(j):
             mix[j] = dot(cat(left), grad[j]).astype(BF16)
 
-        loop(4, mixed, 2)
+        loop(4, mixed, 4)
 
         def raw(j, acc):
             r = dot(cat(mix), right[j])
@@ -191,7 +191,7 @@
             keep[j] = r_s[pl.ds(zr, 64), :]
             return acc + jnp.sum(r * r, axis=0, keepdims=True)
 
-        update_sq = jnp.sum(lax.fori_loop(0, 4, raw, jnp.zeros((1, 256), F32), unroll=2), axis=1, keepdims=True)
+        update_sq = jnp.sum(lax.fori_loop(0, 4, raw, jnp.zeros((1, 256), F32), unroll=4), axis=1, keepdims=True)
 
         ratio = jnp.sqrt(grad_sq[:1, :1] / (update_sq + 1e-6))
         for j in range(4):
@@ -227,10 +227,10 @@
 def step(inputs, output_grads, statistics):
     z = lax.axis_index("tok")
     co = lax.axis_index("co")
-    idx1 = jnp.stack([co, z, lax.axis_index("y") ^ lax.axis_index(("xl", "pair"))]).astype(jnp.int32)
+    idx1 = jnp.stack([co, z, lax.axis_index("y")]).astype(jnp.int32)
     idx2 = jnp.stack([z, co]).astype(jnp.int32)
 
-    table = [(yy * 4 + xx, (xx ^ yy) * 4 + yy) for yy in range(4) for xx in range(4)]
+    table = [(yy * 4 + xx, xx * 4 + yy) for yy in range(4) for xx in range(4)]
     cot = [lax.ppermute(output_grads, ("y", "xl", "pair"), table)]
     a_own = everyone(inputs, ("xl", "pair"), 4)
     for d in range(1, 4):

time: 184 us -> 184 us (level)
    ppermute x1, starting transfers between devices: 4.83 us -> 2.16 us  [step(): st = lax.ppermute(st, ('co', 'pair'), SWAP)]
    ppermute x7, starting transfers between devices: 19.7 us -> 22.2 us  [sibling(): return lax.ppermute(x, 'co', [(0, 1), (1, 0)])]
where the time goes in v5:
time: 184 us; the launch traced here: 183 us
  starting transfers between devices  68.5 us (37%)
  waiting for transfers between devices  54.5 us (30%)
  Pallas kernels  24.3 us (13%)
  blocking collectives  17.8 us (10%)
  local copies, waits for them, and re-layouts  10.2 us (6%)
  other arithmetic  5.83 us (3%)
    ppermute x7, waiting for transfers between devices, along(): return lax.ppermute(x, 'tok', [(i, (i + d) % Z) for i in range(Z)])  31.1 us
    ppermute x7, starting transfers between devices, sibling(): return lax.ppermute(x, 'co', [(0, 1), (1, 0)])  22.2 us
    all_to_all x1, blocking collectives, everyone(): lax.all_to_all(jnp.broadcast_to(x, (n, *x.shape)), axis, 0, 0, tiled=True)  17.8 us
    pallas_call x1, Pallas kernels, step(): pl.pallas_call(chain_kernel, out_shape=(sds((4, 1024, 256), BF16), sds((4...  14.3 us
    ppermute x3, starting transfers between devices, step(): cot.append(lax.ppermute(cot[0], 'y', [(i, i ^ d) for i in range(4)]))  12.5 us
    ppermute x3, waiting for transfers between devices, step(): cot.append(lax.ppermute(cot[0], 'y', [(i, i ^ d) for i in range(4)]))  10.7 us
    ppermute x7, starting transfers between devices, along(): return lax.ppermute(x, 'tok', [(i, (i + d) % Z) for i in range(Z)])  9.25 us
    ppermute x4, starting transfers between devices, pass_on(): return lax.ppermute(x, ('tok', 'co'), perm)  8.91 us
  transfers between devices with their start and end apart: 26, of which 11 were waited for; matrix products, arithmetic and copies ran while one was open for 7% of the time, Pallas kernels for 4%

profile of v5, /device:TPU:33, one launch (start us, length us, event | category | flops | bytes accessed | tf_op | source)
XLA Modules:
  0.0 182.5 jit_solution(9541680240655627849)
XLA Ops:
  1.7 17.8 %all_to_all.10.a_own = bf16[4,512,256]{2,1,0:T(8,128)(2,1)S(1)} all-to-all(bf16[4,512,256]{2,1,0:T(8,128)(2,1)S(1)} %broadcast_in_dim.7), channel_id=1, replica_groups=mesh['tok'=8,'y'=4,'xl'=2,'co'=2,'pair'=2] {'xl','pair'}, dimensions={0} | all-to-all | bytes 2097152 | tf_op jit(solution)/shard_map/all_to_all | solution.py:216
  19.5 1.8 collective-permute-start.8
  24.6 4.6 %collective-permute-done.3 = f16[136,640]{1,0:T(8,128)(2,1)S(1)} collective-permute-done((f16[136,640]{1,0:T(8,128)(2,1)S(1)}, f16[136,640]{1,0:T(8,128)(2,1)S(1)}, u32[]{:S(2)}, u32[]{:S(2)}) %collective-permute-start.3) | collective-permute-done | bytes 174112 | tf_op jit(solution)/shard_map/ppermute | solution.py:224
  29.2 2.9 %collective-permute-start.4 = (f16[136,640]{1,0:T(8,128)(2,1)S(1)}, f16[136,640]{1,0:T(8,128)(2,1)S(1)}, u32[]{:S(2)}, u32[]{:S(2)}) collective-permute-start(f16[136,640]{1,0:T(8,128)(2,1)S(1)} %collective-permute-done.3), channel_id=1, source_target_pairs={{0,224},{32,0},{64,32},{96,64},{128,96},{160,128},{192,160},{224,1... | collective-permute-start | bytes 522248 | tf_op jit(solution)/shard_map/ppermute | solution.py:224
  35.0 3.4 %collective-permute-start.5 = (f16[136,640]{1,0:T(8,128)(2,1)S(1)}, f16[136,640]{1,0:T(8,128)(2,1)}, u32[]{:S(2)}, u32[]{:S(2)}) collective-permute-start(f16[136,640]{1,0:T(8,128)(2,1)S(1)} %collective-permute-done.4), channel_id=1, source_target_pairs={{0,224},{32,0},{64,32},{96,64},{128,96},{160,128},{192,160},{224,1... | collective-permute-start | bytes 522248 | tf_op jit(solution)/shard_map/ppermute | solution.py:224
  38.4 2.4 %collective-permute-done.1 = f16[136,640]{1,0:T(8,128)(2,1)} collective-permute-done((f16[136,640]{1,0:T(8,128)(2,1)S(1)}, f16[136,640]{1,0:T(8,128)(2,1)}, u32[]{:S(2)}, u32[]{:S(2)}) %collective-permute-start.1) | collective-permute-done | bytes 174112 | tf_op jit(solution)/shard_map/ppermute | solution.py:224
  40.9 12.0 %collective-permute-start.12 = (bf16[512,256]{1,0:T(8,128)(2,1)S(1)}, bf16[512,256]{1,0:T(8,128)(2,1)S(1)}, u32[]{:S(2)}, u32[]{:S(2)}) collective-permute-start(bf16[512,256]{1,0:T(8,128)(2,1)S(1)} %collective-permute-done.9.b0), channel_id=1, source_target_pairs={{0,24},{8,16},{16,8},{24,0},{1,25},{9,17},{17,9},{25,1},{2,26},{10... | collective-permute-start | bytes 786440 | tf_op jit(solution)/shard_map/ppermute | solution.py:237
  54.2 10.3 %collective-permute-done.12.b3 = bf16[512,256]{1,0:T(8,128)(2,1)S(1)} collective-permute-done((bf16[512,256]{1,0:T(8,128)(2,1)S(1)}, bf16[512,256]{1,0:T(8,128)(2,1)S(1)}, u32[]{:S(2)}, u32[]{:S(2)}) %collective-permute-start.12) | collective-permute-done | bytes 262176 | tf_op jit(solution)/shard_map/ppermute | solution.py:237
  64.9 2.1 %partial_gradient.1 = f32[8,136,512]{2,1,0:T(8,128)S(1)} custom-call(s32[3]{0:T(128)S(1)} %pad_add_fusion.1.idx, bf16[4,512,256]{2,1,0:T(8,128)(2,1)S(1)} %all_to_all.10.a_own, bf16[4,512,256]{2,1,0:T(8,128)(2,1)S(1)} %collective-permute-done.8.a_oth, bf16[512,256]{1,0:T(8,128)(2,1)S(1)} %collective-permute-done.9.b0, ...), custom_call_target="tpu_custom_call" | custom-call | tf_op jit(solution)/shard_map/partial_gradient/pallas_call | solution.py:250
  68.3 7.0 %all-to-all-start.1 = ((f16[8,136,512]{2,1,0:T(8,128)(2,1)}), f16[8,136,512]{2,1,0:T(8,128)(2,1)S(1)}, u32[]{:S(2)}, u32[]{:S(2)}) async-start(f16[8,136,512]{2,1,0:T(8,128)(2,1)} %convert_element_type.29), calls=%async_computation.1 | async-start | bytes 2228224 | tf_op jit(solution)/shard_map/all_to_all | solution.py:272
  80.5 22.7 %collective-permute-done.6 = f16[136,640]{1,0:T(8,128)(2,1)S(1)} collective-permute-done((f16[136,640]{1,0:T(8,128)(2,1)}, f16[136,640]{1,0:T(8,128)(2,1)S(1)}, u32[]{:S(2)}, u32[]{:S(2)}) %collective-permute-start.6) | collective-permute-done | bytes 174112 | tf_op jit(solution)/shard_map/ppermute | solution.py:224
  106.9 2.2 %collective-permute-start.7 = (f16[8,136,640]{2,1,0:T(8,128)(2,1)}, f16[8,136,640]{2,1,0:T(8,128)(2,1)}, u32[]{:S(2)}, u32[]{:S(2)}) collective-permute-start(f16[8,136,640]{2,1,0:T(8,128)(2,1)} %bitcast_dynamic-update-slice_fusion), channel_id=1, source_target_pairs={{0,0},{1,2},{2,1},{3,3},{4,4},{5,6},{6,5},{7,7},{8,8},{9,10},{10,9... | collective-permute-start | bytes 4177928 | tf_op jit(solution)/shard_map/ppermute | solution.py:262
  109.4 11.8 %collective-permute-start.13 = (bf16[128,512]{1,0:T(8,128)(2,1)S(1)}, bf16[128,512]{1,0:T(8,128)(2,1)S(1)}, u32[]{:S(2)}, u32[]{:S(2)}) collective-permute-start(bf16[128,512]{1,0:T(8,128)(2,1)S(1)} %multiply_reduce_fusion.mine), channel_id=1, source_target_pairs={{0,2},{2,0},{1,3},{3,1},{4,6},{6,4},{5,7},{7,5},{8,10},{10,8},{9,1... | collective-permute-start | bytes 393224 | tf_op jit(solution)/shard_map/ppermute | solution.py:220
  122.8 3.7 %collective-permute-start.15 = (bf16[2,128,512]{2,1,0:T(8,128)(2,1)S(1)}, bf16[2,128,512]{2,1,0:T(8,128)(2,1)S(1)}, u32[]{:S(2)}, u32[]{:S(2)}) collective-permute-start(bf16[2,128,512]{2,1,0:T(8,128)(2,1)S(1)} %merge.1.g0), channel_id=1, source_target_pairs={{0,64},{2,194},{32,96},{34,226},{64,128},{66,2},{96,160},{98,34},{... | collective-permute-start | bytes 786440 | tf_op jit(solution)/shard_map/ppermute | solution.py:284
  127.5 5.1 %collective-permute-done.15.src.r2 = bf16[2,128,512]{2,1,0:T(8,128)(2,1)S(1)} collective-permute-done((bf16[2,128,512]{2,1,0:T(8,128)(2,1)S(1)}, bf16[2,128,512]{2,1,0:T(8,128)(2,1)S(1)}, u32[]{:S(2)}, u32[]{:S(2)}) %collective-permute-start.15) | collective-permute-done | bytes 262176 | tf_op jit(solution)/shard_map/ppermute | solution.py:284
  133.9 3.5 %collective-permute-start.17 = (bf16[2,64,512]{2,1,0:T(8,128)(2,1)S(1)}, bf16[2,64,512]{2,1,0:T(8,128)(2,1)S(1)}, u32[]{:S(2)}, u32[]{:S(2)}) collective-permute-start(bf16[2,64,512]{2,1,0:T(8,128)(2,1)S(1)} %half.1), channel_id=1, source_target_pairs={{0,64},{2,194},{32,96},{34,226},{64,128},{66,2},{96,160},{98,34},{... | collective-permute-start | bytes 393224 | tf_op jit(solution)/shard_map/ppermute | solution.py:284
  138.3 3.1 %collective-permute-start.19 = (bf16[2,128,512]{2,1,0:T(8,128)(2,1)S(1)}, bf16[2,128,512]{2,1,0:T(8,128)(2,1)S(1)}, u32[]{:S(2)}, u32[]{:S(2)}) collective-permute-start(bf16[2,128,512]{2,1,0:T(8,128)(2,1)S(1)} %collective-permute-done.15.src.r2), channel_id=1, source_target_pairs={{0,2},{2,0},{1,3},{3,1},{4,6},{6,4},{5,7},{7,5},{8,10},{10,8},{9,1... | collective-permute-start | bytes 786440 | tf_op jit(solution)/shard_map/ppermute | solution.py:220
  141.9 5.3 %collective-permute-start.21 = (bf16[2,64,512]{2,1,0:T(8,128)(2,1)S(1)}, bf16[2,64,512]{2,1,0:T(8,128)(2,1)S(1)}, u32[]{:S(2)}, u32[]{:S(2)}) collective-permute-start(bf16[2,64,512]{2,1,0:T(8,128)(2,1)S(1)} %collective-permute-done.17.r4), channel_id=1, source_target_pairs={{0,2},{2,0},{1,3},{3,1},{4,6},{6,4},{5,7},{7,5},{8,10},{10,8},{9,1... | collective-permute-start | bytes 393224 | tf_op jit(solution)/shard_map/ppermute | solution.py:220
  149.9 14.3 %inverse_root.1 = (bf16[4,1024,256]{2,1,0:T(8,128)(2,1)S(1)}, bf16[4,1024,256]{2,1,0:T(8,128)(2,1)S(1)}, f32[128,1024]{1,0:T(8,128)S(1)}, f32[8,128]{1,0:T(8,128)S(1)}) custom-call(s32[2]{0:T(128)S(1)} %pad_add_fusion.idx, f32[8,1024,128]{2,1,0:T(8,128)S(1)} %assemble.1.st, bf16[2,128,512]{2,1,0:T(8,128)(2,1)S(1)} %merge.1.g0, ...), custom_call_target="tpu_custom_call" | custom-call | tf_op jit(solution)/shard_map/inverse_root/pallas_call | solution.py:295
  164.3 1.9 %collective-permute-start.24 = (f32[128,1024]{1,0:T(8,128)S(1)}, f32[128,1024]{1,0:T(8,128)S(1)}, u32[]{:S(2)}, u32[]{:S(2)}) collective-permute-start(f32[128,1024]{1,0:T(8,128)S(1)} %get-tuple-element.23), channel_id=1, source_target_pairs={{0,0},{1,2},{2,1},{3,3},{4,4},{5,6},{6,5},{7,7},{8,8},{9,10},{10,9... | collective-permute-start | bytes 1572872 | tf_op jit(solution)/shard_map/ppermute | solution.py:307
  166.3 2.2 %collective-permute-done.22.other = bf16[4,1024,256]{2,1,0:T(8,128)(2,1)S(1)} collective-permute-done((bf16[4,1024,256]{2,1,0:T(8,128)(2,1)S(1)}, bf16[4,1024,256]{2,1,0:T(8,128)(2,1)S(1)}, u32[]{:S(2)}, u32[]{:S(2)}) %collective-permute-start.22) | collective-permute-done | bytes 2097184 | tf_op jit(solution)/shard_map/ppermute | solution.py:220
  168.5 5.6 %update_rows.1 = bf16[1,64,1024]{2,1,0:T(8,128)(2,1)S(1)} custom-call(s32[2]{0:T(128)S(1)} %pad_add_fusion.idx, bf16[4,1024,256]{2,1,0:T(8,128)(2,1)S(1)} %get-tuple-element.20.own, bf16[4,1024,256]{2,1,0:T(8,128)(2,1)S(1)} %collective-permute-done.22.other, bf16[4,1024,256]{2,1,0:T(8,128)(2,1)S(1)} %get-tuple-element.21.grad, ...), custom_call_target="tpu_custom_call" | custom-call | tf_op jit(solution)/shard_map/update_rows/pallas_call | solution.py:308
  174.1 2.9 %collective-permute-start.23 = (bf16[1,64,1024]{2,1,0:T(8,128)(2,1)S(1)}, bf16[1,64,1024]{2,1,0:T(8,128)(2,1)S(1)}, u32[]{:S(2)}, u32[]{:S(2)}) collective-permute-start(bf16[1,64,1024]{2,1,0:T(8,128)(2,1)S(1)} %update_rows.1), channel_id=1, source_target_pairs={{0,0},{1,2},{2,1},{3,3},{4,4},{5,6},{6,5},{7,7},{8,8},{9,10},{10,9... | collective-permute-start | bytes 393224 | tf_op jit(solution)/shard_map/ppermute | solution.py:317
  177.9 4.0 %collective-permute-done.23 = bf16[1,64,1024]{2,1,0:T(8,128)(2,1)S(1)} collective-permute-done((bf16[1,64,1024]{2,1,0:T(8,128)(2,1)S(1)}, bf16[1,64,1024]{2,1,0:T(8,128)(2,1)S(1)}, u32[]{:S(2)}, u32[]{:S(2)}) %collective-permute-start.23) | collective-permute-done | bytes 131104 | tf_op jit(solution)/shard_map/ppermute | solution.py:317
  (65 shorter events, 28.5 us)
Async XLA Ops:
  19.5 45.4 %collective-permute-start.8 = (bf16[4,512,256]{2,1,0:T(8,128)(2,1)S(1)}, bf16[4,512,256]{2,1,0:T(8,128)(2,1)S(1)}, u32[]{:S(2)}, u32[]{:S(2)}) collective-permute-start(bf16[4,512,256]{2,1,0:T(8,128)(2,1)S(1)} %all_to_all.10.a_own), channel_id=1, source_target_pairs={{0,2},{2,0},{1,3},{3,1},{4,6},{6,4},{5,7},{7,5},{8,10},{10,8},{9,1... | collective-permute-start | bytes 3145736 | tf_op jit(solution)/shard_map/ppermute | solution.py:220
  22.8 6.4 %collective-permute-start.3 = (f16[136,640]{1,0:T(8,128)(2,1)S(1)}, f16[136,640]{1,0:T(8,128)(2,1)S(1)}, u32[]{:S(2)}, u32[]{:S(2)}) collective-permute-start(f16[136,640]{1,0:T(8,128)(2,1)S(1)} %concatenate.7), channel_id=1, source_target_pairs={{0,224},{32,0},{64,32},{96,64},{128,96},{160,128},{192,160},{224,1... | collective-permute-start | bytes 522248 | tf_op jit(solution)/shard_map/ppermute | solution.py:224
  22.9 10.8 %collective-permute-start = (f16[136,640]{1,0:T(8,128)(2,1)S(1)}, f16[136,640]{1,0:T(8,128)(2,1)S(1)}, u32[]{:S(2)}, u32[]{:S(2)}) collective-permute-start(f16[136,640]{1,0:T(8,128)(2,1)S(1)} %concatenate.7), channel_id=1, source_target_pairs={{0,32},{32,64},{64,96},{96,128},{128,160},{160,192},{192,224},{224... | collective-permute-start | bytes 522248 | tf_op jit(solution)/shard_map/ppermute | solution.py:224
  29.2 5.8 %collective-permute-start.4 = (f16[136,640]{1,0:T(8,128)(2,1)S(1)}, f16[136,640]{1,0:T(8,128)(2,1)S(1)}, u32[]{:S(2)}, u32[]{:S(2)}) collective-permute-start(f16[136,640]{1,0:T(8,128)(2,1)S(1)} %collective-permute-done.3), channel_id=1, source_target_pairs={{0,224},{32,0},{64,32},{96,64},{128,96},{160,128},{192,160},{224,1... | collective-permute-start | bytes 522248 | tf_op jit(solution)/shard_map/ppermute | solution.py:224
  32.1 8.8 %collective-permute-start.9 = (bf16[512,256]{1,0:T(8,128)(2,1)}, bf16[512,256]{1,0:T(8,128)(2,1)S(1)}, u32[]{:S(2)}, u32[]{:S(2)}) collective-permute-start(bf16[512,256]{1,0:T(8,128)(2,1)} %param.4), channel_id=1, source_target_pairs={{0,0},{1,8},{4,16},{5,24},{8,1},{9,9},{12,17},{13,25},{16,4},{17,1... | collective-permute-start | bytes 786440 | tf_op jit(solution)/shard_map/ppermute | solution.py:234
  33.7 7.2 %collective-permute-start.1 = (f16[136,640]{1,0:T(8,128)(2,1)S(1)}, f16[136,640]{1,0:T(8,128)(2,1)}, u32[]{:S(2)}, u32[]{:S(2)}) collective-permute-start(f16[136,640]{1,0:T(8,128)(2,1)S(1)} %collective-permute-done), channel_id=1, source_target_pairs={{0,32},{32,64},{64,96},{96,128},{128,160},{160,192},{192,224},{224... | collective-permute-start | bytes 522248 | tf_op jit(solution)/shard_map/ppermute | solution.py:224
  35.0 17.8 %collective-permute-start.5 = (f16[136,640]{1,0:T(8,128)(2,1)S(1)}, f16[136,640]{1,0:T(8,128)(2,1)}, u32[]{:S(2)}, u32[]{:S(2)}) collective-permute-start(f16[136,640]{1,0:T(8,128)(2,1)S(1)} %collective-permute-done.4), channel_id=1, source_target_pairs={{0,224},{32,0},{64,32},{96,64},{128,96},{160,128},{192,160},{224,1... | collective-permute-start | bytes 522248 | tf_op jit(solution)/shard_map/ppermute | solution.py:224
  40.9 12.6 %collective-permute-start.2 = (f16[136,640]{1,0:T(8,128)(2,1)}, f16[136,640]{1,0:T(8,128)(2,1)}, u32[]{:S(2)}, u32[]{:S(2)}) collective-permute-start(f16[136,640]{1,0:T(8,128)(2,1)} %collective-permute-done.1), channel_id=1, source_target_pairs={{0,32},{32,64},{64,96},{96,128},{128,160},{160,192},{192,224},{224... | collective-permute-start | bytes 522248 | tf_op jit(solution)/shard_map/ppermute | solution.py:224
  40.9 23.7 %collective-permute-start.12 = (bf16[512,256]{1,0:T(8,128)(2,1)S(1)}, bf16[512,256]{1,0:T(8,128)(2,1)S(1)}, u32[]{:S(2)}, u32[]{:S(2)}) collective-permute-start(bf16[512,256]{1,0:T(8,128)(2,1)S(1)} %collective-permute-done.9.b0), channel_id=1, source_target_pairs={{0,24},{8,16},{16,8},{24,0},{1,25},{9,17},{17,9},{25,1},{2,26},{10... | collective-permute-start | bytes 786440 | tf_op jit(solution)/shard_map/ppermute | solution.py:237
  52.8 11.7 %collective-permute-start.11 = (bf16[512,256]{1,0:T(8,128)(2,1)S(1)}, bf16[512,256]{1,0:T(8,128)(2,1)S(1)}, u32[]{:S(2)}, u32[]{:S(2)}) collective-permute-start(bf16[512,256]{1,0:T(8,128)(2,1)S(1)} %collective-permute-done.9.b0), channel_id=1, source_target_pairs={{0,16},{8,24},{16,0},{24,8},{1,17},{9,25},{17,1},{25,9},{2,18},{10... | collective-permute-start | bytes 786440 | tf_op jit(solution)/shard_map/ppermute | solution.py:237
  52.8 12.1 %collective-permute-start.10 = (bf16[512,256]{1,0:T(8,128)(2,1)S(1)}, bf16[512,256]{1,0:T(8,128)(2,1)S(1)}, u32[]{:S(2)}, u32[]{:S(2)}) collective-permute-start(bf16[512,256]{1,0:T(8,128)(2,1)S(1)} %collective-permute-done.9.b0), channel_id=1, source_target_pairs={{0,8},{8,0},{16,24},{24,16},{1,9},{9,1},{17,25},{25,17},{2,10},{10... | collective-permute-start | bytes 786440 | tf_op jit(solution)/shard_map/ppermute | solution.py:237
  68.3 40.8 %all-to-all-start.1 = ((f16[8,136,512]{2,1,0:T(8,128)(2,1)}), f16[8,136,512]{2,1,0:T(8,128)(2,1)S(1)}, u32[]{:S(2)}, u32[]{:S(2)}) async-start(f16[8,136,512]{2,1,0:T(8,128)(2,1)} %convert_element_type.29), calls=%async_computation.1 | async-start | bytes 2228224 | tf_op jit(solution)/shard_map/all_to_all | solution.py:272
  76.1 27.2 %collective-permute-start.6 = (f16[136,640]{1,0:T(8,128)(2,1)}, f16[136,640]{1,0:T(8,128)(2,1)S(1)}, u32[]{:S(2)}, u32[]{:S(2)}) collective-permute-start(f16[136,640]{1,0:T(8,128)(2,1)} %collective-permute-done.2), channel_id=1, source_target_pairs={{0,32},{32,64},{64,96},{96,128},{128,160},{160,192},{192,224},{224... | collective-permute-start | bytes 522248 | tf_op jit(solution)/shard_map/ppermute | solution.py:224
  106.9 30.4 %collective-permute-start.7 = (f16[8,136,640]{2,1,0:T(8,128)(2,1)}, f16[8,136,640]{2,1,0:T(8,128)(2,1)}, u32[]{:S(2)}, u32[]{:S(2)}) collective-permute-start(f16[8,136,640]{2,1,0:T(8,128)(2,1)} %bitcast_dynamic-update-slice_fusion), channel_id=1, source_target_pairs={{0,0},{1,2},{2,1},{3,3},{4,4},{5,6},{6,5},{7,7},{8,8},{9,10},{10,9... | collective-permute-start | bytes 4177928 | tf_op jit(solution)/shard_map/ppermute | solution.py:262
  109.4 12.8 %collective-permute-start.13 = (bf16[128,512]{1,0:T(8,128)(2,1)S(1)}, bf16[128,512]{1,0:T(8,128)(2,1)S(1)}, u32[]{:S(2)}, u32[]{:S(2)}) collective-permute-start(bf16[128,512]{1,0:T(8,128)(2,1)S(1)} %multiply_reduce_fusion.mine), channel_id=1, source_target_pairs={{0,2},{2,0},{1,3},{3,1},{4,6},{6,4},{5,7},{7,5},{8,10},{10,8},{9,1... | collective-permute-start | bytes 393224 | tf_op jit(solution)/shard_map/ppermute | solution.py:220
  122.8 9.8 %collective-permute-start.15 = (bf16[2,128,512]{2,1,0:T(8,128)(2,1)S(1)}, bf16[2,128,512]{2,1,0:T(8,128)(2,1)S(1)}, u32[]{:S(2)}, u32[]{:S(2)}) collective-permute-start(bf16[2,128,512]{2,1,0:T(8,128)(2,1)S(1)} %merge.1.g0), channel_id=1, source_target_pairs={{0,64},{2,194},{32,96},{34,226},{64,128},{66,2},{96,160},{98,34},{... | collective-permute-start | bytes 786440 | tf_op jit(solution)/shard_map/ppermute | solution.py:284
  126.4 14.9 %collective-permute-start.14 = (bf16[2,128,512]{2,1,0:T(8,128)(2,1)S(1)}, bf16[2,128,512]{2,1,0:T(8,128)(2,1)S(1)}, u32[]{:S(2)}, u32[]{:S(2)}) collective-permute-start(bf16[2,128,512]{2,1,0:T(8,128)(2,1)S(1)} %merge.1.g0), channel_id=1, source_target_pairs={{0,32},{2,226},{32,64},{34,2},{64,96},{66,34},{96,128},{98,66},{12... | collective-permute-start | bytes 786440 | tf_op jit(solution)/shard_map/ppermute | solution.py:284
  132.6 14.5 %collective-permute-start.16 = (bf16[2,128,512]{2,1,0:T(8,128)(2,1)S(1)}, bf16[2,128,512]{2,1,0:T(8,128)(2,1)S(1)}, u32[]{:S(2)}, u32[]{:S(2)}) collective-permute-start(bf16[2,128,512]{2,1,0:T(8,128)(2,1)S(1)} %collective-permute-done.15.src.r2), channel_id=1, source_target_pairs={{0,32},{2,226},{32,64},{34,2},{64,96},{66,34},{96,128},{98,66},{12... | collective-permute-start | bytes 786440 | tf_op jit(solution)/shard_map/ppermute | solution.py:284
  133.9 8.0 %collective-permute-start.17 = (bf16[2,64,512]{2,1,0:T(8,128)(2,1)S(1)}, bf16[2,64,512]{2,1,0:T(8,128)(2,1)S(1)}, u32[]{:S(2)}, u32[]{:S(2)}) collective-permute-start(bf16[2,64,512]{2,1,0:T(8,128)(2,1)S(1)} %half.1), channel_id=1, source_target_pairs={{0,64},{2,194},{32,96},{34,226},{64,128},{66,2},{96,160},{98,34},{... | collective-permute-start | bytes 393224 | tf_op jit(solution)/shard_map/ppermute | solution.py:284
  138.3 11.7 %collective-permute-start.19 = (bf16[2,128,512]{2,1,0:T(8,128)(2,1)S(1)}, bf16[2,128,512]{2,1,0:T(8,128)(2,1)S(1)}, u32[]{:S(2)}, u32[]{:S(2)}) collective-permute-start(bf16[2,128,512]{2,1,0:T(8,128)(2,1)S(1)} %collective-permute-done.15.src.r2), channel_id=1, source_target_pairs={{0,2},{2,0},{1,3},{3,1},{4,6},{6,4},{5,7},{7,5},{8,10},{10,8},{9,1... | collective-permute-start | bytes 786440 | tf_op jit(solution)/shard_map/ppermute | solution.py:220
  141.3 8.6 %collective-permute-start.18 = (bf16[2,128,512]{2,1,0:T(8,128)(2,1)S(1)}, bf16[2,128,512]{2,1,0:T(8,128)(2,1)S(1)}, u32[]{:S(2)}, u32[]{:S(2)}) collective-permute-start(bf16[2,128,512]{2,1,0:T(8,128)(2,1)S(1)} %collective-permute-done.14.r1), channel_id=1, source_target_pairs={{0,2},{2,0},{1,3},{3,1},{4,6},{6,4},{5,7},{7,5},{8,10},{10,8},{9,1... | collective-permute-start | bytes 786440 | tf_op jit(solution)/shard_map/ppermute | solution.py:220
  141.9 8.0 %collective-permute-start.21 = (bf16[2,64,512]{2,1,0:T(8,128)(2,1)S(1)}, bf16[2,64,512]{2,1,0:T(8,128)(2,1)S(1)}, u32[]{:S(2)}, u32[]{:S(2)}) collective-permute-start(bf16[2,64,512]{2,1,0:T(8,128)(2,1)S(1)} %collective-permute-done.17.r4), channel_id=1, source_target_pairs={{0,2},{2,0},{1,3},{3,1},{4,6},{6,4},{5,7},{7,5},{8,10},{10,8},{9,1... | collective-permute-start | bytes 393224 | tf_op jit(solution)/shard_map/ppermute | solution.py:220
  164.3 12.7 %collective-permute-start.24 = (f32[128,1024]{1,0:T(8,128)S(1)}, f32[128,1024]{1,0:T(8,128)S(1)}, u32[]{:S(2)}, u32[]{:S(2)}) collective-permute-start(f32[128,1024]{1,0:T(8,128)S(1)} %get-tuple-element.23), channel_id=1, source_target_pairs={{0,0},{1,2},{2,1},{3,3},{4,4},{5,6},{6,5},{7,7},{8,8},{9,10},{10,9... | collective-permute-start | bytes 1572872 | tf_op jit(solution)/shard_map/ppermute | solution.py:307
  174.1 7.8 %collective-permute-start.23 = (bf16[1,64,1024]{2,1,0:T(8,128)(2,1)S(1)}, bf16[1,64,1024]{2,1,0:T(8,128)(2,1)S(1)}, u32[]{:S(2)}, u32[]{:S(2)}) collective-permute-start(bf16[1,64,1024]{2,1,0:T(8,128)(2,1)S(1)} %update_rows.1), channel_id=1, source_target_pairs={{0,0},{1,2},{2,1},{3,3},{4,4},{5,6},{6,5},{7,7},{8,8},{9,10},{10,9... | collective-permute-start | bytes 393224 | tf_op jit(solution)/shard_map/ppermute | solution.py:317
  (5 other events, 36.0 us)
